TPU v7x, 32 devices: a whole 2x2x4 slice. The times are simulated.
32 devices in a mesh: gx: 8 (over y, x, core), yz: 4 (over z).
Axes of the slice: x: 2, y: 2, z: 4, core: 2. Of those that a mesh axis runs over, the one named last changes fastest.
Arguments:
- vel: float32 [3, 48, 192, 1024], P(None, 'gx', 'yz'), may hold values from -6 to 6
- q_old: float32 [3, 48, 192, 1024], P(None, 'gx', None, 'yz'), may hold values from -6 to 6
- pressure_guess: float32 [48, 192, 1024], P('gx', None, 'yz'), may hold values from -6 to 6
- shear_shift: int32 [1], replicated, may hold values from 0 to 1023
Outputs:
- vel_next: float32 [3, 48, 192, 1024], P(None, 'gx', 'yz')
- q_next: float32 [3, 48, 192, 1024], P(None, 'gx', None, 'yz')
- pressure: float32 [48, 192, 1024], P('gx', None, 'yz')
All inputs are finite; a program needn't handle non-finite values.
Results may differ from a plain program's by a relative error of at most 0.00013.
Values sent between devices are 32-bit elements; how exact they have to be, the bound alone decides.
A program may use at most 128 MiB of HBM per device.

v0:
```python
import functools
import math

import jax
import jax.numpy as jnp
import ml_dtypes
import numpy as np
from jax import lax
from jax.experimental import pallas as pl
from jax.experimental.pallas import tpu as pltpu
from jax.sharding import PartitionSpec as P


viscosity = 0.05
time_step = 0.2
keep_weight = -5.0 / 9.0
section_weight = 15.0 / 16.0
shear_param = 1.5
fraction = 0.375

F32 = jnp.float32
BF16 = jnp.bfloat16
VMEM_LIMIT = 62 * 1024 * 1024


def np_parts(matrix):
    high = matrix.astype(np.float32).astype(ml_dtypes.bfloat16)
    low = (matrix - high.astype(np.float64)).astype(np.float32).astype(ml_dtypes.bfloat16)
    return high, low


def parts(x):
    high = x.astype(BF16)
    return high, (x - high.astype(F32)).astype(BF16)


def dot(x, y):
    return jnp.dot(x, y, preferred_element_type=F32)


def dot_t(x, y):
    return lax.dot_general(x, y, (((1,), (1,)), ((), ())), preferred_element_type=F32)


def dot3(a, b, op=dot):
    return op(a[0], b[0]) + (op(a[1], b[0]) + op(a[0], b[1]))


def swap(x):
    return pltpu.roll(x, x.shape[-1] // 2, axis=x.ndim - 1)


def sign_row(cols):
    lane = lax.broadcasted_iota(jnp.int32, (1, cols), 1)
    return jnp.where(lane < cols // 2, -1.0, 1.0).astype(F32)


def take_chunk(v, e, chunks):
    if chunks == 1:
        return v
    w = v.shape[-1] // 2
    lane = lax.broadcasted_iota(jnp.int32, v.shape[:-1] + (w,), v.ndim - 1)
    re, im = v[..., :w], v[..., w:]
    if e == 0:
        return jnp.where(lane < w // 2, re, swap(im))
    return jnp.where(lane < w // 2, swap(re), im)


def merge_chunks(a, b):
    w = a.shape[-1]
    lane = lax.broadcasted_iota(jnp.int32, a.shape, a.ndim - 1)
    re = jnp.where(lane < w // 2, a, swap(b))
    im = jnp.where(lane < w // 2, swap(a), b)
    return re, im


def put(outs, field, value, cw):
    send, keep = outs
    place = pl.program_id(0)
    pairs = pl.num_programs(0) // 2
    _, _, nx, nz, _ = send[0].shape

    def store(refs):
        for e, ref in enumerate(refs):
            ref[0, field] = value[:, e * cw : (e + 1) * cw].reshape(nx, nz, cw)

    pl.when(place < pairs)(lambda: store(send))
    pl.when(place >= pairs)(lambda: store(keep))


def still_fields(order_ref, uz_ref, u_ref, wh_ref, wl_ref, *refs, chunks):
    send, keep = refs[:chunks], refs[chunks : 2 * chunks]
    high, low = refs[2 * chunks :]
    g = order_ref[pl.program_id(0)]
    _, nx, nz, _ = u_ref.shape
    m = nx * nz
    cw = send[0].shape[-1]

    @pl.when(pl.program_id(0) == 0)
    def _():
        for x in range(nx):
            u = u_ref[0, x]
            for at, v in ((x * nz, u), (m + x * nz, -uz_ref[0, x] * u)):
                h, l = parts(v)
                high[at : at + nz] = h
                low[at : at + nz] = l

    out = dot3((high[...], low[...]), (wh_ref[g], wl_ref[g]))
    put((send, keep), 0, out[:m], cw)
    put((send, keep), 1, out[m:], cw)


def moving_field(
    order_ref, shift_ref, mix_ref, back_ref, ux_ref, uy_ref, u_ref, tx_ref, t_ref, fx_ref, f_ref,
    ky_ref, wh_ref, wl_ref, *refs, c, omega, chunks,
):
    us_send, us_keep = refs[:chunks], refs[chunks : 2 * chunks]
    send, keep = refs[2 * chunks : 3 * chunks], refs[3 * chunks : 4 * chunks]
    ghost, high, low = refs[4 * chunks :]
    place = pl.program_id(0)
    pairs = pl.num_programs(0) // 2
    g = order_ref[place]
    _, nx, nz, ny = u_ref.shape
    m = nx * nz
    cw = send[0].shape[-1]

    @pl.when(place == 0)
    def _():
        for i, (tail, front) in enumerate(((tx_ref, fx_ref), (t_ref, f_ref))):
            if i and not c:
                continue
            for j in range(3):
                t = tail[j]
                ghost[i, j] = mix_ref[0] * pltpu.roll(t, shift_ref[0], axis=1) + mix_ref[
                    1
                ] * pltpu.roll(t, shift_ref[1], axis=1)
                f = front[j]
                ghost[i, 3 + j] = mix_ref[2] * pltpu.roll(f, shift_ref[2], axis=1) + mix_ref[
                    3
                ] * pltpu.roll(f, shift_ref[3], axis=1)

        def chunk(i, carry):
            lanes = pl.ds(pl.multiple_of(i * 128, 128), 128)

            def plane(which, x):
                if x < 0:
                    return ghost[which, x + 3, :, lanes]
                if x >= nx:
                    return ghost[which, x - nx + 3, :, lanes]
                return (u_ref if which else ux_ref)[0, x, :, lanes]

            for x in range(nx):
                ux = [plane(0, x + j) for j in range(-3, 4)]
                uy = uy_ref[0, x, :, lanes]
                moving = uy + back_ref[x]
                v = ux if c == 0 else [plane(1, x + j) for j in range(-3, 4)]
                f = [ux[j] * v[j] for j in range(7) if j != 3]
                d1 = (45.0 * (f[3] - f[2]) - 9.0 * (f[4] - f[1]) + (f[5] - f[0])) * (1.0 / 60.0)
                d2 = (
                    2.0 * (v[6] + v[0])
                    - 27.0 * (v[5] + v[1])
                    + 270.0 * (v[4] + v[2])
                    - 490.0 * v[3]
                ) * (1.0 / 180.0)
                a = viscosity * d2 - d1
                if c == 0:
                    a = a + (2.0 * omega) * uy
                if c == 1:
                    a = a - ((2.0 - shear_param) * omega) * ux[3]
                for at, value in ((x * nz, a), (m + x * nz, -moving * v[3])):
                    h, l = parts(value)
                    high[at : at + nz, lanes] = h
                    low[at : at + nz, lanes] = l
            return carry

        lax.fori_loop(0, ny // 128, chunk, 0)

    out = dot3((high[...], low[...]), (wh_ref[g], wl_ref[g]))
    ky = ky_ref[g]
    sign = sign_row(cw)

    def store(old, new):
        for e, (u, ref) in enumerate(zip(old, new)):
            lanes = slice(e * cw, (e + 1) * cw)
            k = ky[:, lanes]
            yu = u[0, 0].reshape(m, cw)
            w = out[:m, lanes] + swap(out[m:, lanes]) * (k * sign) - viscosity * (k * k) * yu
            ref[0, 0] = w.reshape(nx, nz, cw)

    pl.when(place < pairs)(lambda: store(us_send, send))
    pl.when(place >= pairs)(lambda: store(us_keep, keep))


def z_partial(kw_ref, rw_ref, ks_ref, rs_ref, ah_ref, *outs):
    pairs, _, zb, _, cw = kw_ref.shape
    depth = outs[0].shape[1]
    sign = sign_row(cw)
    for at in tuple(range(1, pairs)) + (0,):
        ref = outs[at]
        for x0 in range(0, zb, 2):
            xs = range(x0, min(x0 + 2, zb))
            columns = [
                jnp.concatenate(
                    [
                        kw_ref[at, 0, x], rw_ref[at, 0, x],
                        ks_ref[at, 1, x], rs_ref[at, 1, x],
                        ks_ref[at, 0, x], rs_ref[at, 0, x],
                    ],
                    axis=0,
                )
                for x in xs
            ]
            h, l = parts(jnp.concatenate(columns, axis=-1))
            out = dot(ah_ref[...], jnp.concatenate([h, h, l], axis=0))
            for i, x in enumerate(xs):
                lanes = slice(i * cw, (i + 1) * cw)
                ref[x] = out[:depth, lanes] + swap(out[depth:, lanes]) * sign


def first_sweep(*refs, e, chunks, pieces):
    tx, ty, tz = (refs[c * pieces : (c + 1) * pieces] for c in range(3))
    (
        p_ref, txl_ref, txh_ref, pl_ref, ph_ref, rot_ref, ky_ref, kz_ref, rden_ref,
        div_ref, out_ref, lo_ref, hi_ref,
    ) = refs[3 * pieces :]
    nx, _, cols = div_ref.shape
    sign = sign_row(cols)
    ky = ky_ref[...] * sign
    kz = kz_ref[...] * sign
    rden = rden_ref[...]

    def total(pieces_of, x):
        out = pieces_of[0][x]
        for ref in pieces_of[1:]:
            out = out + ref[x]
        return out

    def rot(v, k):
        return v * rot_ref[2 * k : 2 * k + 1] + swap(v) * rot_ref[2 * k + 1 : 2 * k + 2]

    def guess(v):
        return take_chunk(v, e, chunks)

    for x in range(nx):
        below = total(tx, x - 1) if x else rot(txl_ref[...], 0)
        above = total(tx, x + 1) if x < nx - 1 else rot(txh_ref[...], 1)
        p_below = guess(p_ref[x - 1]) if x else rot(guess(pl_ref[0]), 0)
        p_above = guess(p_ref[x + 1]) if x < nx - 1 else rot(guess(ph_ref[0]), 1)
        div = 0.5 * (above - below) + swap(total(ty, x)) * ky + swap(total(tz, x)) * kz
        div_ref[x] = div
        p = (p_above + p_below - div) * rden
        out_ref[x] = p
        if x == 0:
            lo_ref[0] = p
            lo_ref[1] = -div
        if x == 1:
            lo_ref[1] = lo_ref[1] + p
        if x == nx - 2:
            hi_ref[1] = p
        if x == nx - 1:
            hi_ref[0] = p
            hi_ref[1] = hi_ref[1] - div


def finish(*refs, e, chunks, pieces):
    p1_ref, div_ref, lo_ref, hi_ref, rot_ref, ky_ref, kz_ref, rden_ref, ck_ref = refs[:9]
    refs = refs[9:]
    t_refs = [refs[c * pieces : (c + 1) * pieces] for c in range(3)]
    q_ref, bh_ref, bl_ref = refs[3 * pieces : 3 * pieces + 3]
    refs = refs[3 * pieces + 3 :]
    last = e == chunks - 1
    earlier = chunks > 1 and last
    if earlier:
        q_first, p_first = refs[:2]
        refs = refs[2:]
    qn_ref, p_ref = refs[:2]
    h_refs, press = refs[2:-1], refs[-1]
    nx, depth, cols = p1_ref.shape
    step = pl.program_id(0)
    _, planes, nz, _ = h_refs[0].shape
    sign = sign_row(cols)

    @pl.when(step == 0)
    def _():
        rden = rden_ref[...]

        def rot(v, k):
            return v * rot_ref[2 * k : 2 * k + 1] + swap(v) * rot_ref[2 * k + 1 : 2 * k + 2]

        low = rot(lo_ref[0], 0)
        high = rot(hi_ref[0], 1)
        press[0] = (p1_ref[0] + rot(lo_ref[1], 0)) * rden
        press[nx + 1] = (p1_ref[nx - 1] + rot(hi_ref[1], 1)) * rden
        for i in range(nx):
            below = p1_ref[i - 1] if i else low
            above = p1_ref[i + 1] if i < nx - 1 else high
            press[i + 1] = (above + below - div_ref[i]) * rden

    def leave(ref, at, value, first):
        if earlier:
            re, im = merge_chunks(first, value)
            ref[at + (slice(None), slice(0, cols))] = re
            ref[at + (slice(None), slice(cols, 2 * cols))] = im
        else:
            ref[at] = value

    for i in range(planes):
        x = step * planes + i
        p = press[x + 1]
        leave(p_ref, (i,), p, p_first[i] if earlier else None)
        turned = swap(p) * sign
        grads = (0.5 * (press[x + 2] - press[x]), turned * ky_ref[...], turned * kz_ref[...])
        fresh = []
        for c in range(3):
            t = t_refs[c][0][i]
            for ref in t_refs[c][1:]:
                t = t + ref[i]
            q = keep_weight * take_chunk(q_ref[c, i], e, chunks) + time_step * (t - grads[c])
            leave(qn_ref, (c, i), q, q_first[c, i] if earlier else None)
            fresh.append(q)
        out = dot3((bh_ref[...], bl_ref[...]), parts(jnp.concatenate(fresh, axis=-1)))
        for c in range(3):
            lanes = slice(c * cols, (c + 1) * cols)
            h = (out[:depth, lanes] + swap(out[depth:, lanes]) * sign) * ck_ref[...]
            for k, ref in enumerate(h_refs):
                ref[c, i] = h[k * nz : (k + 1) * nz]


def y_inverse(order_ref, *refs, terms):
    base_ref, wh_ref, wl_ref, out_ref, th, tl = refs[-6:]
    blocks = refs[:-6]
    _, xb, nz, cols = blocks[0].shape

    @pl.when((pl.program_id(0) == 0) & (pl.program_id(1) == 0))
    def _():
        for i, (e, place) in enumerate(terms):
            g = order_ref[place]
            at = slice(i * cols, (i + 1) * cols)
            th[:, at] = wh_ref[g, :, e * cols : (e + 1) * cols]
            tl[:, at] = wl_ref[g, :, e * cols : (e + 1) * cols]

    rows = jnp.concatenate([b[0].reshape(xb * nz, cols) for b in blocks], axis=-1)
    total = dot3(parts(rows), (th[...], tl[...]), dot_t)
    ny = total.shape[-1]
    out_ref[0] = base_ref[0] + section_weight * total.reshape(xb, nz, ny)


def whole(shape):
    return pl.BlockSpec(shape, lambda *_: (0,) * len(shape))


SMEM = pl.BlockSpec(memory_space=pltpu.SMEM)


def shaped(*shape):
    return jax.ShapeDtypeStruct(shape, F32)


def call(body, flops, moved, **kw):
    return pl.pallas_call(
        body,
        compiler_params=pltpu.CompilerParams(vmem_limit_bytes=VMEM_LIMIT),
        cost_estimate=pl.CostEstimate(flops=int(flops), bytes_accessed=int(moved), transcendentals=0),
        **kw,
    )


def section(vel, q_old, pressure_guess, shear_shift):
    _, nx, nz, ny = vel.shape
    depth = q_old.shape[2]
    groups = lax.axis_size("yz")
    slabs = lax.axis_size("gx")
    pairs = groups // 2
    cols = ny // groups
    chunks = 2 if cols % 256 == 0 else 1
    cw = cols // chunks
    half = cw // 2
    block_len = cols // 2
    group_id = lax.axis_index("yz")
    slab_id = lax.axis_index("gx")
    bit = group_id % 2
    pair = group_id // 2
    total_x = nx * slabs
    omega = 2.0 / total_x
    offset = shear_shift[0]
    is_low = slab_id == 0
    is_high = slab_id == slabs - 1

    modes = np.arange(ny // 2).reshape(groups, 1, chunks, half)
    angle = 2.0 * np.pi / ny * (np.arange(ny).reshape(1, ny, 1, 1) * modes % ny)
    table = np.concatenate([np.cos(angle), -np.sin(angle)], axis=-1) / math.sqrt(ny)
    wh, wl = (jnp.asarray(t) for t in np_parts(table.reshape(groups, ny, cols)))
    kz_np = np.fft.fftfreq(depth) * 2.0 * np.pi
    angle_z = 2.0 * np.pi / depth * (np.arange(depth)[:, None] * np.arange(depth)[None, :] % depth)
    cz = np.cos(angle_z) / math.sqrt(depth)
    sz = np.sin(angle_z) / math.sqrt(depth)
    k1 = kz_np[:, None]
    k2 = viscosity * k1 * k1
    forward = np.concatenate(
        [
            np.concatenate([cz, k1 * sz, -k2 * cz], axis=1),
            np.concatenate([-sz, k1 * cz, k2 * sz], axis=1),
        ],
        axis=0,
    )
    paired = groups & (groups - 1) == 0
    paired_cross = pairs & (pairs - 1) == 0

    def partner(i, place):
        return i ^ place if paired else (i + place) % groups

    def across(j, s):
        return j ^ s if paired_cross else (j + s) % pairs

    order = jnp.stack([partner(group_id, place) for place in range(groups)])
    source = order if paired else (group_id - jnp.arange(groups)) % groups
    places = jnp.stack(
        [across(pair, s) * 2 + (1 - bit) for s in range(pairs)]
        + [across(pair, s) * 2 + bit for s in range(pairs)]
    )

    def forward_part(t):
        shaped_t = jnp.asarray(t.reshape(2 * depth, 3, groups, nz))
        rows = jnp.stack([group_id, group_id + 1 - 2 * bit])
        return jnp.take(shaped_t, rows, axis=2).reshape(2 * depth, 3 * 2 * nz)

    def inverse_part(t):
        shaped_t = jnp.asarray(t.reshape(2, groups, nz, depth))
        return jnp.take(shaped_t, order, axis=1).reshape(2 * depth, depth)

    fh, fl = (forward_part(t) for t in np_parts(forward))
    az = jnp.concatenate([fh, fl, fh], axis=1)
    bh, bl = (inverse_part(t) for t in np_parts(np.concatenate([cz, sz], axis=0)))
    ky_half = 2.0 * np.pi / ny * modes
    ky_all = jnp.asarray(
        np.concatenate([ky_half, ky_half], axis=-1).reshape(groups, 1, cols).astype(np.float32)
    )
    kz = jnp.asarray(kz_np.astype(np.float32)[:, None])
    lane = jnp.arange(cw, dtype=jnp.int32)
    sign = jnp.where(lane < half, -1.0, 1.0)
    kys, cks, rdens, rots = [], [], [], []
    for e in range(chunks):
        own = group_id * block_len + e * half + lane % half
        ky = (2.0 * math.pi / ny * own.astype(F32)).reshape(1, cw)
        edge = (
            2.0 * math.pi / ny
            * ((own * offset % ny).astype(F32) + fraction * own.astype(F32))
        )
        cos_e, sin_e = jnp.cos(edge), jnp.sin(edge) * sign
        kys.append(ky)
        cks.append(jnp.where(own == 0, 1.0, 2.0).astype(F32).reshape(1, cw))
        rdens.append(1.0 / (2.0 + ky * ky + kz * kz))
        rots.append(
            jnp.stack(
                [
                    jnp.where(is_low, cos_e, 1.0),
                    jnp.where(is_low, sin_e, 0.0),
                    jnp.where(is_high, cos_e, 1.0),
                    jnp.where(is_high, -sin_e, 0.0),
                ]
            ).astype(F32)
        )
    shifts = jnp.stack([(ny - offset) % ny, (2 * ny - 1 - offset) % ny, offset % ny, (offset + 1) % ny])
    at_edge = jnp.stack([is_low, is_low, is_high, is_high])
    shifts = jnp.where(at_edge, shifts, 0).astype(jnp.int32)
    mix = jnp.where(
        at_edge,
        jnp.array([1.0 - fraction, fraction] * 2, F32),
        jnp.array([1.0, 0.0] * 2, F32),
    )
    xpos = (slab_id * nx + jnp.arange(nx, dtype=jnp.int32)).astype(F32) + 0.5 - total_x / 2.0
    background = -shear_param * omega * xpos

    up = [(i, (i + 1) % slabs) for i in range(slabs)]
    down = [((i + 1) % slabs, i) for i in range(slabs)]
    twins = [(i, i ^ 1) for i in range(groups)]

    def exchange(first, last):
        return lax.ppermute(last, "gx", up), lax.ppermute(first, "gx", down)

    halos = [exchange(vel[0, :3], vel[0, nx - 3 :])]

    m = nx * nz
    y_flops = 2 * m * ny * ny * 3
    half_bytes = 4 * m * ny
    comp = lambda c: pl.BlockSpec((1, nx, nz, ny), lambda p: (c, 0, 0, 0))
    mats = [pltpu.VMEM((2 * m, ny), BF16)] * 2

    def field_specs(fields):
        block = (1, fields, nx, nz, cw)
        send = pl.BlockSpec(block, lambda p: (jnp.minimum(p, pairs - 1), 0, 0, 0, 0))
        keep = pl.BlockSpec(block, lambda p: (jnp.maximum(p - pairs, 0), 0, 0, 0, 0))
        return [send] * chunks + [keep] * chunks

    def still(c):
        return call(
            functools.partial(still_fields, chunks=chunks),
            2 * y_flops,
            4 * half_bytes,
            grid=(groups,),
            in_specs=[SMEM, comp(2), comp(c), whole(wh.shape), whole(wl.shape)],
            out_specs=field_specs(2),
            out_shape=[shaped(pairs, 2, nx, nz, cw)] * (2 * chunks),
            scratch_shapes=mats,
        )(places, vel, vel, wh, wl)

    def moving(c, us):
        return call(
            functools.partial(moving_field, c=c, omega=omega, chunks=chunks),
            2 * y_flops,
            6 * half_bytes,
            grid=(groups,),
            in_specs=[SMEM] * 4
            + [comp(0), comp(1), comp(c)]
            + [whole((3, nz, ny))] * 4
            + [whole(ky_all.shape), whole(wh.shape), whole(wl.shape)]
            + field_specs(1),
            out_specs=field_specs(1),
            out_shape=[shaped(pairs, 1, nx, nz, cw)] * (2 * chunks),
            scratch_shapes=[pltpu.VMEM((2, 6, nz, ny), F32)] + mats,
        )(
            places, shifts, mix, background, vel, vel, vel, halos[0][0], halos[c][0],
            halos[0][1], halos[c][1], ky_all, wh, wl, *us,
        )

    zb = 2 if nx % 2 == 0 else 1
    plane = (depth, cw)

    def z_part(kw, rw, ks, rs):
        outs = call(
            z_partial,
            2 * az.size * pairs * nx * cw,
            10 * half_bytes // groups,
            grid=(nx // zb,),
            in_specs=[
                pl.BlockSpec((pairs, f, zb, nz, cw), lambda x: (0, 0, x, 0, 0)) for f in (1, 1, 2, 2)
            ]
            + [whole(az.shape)],
            out_specs=[pl.BlockSpec((zb,) + plane, lambda x: (x, 0, 0))] * pairs,
            out_shape=[shaped(nx, *plane)] * pairs,
        )(kw, rw, ks, rs, az)
        pieces = [outs[0]]
        for s in range(1, pairs):
            to = [(i, across(i // 2, s) * 2 + i % 2) for i in range(groups)]
            pieces.append(lax.ppermute(outs[s], "yz", to))
        return pieces

    tend = [[None] * 3 for _ in range(chunks)]
    for c in range(3):
        us = still(c)
        if c == 0:
            later, guess, us = lax.optimization_barrier((vel, pressure_guess, us))
            for d in (1, 2):
                halos.append(exchange(later[d, :3], later[d, nx - 3 :]))
            p_low, p_high = exchange(guess[:1], guess[nx - 1 :])
        r_us = [lax.ppermute(us[e], "yz", twins) for e in range(chunks)]
        w = moving(c, us)
        r_w = [lax.ppermute(w[e], "yz", twins) for e in range(chunks)]
        for e in range(chunks):
            tend[e][c] = z_part(w[chunks + e], r_w[e], us[chunks + e], r_us[e])

    fb = 2 if nx % 2 == 0 else 1
    one = pl.BlockSpec((fb,) + plane, lambda x: (x, 0, 0))
    three = pl.BlockSpec((3, fb) + plane, lambda x: (0, x, 0, 0))
    packed = (depth, cols)
    q_done = []
    edges = []
    for e in range(chunks):
        edge_of = lambda x: functools.reduce(jnp.add, [piece[x] for piece in tend[e][0]])
        edges.append(exchange(edge_of(0), edge_of(nx - 1)))
    back = []
    for e in range(chunks):
        flat = [piece for c in range(3) for piece in tend[e][c]]
        t_low, t_high = edges[e]
        div, p1, lo, hi = call(
            functools.partial(first_sweep, e=e, chunks=chunks, pieces=pairs),
            2000 * nx * depth * cw,
            2 * half_bytes,
            out_shape=[shaped(nx, *plane)] * 2 + [shaped(2, *plane)] * 2,
        )(*flat, pressure_guess, t_low, t_high, p_low, p_high, rots[e], kys[e], kz, rdens[e])
        lo_halo, hi_halo = exchange(lo, hi)
        last = e == chunks - 1
        earlier = chunks > 1 and last
        out_plane = packed if last else plane
        consts = (p1, div, lo_halo, hi_halo, rots[e], kys[e], kz, rdens[e], cks[e])
        outs = call(
            functools.partial(finish, e=e, chunks=chunks, pieces=pairs),
            2 * 3 * 3 * nx * 2 * depth * depth * cw,
            3 * half_bytes,
            grid=(nx // fb,),
            in_specs=[whole(v.shape) for v in consts]
            + [one] * len(flat)
            + [pl.BlockSpec((3, fb) + packed, lambda x: (0, x, 0, 0)), whole(bh.shape), whole(bl.shape)]
            + ([three, one] if earlier else []),
            out_specs=[
                pl.BlockSpec((3, fb) + out_plane, lambda x: (0, x, 0, 0)),
                pl.BlockSpec((fb,) + out_plane, lambda x: (x, 0, 0)),
            ]
            + [pl.BlockSpec((3, fb, nz, cw), lambda x: (0, x, 0, 0))] * groups,
            out_shape=[shaped(3, nx, *out_plane), shaped(nx, *out_plane)]
            + [shaped(3, nx, nz, cw)] * groups,
            scratch_shapes=[pltpu.VMEM((nx + 2,) + plane, F32)],
        )(*consts, *flat, q_old, bh, bl, *q_done)
        q_done = list(outs[:2])
        got = [outs[2]]
        for place in range(1, groups):
            to = [(i, partner(i, place)) for i in range(groups)]
            got.append(lax.ppermute(outs[2 + place], "yz", to))
        back.append(got)

    vb = 3 if nx % 3 == 0 else 1
    vel_block = pl.BlockSpec((1, vb, nz, ny), lambda c, x: (c, x, 0, 0))
    batches = [[(e, place) for place in range(groups)] for e in range(chunks - 1)]
    batches += [[(chunks - 1, place) for place in range(2)]]
    batches += [[(chunks - 1, place) for place in range(2, groups)]]
    vel_next = vel
    for terms in batches:
        vel_next = call(
            functools.partial(y_inverse, terms=terms),
            3 * y_flops * len(terms) // (chunks * groups),
            6 * half_bytes,
            grid=(3, nx // vb),
            in_specs=[SMEM]
            + [pl.BlockSpec((1, vb, nz, cw), lambda c, x: (c, x, 0, 0))] * len(terms)
            + [vel_block, whole(wh.shape), whole(wl.shape)],
            out_specs=vel_block,
            out_shape=jax.ShapeDtypeStruct(vel.shape, F32),
            scratch_shapes=[pltpu.VMEM((ny, len(terms) * cw), BF16)] * 2,
        )(source, *[back[e][place] for e, place in terms], vel_next, wh, wl)
    return (vel_next, q_done[0], q_done[1])


def solution(mesh):
    placed = (P(None, "gx", "yz", None), P(None, "gx", None, "yz"), P("gx", None, "yz"), P())
    return jax.shard_map(
        section,
        mesh=mesh,
        in_specs=placed,
        out_specs=(P(None, "gx", "yz", None), P(None, "gx", None, "yz"), P("gx", None, "yz")),
        check_vma=False,
    )
```

profile of v0, /device:TPU:13, one launch (start us, length us, event | category | flops | bytes accessed | tf_op | source)
XLA Modules:
  0.0 387.7 jit_solution(15873442673384784056)
XLA Ops:
  0.6 2.4 slice_bitcast_fusion.4
  3.0 1.8 collective-permute-start
  5.3 9.0 %shard_map.157 = (f32[2,2,6,48,128]{4,3,2,1,0:T(8,128)}, f32[2,2,6,48,128]{4,3,2,1,0:T(8,128)}, f32[2,2,6,48,128]{4,3,2,1,0:T(8,128)}, f32[2,2,6,48,128]{4,3,2,1,0:T(8,128)}) custom-call(s32[4]{0:T(128)} %pad_add_fusion.2.order_ref, f32[3,6,48,1024]{3,2,1,0:T(8,128)} %refs_4_.3, f32[3,6,48,1024]{3,2,1,0:T(8,128)} %refs_4_.3, ...), custom_call_target="tpu_custom_call" | custom-call | flops 3623878656 | bytes 4718592 | tf_op jit(solution)/shard_map/pallas_call | solution.py:496
  14.6 3.1 slice_bitcast_fusion
  17.6 2.0 collective-permute-start.5
  19.7 1.7 fusion.16
  21.4 9.1 %shard_map.160 = (f32[2,2,6,48,128]{4,3,2,1,0:T(8,128)}, f32[2,2,6,48,128]{4,3,2,1,0:T(8,128)}, f32[2,2,6,48,128]{4,3,2,1,0:T(8,128)}, f32[2,2,6,48,128]{4,3,2,1,0:T(8,128)}) custom-call(s32[4]{0:T(128)} %pad_add_fusion.2.order_ref, f32[3,6,48,1024]{3,2,1,0:T(8,128)} %refs_4_.3, f32[3,6,48,1024]{3,2,1,0:T(8,128)} %refs_4_.3, ...), custom_call_target="tpu_custom_call" | custom-call | flops 3623878656 | bytes 4718592 | tf_op jit(solution)/shard_map/pallas_call | solution.py:496
  30.5 9.2 %shard_map.163 = (f32[2,2,6,48,128]{4,3,2,1,0:T(8,128)}, f32[2,2,6,48,128]{4,3,2,1,0:T(8,128)}, f32[2,2,6,48,128]{4,3,2,1,0:T(8,128)}, f32[2,2,6,48,128]{4,3,2,1,0:T(8,128)}) custom-call(s32[4]{0:T(128)} %pad_add_fusion.2.order_ref, f32[3,6,48,1024]{3,2,1,0:T(8,128)} %refs_4_.3, f32[3,6,48,1024]{3,2,1,0:T(8,128)} %refs_4_.3, ...), custom_call_target="tpu_custom_call" | custom-call | flops 3623878656 | bytes 4718592 | tf_op jit(solution)/shard_map/pallas_call | solution.py:496
  40.4 1.6 gather_fusion.1
  43.5 1.1 pad_maximum_fusion.ah_ref
  45.4 0.8 add_divide_fusion
  47.7 1.3 collective-permute-start.8
  50.8 0.8 select_bitcast_fusion.2
  51.6 1.6 collective-permute-start.10
  53.2 0.9 collective-permute-start.11
  54.3 12.9 %shard_map.158 = (f32[2,1,6,48,128]{4,3,2,1,0:T(8,128)}, f32[2,1,6,48,128]{4,3,2,1,0:T(8,128)}, f32[2,1,6,48,128]{4,3,2,1,0:T(8,128)}, f32[2,1,6,48,128]{4,3,2,1,0:T(8,128)}) custom-call(s32[4]{0:T(128)} %pad_add_fusion.2.order_ref, s32[4]{0:T(128)} %add_select_fusion.shift_ref, f32[4]{0:T(128)} %fusion.15.mix_ref, f32[6]{0:T(128)} %add_multiply_fusion.back_ref, ...), custom_call_target="tpu_custom_call" | custom-call | flops 3623878656 | bytes 7077888 | tf_op jit(solution)/shard_map/pallas_call | solution.py:508
  67.2 1.4 collective-permute-start.25
  68.8 13.9 %shard_map.161 = (f32[2,1,6,48,128]{4,3,2,1,0:T(8,128)}, f32[2,1,6,48,128]{4,3,2,1,0:T(8,128)}, f32[2,1,6,48,128]{4,3,2,1,0:T(8,128)}, f32[2,1,6,48,128]{4,3,2,1,0:T(8,128)}) custom-call(s32[4]{0:T(128)} %pad_add_fusion.2.order_ref, s32[4]{0:T(128)} %add_select_fusion.shift_ref, f32[4]{0:T(128)} %fusion.15.mix_ref, f32[6]{0:T(128)} %add_multiply_fusion.back_ref, ...), custom_call_target="tpu_custom_call" | custom-call | flops 3623878656 | bytes 7077888 | tf_op jit(solution)/shard_map/pallas_call | solution.py:508
  82.7 1.4 collective-permute-start.13
  84.2 1.3 collective-permute-start.24
  85.5 13.7 %shard_map.164 = (f32[2,1,6,48,128]{4,3,2,1,0:T(8,128)}, f32[2,1,6,48,128]{4,3,2,1,0:T(8,128)}, f32[2,1,6,48,128]{4,3,2,1,0:T(8,128)}, f32[2,1,6,48,128]{4,3,2,1,0:T(8,128)}) custom-call(s32[4]{0:T(128)} %pad_add_fusion.2.order_ref, s32[4]{0:T(128)} %add_select_fusion.shift_ref, f32[4]{0:T(128)} %fusion.15.mix_ref, f32[6]{0:T(128)} %add_multiply_fusion.back_ref, ...), custom_call_target="tpu_custom_call" | custom-call | flops 3623878656 | bytes 7077888 | tf_op jit(solution)/shard_map/pallas_call | solution.py:508
  99.5 1.4 collective-permute-start.2
  101.4 16.4 %collective-permute-done.21.rw_ref = f32[2,1,6,48,128]{4,3,2,1,0:T(8,128)} collective-permute-done((f32[2,1,6,48,128]{4,3,2,1,0:T(8,128)S(1)}, f32[2,1,6,48,128]{4,3,2,1,0:T(8,128)}, u32[]{:S(2)}, u32[]{:S(2)}) %collective-permute-start.21) | collective-permute-done | bytes 294944 | tf_op jit(solution)/shard_map/ppermute | solution.py:558
  117.8 1.3 collective-permute-start.7
  119.1 5.0 %collective-permute-done.24.rw_ref = f32[2,1,6,48,128]{4,3,2,1,0:T(8,128)} collective-permute-done((f32[2,1,6,48,128]{4,3,2,1,0:T(8,128)}, f32[2,1,6,48,128]{4,3,2,1,0:T(8,128)}, u32[]{:S(2)}, u32[]{:S(2)}) %collective-permute-start.24) | collective-permute-done | bytes 294944 | tf_op jit(solution)/shard_map/ppermute | solution.py:558
  124.1 1.3 collective-permute-start.12
  125.4 4.8 %shard_map.167 = (f32[6,192,128]{2,1,0:T(8,128)}, f32[6,192,128]{2,1,0:T(8,128)}) custom-call(f32[2,1,6,48,128]{4,3,2,1,0:T(8,128)} %get-tuple-element.101.kw_ref, f32[2,1,6,48,128]{4,3,2,1,0:T(8,128)} %collective-permute-done.21.rw_ref, f32[2,2,6,48,128]{4,3,2,1,0:T(8,128)} %get-tuple-element.73.refs_2_.ks_ref, ...), custom_call_target="tpu_custom_call" | custom-call | flops 1019215872 | bytes 2949120 | tf_op jit(solution)/shard_map/pallas_call | solution.py:530
  130.4 2.3 collective-permute-start.23
  132.7 4.8 %shard_map.168 = (f32[6,192,128]{2,1,0:T(8,128)}, f32[6,192,128]{2,1,0:T(8,128)}) custom-call(f32[2,1,6,48,128]{4,3,2,1,0:T(8,128)} %get-tuple-element.105.kw_ref, f32[2,1,6,48,128]{4,3,2,1,0:T(8,128)} %collective-permute-done.24.rw_ref, f32[2,2,6,48,128]{4,3,2,1,0:T(8,128)} %get-tuple-element.82.refs_2_.ks_ref, ...), custom_call_target="tpu_custom_call" | custom-call | flops 1019215872 | bytes 2949120 | tf_op jit(solution)/shard_map/pallas_call | solution.py:530
  137.6 4.9 %shard_map.169 = (f32[6,192,128]{2,1,0:T(8,128)}, f32[6,192,128]{2,1,0:T(8,128)}) custom-call(f32[2,1,6,48,128]{4,3,2,1,0:T(8,128)} %get-tuple-element.109.kw_ref, f32[2,1,6,48,128]{4,3,2,1,0:T(8,128)} %collective-permute-done.27.rw_ref, f32[2,2,6,48,128]{4,3,2,1,0:T(8,128)} %get-tuple-element.90.refs_2_.ks_ref, ...), custom_call_target="tpu_custom_call" | custom-call | flops 1019215872 | bytes 2949120 | tf_op jit(solution)/shard_map/pallas_call | solution.py:530
  142.6 2.8 collective-permute-start.29
  145.4 4.8 %shard_map.159 = (f32[6,192,128]{2,1,0:T(8,128)}, f32[6,192,128]{2,1,0:T(8,128)}) custom-call(f32[2,1,6,48,128]{4,3,2,1,0:T(8,128)} %get-tuple-element.75.kw_ref, f32[2,1,6,48,128]{4,3,2,1,0:T(8,128)} %collective-permute-done.2.rw_ref, f32[2,2,6,48,128]{4,3,2,1,0:T(8,128)} %get-tuple-element.74.refs_3_.ks_ref, ...), custom_call_target="tpu_custom_call" | custom-call | flops 1019215872 | bytes 2949120 | tf_op jit(solution)/shard_map/pallas_call | solution.py:530
  150.2 5.6 %collective-permute-done.7.rw_ref = f32[2,1,6,48,128]{4,3,2,1,0:T(8,128)} collective-permute-done((f32[2,1,6,48,128]{4,3,2,1,0:T(8,128)}, f32[2,1,6,48,128]{4,3,2,1,0:T(8,128)}, u32[]{:S(2)}, u32[]{:S(2)}) %collective-permute-start.7) | collective-permute-done | bytes 294944 | tf_op jit(solution)/shard_map/ppermute | solution.py:558
  155.8 7.5 %collective-permute-start.18 = (f32[1,192,256]{2,1,0:T(8,128)}, f32[1,192,256]{2,1,0:T(8,128)S(1)}, u32[]{:S(2)}, u32[]{:S(2)}) collective-permute-start(f32[1,192,256]{2,1,0:T(8,128)} %get-tuple-element.141), channel_id=1, source_target_pairs={{4,0},{8,4},{12,8},{16,12},{20,16},{24,20},{28,24},{0,28},{5,1},{9... | collective-permute-start | bytes 589832 | tf_op jit(solution)/shard_map/ppermute | solution.py:479
  163.3 2.2 collective-permute-start.4
  166.1 4.8 %shard_map.162 = (f32[6,192,128]{2,1,0:T(8,128)}, f32[6,192,128]{2,1,0:T(8,128)}) custom-call(f32[2,1,6,48,128]{4,3,2,1,0:T(8,128)} %get-tuple-element.84.kw_ref, f32[2,1,6,48,128]{4,3,2,1,0:T(8,128)} %collective-permute-done.7.rw_ref, f32[2,2,6,48,128]{4,3,2,1,0:T(8,128)} %get-tuple-element.83.refs_3_.ks_ref, ...), custom_call_target="tpu_custom_call" | custom-call | flops 1019215872 | bytes 2949120 | tf_op jit(solution)/shard_map/pallas_call | solution.py:530
  170.9 4.8 %shard_map.165 = (f32[6,192,128]{2,1,0:T(8,128)}, f32[6,192,128]{2,1,0:T(8,128)}) custom-call(f32[2,1,6,48,128]{4,3,2,1,0:T(8,128)} %get-tuple-element.92.kw_ref, f32[2,1,6,48,128]{4,3,2,1,0:T(8,128)} %collective-permute-done.12.rw_ref, f32[2,2,6,48,128]{4,3,2,1,0:T(8,128)} %get-tuple-element.91.refs_3_.ks_ref, f32[2,2,6,48,128]{4,3,2,1,0:T(8,128)} %copy-done.25, ...), custom_call_target="tpu_custom_call" | custom-call | flops 1019215872 | bytes 2949120 | tf_op jit(solution)/shard_map/pallas_call | solution.py:530
  176.6 2.2 collective-permute-start.14
  178.8 1.0 fusion
  179.7 43.7 %collective-permute-done.26.refs_3_.refs_12_ = f32[6,192,128]{2,1,0:T(8,128)} collective-permute-done((f32[6,192,128]{2,1,0:T(8,128)}, f32[6,192,128]{2,1,0:T(8,128)}, u32[]{:S(2)}, u32[]{:S(2)}) %collective-permute-start.26) | collective-permute-done | bytes 589856 | tf_op jit(solution)/shard_map/ppermute | solution.py:545
  223.4 16.9 %collective-permute-start.30 = (f32[192,128]{1,0:T(8,128)S(1)}, f32[192,128]{1,0:T(8,128)S(1)}, u32[]{:S(2)}, u32[]{:S(2)}) collective-permute-start(f32[192,128]{1,0:T(8,128)S(1)} %get-tuple-element.140), channel_id=1, source_target_pairs={{0,4},{4,8},{8,12},{12,16},{16,20},{20,24},{24,28},{28,0},{1,5},{5... | collective-permute-start | bytes 294920 | tf_op jit(solution)/shard_map/ppermute | solution.py:479
  240.3 2.1 collective-permute-done.29.refs_5_.refs_14_
  242.4 17.4 %collective-permute-start.31 = (f32[192,128]{1,0:T(8,128)S(1)}, f32[192,128]{1,0:T(8,128)S(1)}, u32[]{:S(2)}, u32[]{:S(2)}) collective-permute-start(f32[192,128]{1,0:T(8,128)S(1)} %get-tuple-element.139), channel_id=1, source_target_pairs={{4,0},{8,4},{12,8},{16,12},{20,16},{24,20},{28,24},{0,28},{5,1},{9... | collective-permute-start | bytes 294920 | tf_op jit(solution)/shard_map/ppermute | solution.py:479
  261.7 4.7 %shard_map.170 = (f32[6,192,128]{2,1,0:T(8,128)}, f32[6,192,128]{2,1,0:T(8,128)}, f32[2,192,128]{2,1,0:T(8,128)}, f32[2,192,128]{2,1,0:T(8,128)}) custom-call(f32[6,192,128]{2,1,0:T(8,128)} %get-tuple-element.103.refs_0_.refs_9_, f32[6,192,128]{2,1,0:T(8,128)} %copy-done.3, f32[6,192,128]{2,1,0:T(8,128)} %get-tuple-element.107.refs_2_.refs_11_, ...), custom_call_target="tpu_custom_call" | custom-call | flops 294912000 | bytes 2359296 | tf_op jit(solution)/shard_map/pallas_call | solution.py:575
  266.4 1.1 collective-permute-start.33
  267.4 1.2 fusion.2
  268.6 1.8 collective-permute-start.15
  270.4 4.7 %collective-permute-start.16 = (f32[192,128]{1,0:T(8,128)S(1)}, f32[192,128]{1,0:T(8,128)}, u32[]{:S(2)}, u32[]{:S(2)}) collective-permute-start(f32[192,128]{1,0:T(8,128)S(1)} %get-tuple-element.143), channel_id=1, source_target_pairs={{4,0},{8,4},{12,8},{16,12},{20,16},{24,20},{28,24},{0,28},{5,1},{9... | collective-permute-start | bytes 294920 | tf_op jit(solution)/shard_map/ppermute | solution.py:479
  275.7 1.6 copy.22
  278.6 8.3 %shard_map.171 = (f32[3,6,192,128]{3,2,1,0:T(8,128)}, f32[6,192,128]{2,1,0:T(8,128)}, f32[3,6,48,128]{3,2,1,0:T(8,128)}, f32[3,6,48,128]{3,2,1,0:T(8,128)}, f32[...) custom-call(f32[6,192,128]{2,1,0:T(8,128)} %get-tuple-element.113.refs_0_, f32[6,192,128]{2,1,0:T(8,128)} %get-tuple-element.114.refs_1_, ...), custom_call_target="tpu_custom_call" | custom-call | flops 1019215872 | bytes 3538944 | tf_op jit(solution)/shard_map/pallas_call | solution.py:586
  287.0 2.5 collective-permute-start.37
  289.5 0.8 copy-done.4
  290.3 4.6 %shard_map.166 = (f32[6,192,128]{2,1,0:T(8,128)}, f32[6,192,128]{2,1,0:T(8,128)}, f32[2,192,128]{2,1,0:T(8,128)}, f32[2,192,128]{2,1,0:T(8,128)}) custom-call(f32[6,192,128]{2,1,0:T(8,128)} %get-tuple-element.77.refs_0_.refs_9_, f32[6,192,128]{2,1,0:T(8,128)} %copy-done.2, f32[6,192,128]{2,1,0:T(8,128)} %get-tuple-element.86.refs_2_.refs_11_, ...), custom_call_target="tpu_custom_call" | custom-call | flops 294912000 | bytes 2359296 | tf_op jit(solution)/shard_map/pallas_call | solution.py:575
  294.9 1.1 collective-permute-start.20
  296.1 0.9 collective-permute-start.38
  297.0 2.5 collective-permute-start.39
  300.1 2.3 collective-permute-done.20.refs_3_
  303.1 9.8 %shard_map.172 = (f32[3,6,192,256]{3,2,1,0:T(8,128)}, f32[6,192,256]{2,1,0:T(8,128)}, f32[3,6,48,128]{3,2,1,0:T(8,128)}, f32[3,6,48,128]{3,2,1,0:T(8,128)}, f32[...) custom-call(f32[6,192,128]{2,1,0:T(8,128)} %get-tuple-element.97.refs_0_, f32[6,192,128]{2,1,0:T(8,128)} %get-tuple-element.98.refs_1_, ...), custom_call_target="tpu_custom_call" | custom-call | flops 1019215872 | bytes 3538944 | tf_op jit(solution)/shard_map/pallas_call | solution.py:586
  312.9 2.4 collective-permute-start.34
  315.6 9.0 %collective-permute-done.38.refs_2_ = f32[3,6,48,128]{3,2,1,0:T(8,128)S(1)} collective-permute-done((f32[3,6,48,128]{3,2,1,0:T(8,128)}, f32[3,6,48,128]{3,2,1,0:T(8,128)S(1)}, u32[]{:S(2)}, u32[]{:S(2)}) %collective-permute-start.38) | collective-permute-done | bytes 442400 | tf_op jit(solution)/shard_map/ppermute | solution.py:608
  324.6 32.1 %collective-permute-done.39.refs_3_ = f32[3,6,48,128]{3,2,1,0:T(8,128)S(1)} collective-permute-done((f32[3,6,48,128]{3,2,1,0:T(8,128)}, f32[3,6,48,128]{3,2,1,0:T(8,128)S(1)}, u32[]{:S(2)}, u32[]{:S(2)}) %collective-permute-start.39) | collective-permute-done | bytes 442400 | tf_op jit(solution)/shard_map/ppermute | solution.py:608
  357.5 11.4 %shard_map.173.refs_2_ = f32[3,6,48,1024]{3,2,1,0:T(8,128)} custom-call(s32[4]{0:T(128)} %copy-done.21, f32[3,6,48,128]{3,2,1,0:T(8,128)} %get-tuple-element.123.refs_0_, f32[3,6,48,128]{3,2,1,0:T(8,128)} %copy-done.9, f32[3,6,48,128]{3,2,1,0:T(8,128)} %copy-done.10, f32[3,6,48,128]{3,2,1,0:T(8,128)} %copy-done.11, f32[3,6,48,1024]{3,2,1,0:T(8,128)} %refs_4_.3, ...), custom_call_target="tpu_custom_call" | custom-call | flops 2717908992 | bytes 7077888 | tf_op jit(solution)/shard_map/pallas_call | solution.py:618
  368.9 9.0 %shard_map.174.refs_2_ = f32[3,6,48,1024]{3,2,1,0:T(8,128)} custom-call(s32[4]{0:T(128)} %copy-done.21, f32[3,6,48,128]{3,2,1,0:T(8,128)} %get-tuple-element.121.refs_0_, f32[3,6,48,128]{3,2,1,0:T(8,128)} %collective-permute-done.36.refs_1_, f32[3,6,48,1024]{3,2,1,0:T(8,128)} %shard_map.173.refs_2_, ...), custom_call_target="tpu_custom_call" | custom-call | flops 1358954496 | bytes 7077888 | tf_op jit(solution)/shard_map/pallas_call | solution.py:618
  378.7 9.0 %shard_map.175 = f32[3,6,48,1024]{3,2,1,0:T(8,128)} custom-call(s32[4]{0:T(128)} %copy-done.21, f32[3,6,48,128]{3,2,1,0:T(8,128)} %copy-done.12, f32[3,6,48,128]{3,2,1,0:T(8,128)} %collective-permute-done.35.refs_1_, f32[3,6,48,1024]{3,2,1,0:T(8,128)} %shard_map.174.refs_2_, bf16[4,1024,256]{2,1,0:T(8,128)(2,1)} %constant.158.clone.wh_ref.refs_5_.refs_3_, ...), custom_call_target="tpu_custom_call" | custom-call | flops 1358954496 | bytes 7077888 | tf_op jit(solution)/shard_map/pallas_call | solution.py:618
  (128 shorter events, 16.3 us)
Async XLA Ops:
  3.0 44.7 %collective-permute-start = (f32[3,48,1024]{2,1,0:T(8,128)}, f32[3,48,1024]{2,1,0:T(8,128)S(1)}, u32[]{:S(2)}, u32[]{:S(2)}) collective-permute-start(f32[3,48,1024]{2,1,0:T(8,128)} %get-tuple-element.138), channel_id=1, source_target_pairs={{0,4},{4,8},{8,12},{12,16},{16,20},{20,24},{24,28},{28,0},{1,5},{5... | collective-permute-start | bytes 1769480 | tf_op jit(solution)/shard_map/ppermute | solution.py:479
  4.8 46.8 %collective-permute-start.1 = (f32[3,48,1024]{2,1,0:T(8,128)}, f32[3,48,1024]{2,1,0:T(8,128)S(1)}, u32[]{:S(2)}, u32[]{:S(2)}) collective-permute-start(f32[3,48,1024]{2,1,0:T(8,128)} %get-tuple-element.137), channel_id=1, source_target_pairs={{4,0},{8,4},{12,8},{16,12},{20,16},{24,20},{28,24},{0,28},{5,1},{9... | collective-permute-start | bytes 1769480 | tf_op jit(solution)/shard_map/ppermute | solution.py:479
  14.4 38.8 %collective-permute-start.3 = (f32[2,2,6,48,128]{4,3,2,1,0:T(8,128)}, f32[2,2,6,48,128]{4,3,2,1,0:T(8,128)}, u32[]{:S(2)}, u32[]{:S(2)}) collective-permute-start(f32[2,2,6,48,128]{4,3,2,1,0:T(8,128)} %get-tuple-element.72.refs_1_), channel_id=1, source_target_pairs={{0,1},{1,0},{2,3},{3,2},{4,5},{5,4},{6,7},{7,6},{8,9},{9,8},{10,11... | collective-permute-start | bytes 1769480 | tf_op jit(solution)/shard_map/ppermute | solution.py:556
  17.6 36.5 %collective-permute-start.5 = (f32[3,48,1024]{2,1,0:T(8,128)}, f32[3,48,1024]{2,1,0:T(8,128)}, u32[]{:S(2)}, u32[]{:S(2)}) collective-permute-start(f32[3,48,1024]{2,1,0:T(8,128)} %get-tuple-element.136), channel_id=1, source_target_pairs={{0,4},{4,8},{8,12},{12,16},{16,20},{20,24},{24,28},{28,0},{1,5},{5... | collective-permute-start | bytes 1769480 | tf_op jit(solution)/shard_map/ppermute | solution.py:479
  21.4 25.9 %collective-permute-start.17 = (f32[1,192,256]{2,1,0:T(8,128)S(1)}, f32[1,192,256]{2,1,0:T(8,128)S(1)}, u32[]{:S(2)}, u32[]{:S(2)}) collective-permute-start(f32[1,192,256]{2,1,0:T(8,128)S(1)} %get-tuple-element.142), channel_id=1, source_target_pairs={{0,4},{4,8},{8,12},{12,16},{16,20},{20,24},{24,28},{28,0},{1,5},{5... | collective-permute-start | bytes 589832 | tf_op jit(solution)/shard_map/ppermute | solution.py:479
  30.5 11.5 %copy-start.5 = (bf16[384,3,4,48]{0,3,2,1:T(8,128)(2,1)S(1)}, bf16[384,3,4,48]{0,3,2,1:T(8,128)(2,1)}, u32[]{:S(2)}) copy-start(bf16[384,3,4,48]{0,3,2,1:T(8,128)(2,1)} %constant.160.clone2.1) | copy-start | bytes 1327108
  42.6 2.7 copy-start.22
  42.6 4.0 %copy-start.23 = (f32[4]{0:T(128)S(1)}, f32[4]{0:T(128)}, u32[]{:S(2)}) copy-start(f32[4]{0:T(128)} %constant.166.clone) | copy-start | bytes 52
  42.7 4.0 %copy-start.24 = (f32[4]{0:T(128)S(1)}, f32[4]{0:T(128)}, u32[]{:S(2)}) copy-start(f32[4]{0:T(128)} %constant.167.clone) | copy-start | bytes 52
  42.7 7.0 %copy-start.14 = (bf16[2,4,48,192]{3,2,1,0:T(8,128)(2,1)S(1)}, bf16[2,4,48,192]{3,2,1,0:T(8,128)(2,1)}, u32[]{:S(2)}) copy-start(bf16[2,4,48,192]{3,2,1,0:T(8,128)(2,1)} %constant.163.clone2.1) | copy-start | bytes 442372
  42.8 7.4 %copy-start.13 = (bf16[2,4,48,192]{3,2,1,0:T(8,128)(2,1)S(1)}, bf16[2,4,48,192]{3,2,1,0:T(8,128)(2,1)}, u32[]{:S(2)}) copy-start(bf16[2,4,48,192]{3,2,1,0:T(8,128)(2,1)} %constant.162.clone2.1) | copy-start | bytes 442372
  43.4 23.7 %copy-start.21 = (s32[4]{0:T(128)}, s32[4]{0:T(128)S(1)}, u32[]{:S(2)}) copy-start(s32[4]{0:T(128)S(1)} %get-tuple-element.130.order_ref) | copy-start | bytes 52
  47.3 19.9 %copy-start.6 = (f32[1,192,256]{2,1,0:T(8,128)}, f32[1,192,256]{2,1,0:T(8,128)S(1)}, u32[]{:S(2)}) copy-start(f32[1,192,256]{2,1,0:T(8,128)S(1)} %collective-permute-done.17.refs_9_) | copy-start | bytes 589828
  47.3 20.0 %collective-permute-start.6 = (f32[3,48,1024]{2,1,0:T(8,128)}, f32[3,48,1024]{2,1,0:T(8,128)}, u32[]{:S(2)}, u32[]{:S(2)}) collective-permute-start(f32[3,48,1024]{2,1,0:T(8,128)} %get-tuple-element.135), channel_id=1, source_target_pairs={{4,0},{8,4},{12,8},{16,12},{20,16},{24,20},{28,24},{0,28},{5,1},{9... | collective-permute-start | bytes 1769480 | tf_op jit(solution)/shard_map/ppermute | solution.py:479
  47.7 6.6 %copy-start = (f32[3,48,1024]{2,1,0:T(8,128)}, f32[3,48,1024]{2,1,0:T(8,128)S(1)}, u32[]{:S(2)}) copy-start(f32[3,48,1024]{2,1,0:T(8,128)S(1)} %collective-permute-done.tx_ref.t_ref) | copy-start | bytes 1769476
  47.7 20.9 %collective-permute-start.8 = (f32[2,2,6,48,128]{4,3,2,1,0:T(8,128)}, f32[2,2,6,48,128]{4,3,2,1,0:T(8,128)}, u32[]{:S(2)}, u32[]{:S(2)}) collective-permute-start(f32[2,2,6,48,128]{4,3,2,1,0:T(8,128)} %get-tuple-element.81.refs_1_), channel_id=1, source_target_pairs={{0,1},{1,0},{2,3},{3,2},{4,5},{5,4},{6,7},{7,6},{8,9},{9,8},{10,11... | collective-permute-start | bytes 1769480 | tf_op jit(solution)/shard_map/ppermute | solution.py:556
  51.6 2.7 copy-start.1
  51.6 31.0 %collective-permute-start.10 = (f32[3,48,1024]{2,1,0:T(8,128)}, f32[3,48,1024]{2,1,0:T(8,128)}, u32[]{:S(2)}, u32[]{:S(2)}) collective-permute-start(f32[3,48,1024]{2,1,0:T(8,128)} %get-tuple-element.134), channel_id=1, source_target_pairs={{0,4},{4,8},{8,12},{12,16},{16,20},{20,24},{24,28},{28,0},{1,5},{5... | collective-permute-start | bytes 1769480 | tf_op jit(solution)/shard_map/ppermute | solution.py:479
  53.2 30.8 %collective-permute-start.11 = (f32[3,48,1024]{2,1,0:T(8,128)}, f32[3,48,1024]{2,1,0:T(8,128)}, u32[]{:S(2)}, u32[]{:S(2)}) collective-permute-start(f32[3,48,1024]{2,1,0:T(8,128)} %get-tuple-element.133), channel_id=1, source_target_pairs={{4,0},{8,4},{12,8},{16,12},{20,16},{24,20},{28,24},{0,28},{5,1},{9... | collective-permute-start | bytes 1769480 | tf_op jit(solution)/shard_map/ppermute | solution.py:479
  54.1 30.1 %collective-permute-start.22 = (f32[2,2,6,48,128]{4,3,2,1,0:T(8,128)}, f32[2,2,6,48,128]{4,3,2,1,0:T(8,128)}, u32[]{:S(2)}, u32[]{:S(2)}) collective-permute-start(f32[2,2,6,48,128]{4,3,2,1,0:T(8,128)} %get-tuple-element.71.refs_0_), channel_id=1, source_target_pairs={{0,1},{1,0},{2,3},{3,2},{4,5},{5,4},{6,7},{7,6},{8,9},{9,8},{10,11... | collective-permute-start | bytes 1769480 | tf_op jit(solution)/shard_map/ppermute | solution.py:556
  67.2 31.9 %collective-permute-start.25 = (f32[2,2,6,48,128]{4,3,2,1,0:T(8,128)}, f32[2,2,6,48,128]{4,3,2,1,0:T(8,128)}, u32[]{:S(2)}, u32[]{:S(2)}) collective-permute-start(f32[2,2,6,48,128]{4,3,2,1,0:T(8,128)} %get-tuple-element.80.refs_0_), channel_id=1, source_target_pairs={{0,1},{1,0},{2,3},{3,2},{4,5},{5,4},{6,7},{7,6},{8,9},{9,8},{10,11... | collective-permute-start | bytes 1769480 | tf_op jit(solution)/shard_map/ppermute | solution.py:556
  68.6 30.9 %collective-permute-start.28 = (f32[2,2,6,48,128]{4,3,2,1,0:T(8,128)}, f32[2,2,6,48,128]{4,3,2,1,0:T(8,128)}, u32[]{:S(2)}, u32[]{:S(2)}) collective-permute-start(f32[2,2,6,48,128]{4,3,2,1,0:T(8,128)} %get-tuple-element.88.refs_0_), channel_id=1, source_target_pairs={{0,1},{1,0},{2,3},{3,2},{4,5},{5,4},{6,7},{7,6},{8,9},{9,8},{10,11... | collective-permute-start | bytes 1769480 | tf_op jit(solution)/shard_map/ppermute | solution.py:556
  68.8 13.9 %copy-start.8 = (f32[2,2,6,48,128]{4,3,2,1,0:T(8,128)S(1)}, f32[2,2,6,48,128]{4,3,2,1,0:T(8,128)}, u32[]{:S(2)}) copy-start(f32[2,2,6,48,128]{4,3,2,1,0:T(8,128)} %get-tuple-element.89.refs_1_) | copy-start | bytes 1769476
  68.8 15.3 %copy-start.26 = (f32[2,1,6,48,128]{4,3,2,1,0:T(8,128)S(1)}, f32[2,1,6,48,128]{4,3,2,1,0:T(8,128)}, u32[]{:S(2)}) copy-start(f32[2,1,6,48,128]{4,3,2,1,0:T(8,128)} %get-tuple-element.102) | copy-start | bytes 884740
  82.7 59.8 %collective-permute-start.13 = (f32[2,2,6,48,128]{4,3,2,1,0:T(8,128)S(1)}, f32[2,2,6,48,128]{4,3,2,1,0:T(8,128)S(1)}, u32[]{:S(2)}, u32[]{:S(2)}) collective-permute-start(f32[2,2,6,48,128]{4,3,2,1,0:T(8,128)S(1)} %copy-done.8), channel_id=1, source_target_pairs={{0,1},{1,0},{2,3},{3,2},{4,5},{5,4},{6,7},{7,6},{8,9},{9,8},{10,11... | collective-permute-start | bytes 1769480 | tf_op jit(solution)/shard_map/ppermute | solution.py:556
  84.0 33.8 %collective-permute-start.21 = (f32[2,1,6,48,128]{4,3,2,1,0:T(8,128)S(1)}, f32[2,1,6,48,128]{4,3,2,1,0:T(8,128)}, u32[]{:S(2)}, u32[]{:S(2)}) collective-permute-start(f32[2,1,6,48,128]{4,3,2,1,0:T(8,128)S(1)} %copy-done.26), channel_id=1, source_target_pairs={{0,1},{1,0},{2,3},{3,2},{4,5},{5,4},{6,7},{7,6},{8,9},{9,8},{10,11... | collective-permute-start | bytes 884744 | tf_op jit(solution)/shard_map/ppermute | solution.py:558
  84.2 39.9 %collective-permute-start.24 = (f32[2,1,6,48,128]{4,3,2,1,0:T(8,128)}, f32[2,1,6,48,128]{4,3,2,1,0:T(8,128)}, u32[]{:S(2)}, u32[]{:S(2)}) collective-permute-start(f32[2,1,6,48,128]{4,3,2,1,0:T(8,128)} %get-tuple-element.106), channel_id=1, source_target_pairs={{0,1},{1,0},{2,3},{3,2},{4,5},{5,4},{6,7},{7,6},{8,9},{9,8},{10,11... | collective-permute-start | bytes 884744 | tf_op jit(solution)/shard_map/ppermute | solution.py:558
  99.2 31.2 %collective-permute-start.27 = (f32[2,1,6,48,128]{4,3,2,1,0:T(8,128)}, f32[2,1,6,48,128]{4,3,2,1,0:T(8,128)}, u32[]{:S(2)}, u32[]{:S(2)}) collective-permute-start(f32[2,1,6,48,128]{4,3,2,1,0:T(8,128)} %get-tuple-element.110), channel_id=1, source_target_pairs={{0,1},{1,0},{2,3},{3,2},{4,5},{5,4},{6,7},{7,6},{8,9},{9,8},{10,11... | collective-permute-start | bytes 884744 | tf_op jit(solution)/shard_map/ppermute | solution.py:558
  99.5 43.1 %collective-permute-start.2 = (f32[2,1,6,48,128]{4,3,2,1,0:T(8,128)}, f32[2,1,6,48,128]{4,3,2,1,0:T(8,128)}, u32[]{:S(2)}, u32[]{:S(2)}) collective-permute-start(f32[2,1,6,48,128]{4,3,2,1,0:T(8,128)} %get-tuple-element.76), channel_id=1, source_target_pairs={{0,1},{1,0},{2,3},{3,2},{4,5},{5,4},{6,7},{7,6},{8,9},{9,8},{10,11... | collective-permute-start | bytes 884744 | tf_op jit(solution)/shard_map/ppermute | solution.py:558
  117.8 38.0 %collective-permute-start.7 = (f32[2,1,6,48,128]{4,3,2,1,0:T(8,128)}, f32[2,1,6,48,128]{4,3,2,1,0:T(8,128)}, u32[]{:S(2)}, u32[]{:S(2)}) collective-permute-start(f32[2,1,6,48,128]{4,3,2,1,0:T(8,128)} %get-tuple-element.85), channel_id=1, source_target_pairs={{0,1},{1,0},{2,3},{3,2},{4,5},{5,4},{6,7},{7,6},{8,9},{9,8},{10,11... | collective-permute-start | bytes 884744 | tf_op jit(solution)/shard_map/ppermute | solution.py:558
  124.1 39.2 %collective-permute-start.12 = (f32[2,1,6,48,128]{4,3,2,1,0:T(8,128)}, f32[2,1,6,48,128]{4,3,2,1,0:T(8,128)}, u32[]{:S(2)}, u32[]{:S(2)}) collective-permute-start(f32[2,1,6,48,128]{4,3,2,1,0:T(8,128)} %get-tuple-element.93), channel_id=1, source_target_pairs={{0,1},{1,0},{2,3},{3,2},{4,5},{5,4},{6,7},{7,6},{8,9},{9,8},{10,11... | collective-permute-start | bytes 884744 | tf_op jit(solution)/shard_map/ppermute | solution.py:558
  130.4 46.2 %collective-permute-start.23 = (f32[6,192,128]{2,1,0:T(8,128)}, f32[6,192,128]{2,1,0:T(8,128)S(1)}, u32[]{:S(2)}, u32[]{:S(2)}) collective-permute-start(f32[6,192,128]{2,1,0:T(8,128)} %get-tuple-element.104), channel_id=1, source_target_pairs={{0,2},{1,3},{2,0},{3,1},{4,6},{5,7},{6,4},{7,5},{8,10},{9,11},{10,... | collective-permute-start | bytes 1769480 | tf_op jit(solution)/shard_map/ppermute | solution.py:545
  142.5 20.9 %copy-start.25 = (f32[2,2,6,48,128]{4,3,2,1,0:T(8,128)}, f32[2,2,6,48,128]{4,3,2,1,0:T(8,128)S(1)}, u32[]{:S(2)}) copy-start(f32[2,2,6,48,128]{4,3,2,1,0:T(8,128)S(1)} %collective-permute-done.13.rs_ref) | copy-start | bytes 1769476
  142.5 80.9 %collective-permute-start.26 = (f32[6,192,128]{2,1,0:T(8,128)}, f32[6,192,128]{2,1,0:T(8,128)}, u32[]{:S(2)}, u32[]{:S(2)}) collective-permute-start(f32[6,192,128]{2,1,0:T(8,128)} %get-tuple-element.108), channel_id=1, source_target_pairs={{0,2},{1,3},{2,0},{3,1},{4,6},{5,7},{6,4},{7,5},{8,10},{9,11},{10,... | collective-permute-start | bytes 1769480 | tf_op jit(solution)/shard_map/ppermute | solution.py:545
  142.6 99.8 %collective-permute-start.29 = (f32[6,192,128]{2,1,0:T(8,128)}, f32[6,192,128]{2,1,0:T(8,128)}, u32[]{:S(2)}, u32[]{:S(2)}) collective-permute-start(f32[6,192,128]{2,1,0:T(8,128)} %get-tuple-element.112), channel_id=1, source_target_pairs={{0,2},{1,3},{2,0},{3,1},{4,6},{5,7},{6,4},{7,5},{8,10},{9,11},{10,... | collective-permute-start | bytes 1769480 | tf_op jit(solution)/shard_map/ppermute | solution.py:545
  155.8 19.9 %collective-permute-start.18 = (f32[1,192,256]{2,1,0:T(8,128)}, f32[1,192,256]{2,1,0:T(8,128)S(1)}, u32[]{:S(2)}, u32[]{:S(2)}) collective-permute-start(f32[1,192,256]{2,1,0:T(8,128)} %get-tuple-element.141), channel_id=1, source_target_pairs={{4,0},{8,4},{12,8},{16,12},{20,16},{24,20},{28,24},{0,28},{5,1},{9... | collective-permute-start | bytes 589832 | tf_op jit(solution)/shard_map/ppermute | solution.py:479
  163.3 104.1 %collective-permute-start.4 = (f32[6,192,128]{2,1,0:T(8,128)}, f32[6,192,128]{2,1,0:T(8,128)S(1)}, u32[]{:S(2)}, u32[]{:S(2)}) collective-permute-start(f32[6,192,128]{2,1,0:T(8,128)} %get-tuple-element.78), channel_id=1, source_target_pairs={{0,2},{1,3},{2,0},{3,1},{4,6},{5,7},{6,4},{7,5},{8,10},{9,11},{10,... | collective-permute-start | bytes 1769480 | tf_op jit(solution)/shard_map/ppermute | solution.py:545
  176.4 113.1 %collective-permute-start.9 = (f32[6,192,128]{2,1,0:T(8,128)}, f32[6,192,128]{2,1,0:T(8,128)S(1)}, u32[]{:S(2)}, u32[]{:S(2)}) collective-permute-start(f32[6,192,128]{2,1,0:T(8,128)} %get-tuple-element.87), channel_id=1, source_target_pairs={{0,2},{1,3},{2,0},{3,1},{4,6},{5,7},{6,4},{7,5},{8,10},{9,11},{10,... | collective-permute-start | bytes 1769480 | tf_op jit(solution)/shard_map/ppermute | solution.py:545
  176.6 85.1 %copy-start.3 = (f32[6,192,128]{2,1,0:T(8,128)}, f32[6,192,128]{2,1,0:T(8,128)S(1)}, u32[]{:S(2)}) copy-start(f32[6,192,128]{2,1,0:T(8,128)S(1)} %collective-permute-done.23.refs_1_.refs_10_) | copy-start | bytes 1769476
  176.6 112.9 %collective-permute-start.14 = (f32[6,192,128]{2,1,0:T(8,128)}, f32[6,192,128]{2,1,0:T(8,128)}, u32[]{:S(2)}, u32[]{:S(2)}) collective-permute-start(f32[6,192,128]{2,1,0:T(8,128)} %get-tuple-element.95), channel_id=1, source_target_pairs={{0,2},{1,3},{2,0},{3,1},{4,6},{5,7},{6,4},{7,5},{8,10},{9,11},{10,... | collective-permute-start | bytes 1769480 | tf_op jit(solution)/shard_map/ppermute | solution.py:545
  223.4 37.0 %collective-permute-start.30 = (f32[192,128]{1,0:T(8,128)S(1)}, f32[192,128]{1,0:T(8,128)S(1)}, u32[]{:S(2)}, u32[]{:S(2)}) collective-permute-start(f32[192,128]{1,0:T(8,128)S(1)} %get-tuple-element.140), channel_id=1, source_target_pairs={{0,4},{4,8},{8,12},{12,16},{16,20},{20,24},{24,28},{28,0},{1,5},{5... | collective-permute-start | bytes 294920 | tf_op jit(solution)/shard_map/ppermute | solution.py:479
  242.4 18.4 %collective-permute-start.31 = (f32[192,128]{1,0:T(8,128)S(1)}, f32[192,128]{1,0:T(8,128)S(1)}, u32[]{:S(2)}, u32[]{:S(2)}) collective-permute-start(f32[192,128]{1,0:T(8,128)S(1)} %get-tuple-element.139), channel_id=1, source_target_pairs={{4,0},{8,4},{12,8},{16,12},{20,16},{24,20},{28,24},{0,28},{5,1},{9... | collective-permute-start | bytes 294920 | tf_op jit(solution)/shard_map/ppermute | solution.py:479
  266.4 4.0 %collective-permute-start.32 = (f32[2,192,128]{2,1,0:T(8,128)}, f32[2,192,128]{2,1,0:T(8,128)S(1)}, u32[]{:S(2)}, u32[]{:S(2)}) collective-permute-start(f32[2,192,128]{2,1,0:T(8,128)} %get-tuple-element.115), channel_id=1, source_target_pairs={{0,4},{4,8},{8,12},{12,16},{16,20},{20,24},{24,28},{28,0},{1,5},{5... | collective-permute-start | bytes 589832 | tf_op jit(solution)/shard_map/ppermute | solution.py:479
  266.4 11.6 %collective-permute-start.33 = (f32[2,192,128]{2,1,0:T(8,128)}, f32[2,192,128]{2,1,0:T(8,128)S(1)}, u32[]{:S(2)}, u32[]{:S(2)}) collective-permute-start(f32[2,192,128]{2,1,0:T(8,128)} %get-tuple-element.116), channel_id=1, source_target_pairs={{4,0},{8,4},{12,8},{16,12},{20,16},{24,20},{28,24},{0,28},{5,1},{9... | collective-permute-start | bytes 589832 | tf_op jit(solution)/shard_map/ppermute | solution.py:479
  267.4 19.6 %copy-start.2 = (f32[6,192,128]{2,1,0:T(8,128)}, f32[6,192,128]{2,1,0:T(8,128)S(1)}, u32[]{:S(2)}) copy-start(f32[6,192,128]{2,1,0:T(8,128)S(1)} %collective-permute-done.4.refs_1_.refs_10_) | copy-start | bytes 1769476
  268.6 20.9 %collective-permute-start.15 = (f32[192,128]{1,0:T(8,128)S(1)}, f32[192,128]{1,0:T(8,128)}, u32[]{:S(2)}, u32[]{:S(2)}) collective-permute-start(f32[192,128]{1,0:T(8,128)S(1)} %get-tuple-element.144), channel_id=1, source_target_pairs={{0,4},{4,8},{8,12},{12,16},{16,20},{20,24},{24,28},{28,0},{1,5},{5... | collective-permute-start | bytes 294920 | tf_op jit(solution)/shard_map/ppermute | solution.py:479
  270.4 7.6 %copy-start.15 = (f32[2,192,128]{2,1,0:T(8,128)}, f32[2,192,128]{2,1,0:T(8,128)S(1)}, u32[]{:S(2)}) copy-start(f32[2,192,128]{2,1,0:T(8,128)S(1)} %collective-permute-done.32.refs_2_) | copy-start | bytes 589828
  270.4 19.1 %collective-permute-start.16 = (f32[192,128]{1,0:T(8,128)S(1)}, f32[192,128]{1,0:T(8,128)}, u32[]{:S(2)}, u32[]{:S(2)}) collective-permute-start(f32[192,128]{1,0:T(8,128)S(1)} %get-tuple-element.143), channel_id=1, source_target_pairs={{4,0},{8,4},{12,8},{16,12},{20,16},{24,20},{28,24},{0,28},{5,1},{9... | collective-permute-start | bytes 294920 | tf_op jit(solution)/shard_map/ppermute | solution.py:479
  278.0 0.7 copy-start.16
  287.0 28.4 %collective-permute-start.37 = (f32[3,6,48,128]{3,2,1,0:T(8,128)}, f32[3,6,48,128]{3,2,1,0:T(8,128)S(1)}, u32[]{:S(2)}, u32[]{:S(2)}) collective-permute-start(f32[3,6,48,128]{3,2,1,0:T(8,128)} %get-tuple-element.124), channel_id=1, source_target_pairs={{0,1},{1,0},{2,3},{3,2},{4,5},{5,4},{6,7},{7,6},{8,9},{9,8},{10,11... | collective-permute-start | bytes 1327112 | tf_op jit(solution)/shard_map/ppermute | solution.py:608
  289.5 0.8 copy-start.4
  294.9 5.1 %collective-permute-start.19 = (f32[2,192,128]{2,1,0:T(8,128)}, f32[2,192,128]{2,1,0:T(8,128)S(1)}, u32[]{:S(2)}, u32[]{:S(2)}) collective-permute-start(f32[2,192,128]{2,1,0:T(8,128)} %get-tuple-element.99), channel_id=1, source_target_pairs={{0,4},{4,8},{8,12},{12,16},{16,20},{20,24},{24,28},{28,0},{1,5},{5... | collective-permute-start | bytes 589832 | tf_op jit(solution)/shard_map/ppermute | solution.py:479
  294.9 7.5 %collective-permute-start.20 = (f32[2,192,128]{2,1,0:T(8,128)}, f32[2,192,128]{2,1,0:T(8,128)S(1)}, u32[]{:S(2)}, u32[]{:S(2)}) collective-permute-start(f32[2,192,128]{2,1,0:T(8,128)} %get-tuple-element.100), channel_id=1, source_target_pairs={{4,0},{8,4},{12,8},{16,12},{20,16},{24,20},{28,24},{0,28},{5,1},{9... | collective-permute-start | bytes 589832 | tf_op jit(solution)/shard_map/ppermute | solution.py:479
  296.1 28.5 %collective-permute-start.38 = (f32[3,6,48,128]{3,2,1,0:T(8,128)}, f32[3,6,48,128]{3,2,1,0:T(8,128)S(1)}, u32[]{:S(2)}, u32[]{:S(2)}) collective-permute-start(f32[3,6,48,128]{3,2,1,0:T(8,128)} %get-tuple-element.125), channel_id=1, source_target_pairs={{0,2},{1,3},{2,0},{3,1},{4,6},{5,7},{6,4},{7,5},{8,10},{9,11},{10,... | collective-permute-start | bytes 1327112 | tf_op jit(solution)/shard_map/ppermute | solution.py:608
  297.0 59.8 %collective-permute-start.39 = (f32[3,6,48,128]{3,2,1,0:T(8,128)}, f32[3,6,48,128]{3,2,1,0:T(8,128)S(1)}, u32[]{:S(2)}, u32[]{:S(2)}) collective-permute-start(f32[3,6,48,128]{3,2,1,0:T(8,128)} %get-tuple-element.126), channel_id=1, source_target_pairs={{0,3},{1,2},{2,1},{3,0},{4,7},{5,6},{6,5},{7,4},{8,11},{9,10},{10,... | collective-permute-start | bytes 1327112 | tf_op jit(solution)/shard_map/ppermute | solution.py:608
  300.1 2.3 copy-start.17
  302.4 0.7 copy-start.18
  312.9 56.1 %collective-permute-start.36 = (f32[3,6,48,128]{3,2,1,0:T(8,128)}, f32[3,6,48,128]{3,2,1,0:T(8,128)}, u32[]{:S(2)}, u32[]{:S(2)}) collective-permute-start(f32[3,6,48,128]{3,2,1,0:T(8,128)} %get-tuple-element.122), channel_id=1, source_target_pairs={{0,1},{1,0},{2,3},{3,2},{4,5},{5,4},{6,7},{7,6},{8,9},{9,8},{10,11... | collective-permute-start | bytes 1327112 | tf_op jit(solution)/shard_map/ppermute | solution.py:608
  312.9 65.1 %collective-permute-start.34 = (f32[3,6,48,128]{3,2,1,0:T(8,128)}, f32[3,6,48,128]{3,2,1,0:T(8,128)S(1)}, u32[]{:S(2)}, u32[]{:S(2)}) collective-permute-start(f32[3,6,48,128]{3,2,1,0:T(8,128)} %get-tuple-element.119), channel_id=1, source_target_pairs={{0,2},{1,3},{2,0},{3,1},{4,6},{5,7},{6,4},{7,5},{8,10},{9,11},{10,... | collective-permute-start | bytes 1327112 | tf_op jit(solution)/shard_map/ppermute | solution.py:608
  315.4 41.4 %copy-start.9 = (f32[3,6,48,128]{3,2,1,0:T(8,128)}, f32[3,6,48,128]{3,2,1,0:T(8,128)S(1)}, u32[]{:S(2)}) copy-start(f32[3,6,48,128]{3,2,1,0:T(8,128)S(1)} %collective-permute-done.37.refs_1_) | copy-start | bytes 1327108
  315.4 62.6 %collective-permute-start.35 = (f32[3,6,48,128]{3,2,1,0:T(8,128)}, f32[3,6,48,128]{3,2,1,0:T(8,128)}, u32[]{:S(2)}, u32[]{:S(2)}) collective-permute-start(f32[3,6,48,128]{3,2,1,0:T(8,128)} %get-tuple-element.120), channel_id=1, source_target_pairs={{0,3},{1,2},{2,1},{3,0},{4,7},{5,6},{6,5},{7,4},{8,11},{9,10},{10,... | collective-permute-start | bytes 1327112 | tf_op jit(solution)/shard_map/ppermute | solution.py:608
  324.6 32.2 %copy-start.10 = (f32[3,6,48,128]{3,2,1,0:T(8,128)}, f32[3,6,48,128]{3,2,1,0:T(8,128)S(1)}, u32[]{:S(2)}) copy-start(f32[3,6,48,128]{3,2,1,0:T(8,128)S(1)} %collective-permute-done.38.refs_2_) | copy-start | bytes 1327108
  356.8 0.8 copy-start.11
  378.0 0.7 copy-start.12
  (3 other events, 1.9 us)
where the time goes:
time: 390 us; the launch traced here: 388 us
  Pallas kernels  154 us (39%)
  waiting for transfers between devices  117 us (30%)
  starting transfers between devices  85.8 us (22%)
  local copies, waits for them, and re-layouts  18.6 us (5%)
  other arithmetic  11.2 us (3%)
    ppermute x16, starting transfers between devices, exchange(): return (lax.ppermute(last, 'gx', up), lax.ppermute(first, 'gx', down))  57.3 us
    ppermute x6, waiting for transfers between devices, z_part(): pieces.append(lax.ppermute(outs[s], 'yz', to))  45.8 us
    ppermute x6, waiting for transfers between devices, section(): got.append(lax.ppermute(outs[2 + place], 'yz', to))  41.2 us
    pallas_call x3, Pallas kernels, moving(): call(functools.partial(moving_field, c=c, omega=omega, chunks=chunks), 2...  40.4 us
    pallas_call x3, Pallas kernels, section(): call(functools.partial(y_inverse, terms=terms), 3 * y_flops * len(terms)...  29.5 us
    pallas_call x6, Pallas kernels, z_part(): call(z_partial, 2 * az.size * pairs * nx * cw, 10 * half_bytes // groups,...  29 us
    pallas_call x3, Pallas kernels, still(): call(functools.partial(still_fields, chunks=chunks), 2 * y_flops, 4 * hal...  27.3 us
    ppermute x6, waiting for transfers between devices, section(): r_w = [lax.ppermute(w[e], 'yz', twins) for e in range(chunks)]  27.2 us
  transfers between devices with their start and end apart: 40, of which 10 were waited for; matrix products, arithmetic and copies ran while one was open for 6% of the time, Pallas kernels for 37%

commit v1 on v0

v1 whole, which is shorter than its diff:
```python
import functools
import math

import jax
import jax.numpy as jnp
import ml_dtypes
import numpy as np
from jax import lax
from jax.experimental import pallas as pl
from jax.experimental.pallas import tpu as pltpu
from jax.sharding import PartitionSpec as P


viscosity = 0.05
time_step = 0.2
keep_weight = -5.0 / 9.0
section_weight = 15.0 / 16.0
shear_param = 1.5
fraction = 0.375

F32 = jnp.float32
BF16 = jnp.bfloat16
VMEM_LIMIT = 62 * 1024 * 1024


def np_parts(matrix):
    high = matrix.astype(np.float32).astype(ml_dtypes.bfloat16)
    low = (matrix - high.astype(np.float64)).astype(np.float32).astype(ml_dtypes.bfloat16)
    return high, low


def parts(x):
    high = x.astype(BF16)
    return high, (x - high.astype(F32)).astype(BF16)


def dot(x, y):
    return jnp.dot(x, y, preferred_element_type=F32)


def dot_t(x, y):
    return lax.dot_general(x, y, (((1,), (1,)), ((), ())), preferred_element_type=F32)


def dot3(a, b, op=dot):
    return op(a[0], b[0]) + (op(a[1], b[0]) + op(a[0], b[1]))


def swap(x):
    return pltpu.roll(x, x.shape[-1] // 2, axis=x.ndim - 1)


def sign_row(cols):
    lane = lax.broadcasted_iota(jnp.int32, (1, cols), 1)
    return jnp.where(lane < cols // 2, -1.0, 1.0).astype(F32)


def take_chunk(v, e, chunks):
    if chunks == 1:
        return v
    w = v.shape[-1] // 2
    lane = lax.broadcasted_iota(jnp.int32, v.shape[:-1] + (w,), v.ndim - 1)
    re, im = v[..., :w], v[..., w:]
    if e == 0:
        return jnp.where(lane < w // 2, re, swap(im))
    return jnp.where(lane < w // 2, swap(re), im)


def merge_chunks(a, b):
    w = a.shape[-1]
    lane = lax.broadcasted_iota(jnp.int32, a.shape, a.ndim - 1)
    re = jnp.where(lane < w // 2, a, swap(b))
    im = jnp.where(lane < w // 2, swap(a), b)
    return re, im


def pick(flag, a, b):
    return jnp.where(flag == 1, a, b)


def across(j, s, pairs):
    return j ^ s if pairs & (pairs - 1) == 0 else lax.rem(j + s, pairs)


def partner(i, place, groups):
    return i ^ place if groups & (groups - 1) == 0 else lax.rem(i + place, groups)


def sender(i, place, groups):
    return i ^ place if groups & (groups - 1) == 0 else lax.rem(i + groups - place, groups)


def mode_numbers(group, e, block_len, cols):
    lane = lax.broadcasted_iota(jnp.int32, (1, cols), 1)
    half = cols // 2
    return group * block_len + e * half + jnp.where(lane < half, lane, lane - half)


def y_fields(ids_ref, *refs, c, e, kind, slabs, chunks):
    moves, stays = kind != "still", kind != "moving"
    s = pl.program_id(0)
    pairs = pl.num_programs(0)
    refs = list(refs)
    u_ref = refs.pop(0)
    uz_ref = refs.pop(0) if stays else None
    if moves:
        ux_ref, uy_ref, tx_ref, t_ref, fx_ref, f_ref = refs[:6]
        refs = refs[6:]
    wh_ref, wl_ref = refs[:2]
    refs = refs[2:]
    if kind == "moving":
        us_send, us_keep = refs[:2]
        refs = refs[2:]
    send, keep, high, low = refs[:4]
    ghost = refs[4] if moves else None
    _, nx, nz, ny = u_ref.shape
    m = nx * nz
    cw = send.shape[-1]
    at_u, at_c = (0, m) if stays else (None, None)
    at_a, at_b = (2 * m, 3 * m) if stays else (0, m)
    group = ids_ref[2]
    bit = group & 1
    j = across(group >> 1, s, pairs)
    total_x = nx * slabs
    omega = 2.0 / total_x

    @pl.when(s == 0)
    def _():
        if moves:
            offset, slab = ids_ref[0], ids_ref[1]
            is_low, is_high = slab == 0, slab == slabs - 1
            shifts = (
                jnp.where(is_low, lax.rem(ny - offset, ny), 0),
                jnp.where(is_low, lax.rem(2 * ny - 1 - offset, ny), 0),
                jnp.where(is_high, offset, 0),
                jnp.where(is_high, lax.rem(offset + 1, ny), 0),
            )
            mix = (
                jnp.where(is_low, 1.0 - fraction, 1.0),
                jnp.where(is_low, fraction, 0.0),
                jnp.where(is_high, 1.0 - fraction, 1.0),
                jnp.where(is_high, fraction, 0.0),
            )
            for i, (tail, front) in enumerate(((tx_ref, fx_ref), (t_ref, f_ref))):
                if i and not c:
                    continue
                for d in range(3):
                    t = tail[d]
                    ghost[i, d] = mix[0] * pltpu.roll(t, shifts[0], axis=1) + mix[1] * pltpu.roll(
                        t, shifts[1], axis=1
                    )
                    f = front[d]
                    ghost[i, 3 + d] = mix[2] * pltpu.roll(f, shifts[2], axis=1) + mix[
                        3
                    ] * pltpu.roll(f, shifts[3], axis=1)

        def chunk(i, carry):
            lanes = pl.ds(pl.multiple_of(i * 128, 128), 128)

            def put(at, value):
                h, l = parts(value)
                high[at : at + nz, lanes] = h
                low[at : at + nz, lanes] = l

            def plane(which, x):
                if x < 0:
                    return ghost[which, x + 3, :, lanes]
                if x >= nx:
                    return ghost[which, x - nx + 3, :, lanes]
                return (u_ref if which else ux_ref)[0, x, :, lanes]

            for x in range(nx):
                if stays:
                    u = u_ref[0, x, :, lanes]
                    put(at_u + x * nz, u)
                    put(at_c + x * nz, -uz_ref[0, x, :, lanes] * u)
                if not moves:
                    continue
                place = (ids_ref[1] * nx + x).astype(F32) + (0.5 - total_x / 2.0)
                ux = [plane(0, x + d) for d in range(-3, 4)]
                uy = uy_ref[0, x, :, lanes]
                moving = uy + (-shear_param * omega) * place
                v = ux if c == 0 else [plane(1, x + d) for d in range(-3, 4)]
                f = [ux[d] * v[d] for d in range(7) if d != 3]
                d1 = (45.0 * (f[3] - f[2]) - 9.0 * (f[4] - f[1]) + (f[5] - f[0])) * (1.0 / 60.0)
                d2 = (
                    2.0 * (v[6] + v[0])
                    - 27.0 * (v[5] + v[1])
                    + 270.0 * (v[4] + v[2])
                    - 490.0 * v[3]
                ) * (1.0 / 180.0)
                a = viscosity * d2 - d1
                if c == 0:
                    a = a + (2.0 * omega) * uy
                if c == 1:
                    a = a - ((2.0 - shear_param) * omega) * ux[3]
                put(at_a + x * nz, a)
                put(at_b + x * nz, -moving * v[3])
            return carry

        lax.fori_loop(0, ny // 128, chunk, 0)

    out = dot3((high[...], low[...]), (wh_ref[0, j], wl_ref[0, j]))
    sign = sign_row(cw)
    halves = []
    for b in range(2):
        o = out[:, b * cw : (b + 1) * cw]
        got = [o[at_u : at_u + m], o[at_c : at_c + m]] if stays else []
        if moves:
            modes = mode_numbers(2 * j + b, e, cw * chunks // 2, cw)
            k = (2.0 * math.pi / ny) * modes.astype(F32)
            if stays:
                yu = got[0]
            else:
                sent, kept = us_send[0, 0].reshape(m, cw), us_keep[0, 0].reshape(m, cw)
                yu = pick(bit, kept, sent) if b else pick(bit, sent, kept)
            got.append(
                o[at_a : at_a + m] + swap(o[at_b : at_b + m]) * (k * sign) - viscosity * (k * k) * yu
            )
        halves.append(got)
    for f, (lo, hi) in enumerate(zip(*halves)):
        send[0, f] = pick(bit, lo, hi).reshape(nx, nz, cw)
        keep[0, f] = pick(bit, hi, lo).reshape(nx, nz, cw)


def z_partial(ids_ref, *refs, layout):
    count = 2 * (max(a for a, _ in layout) + 1)
    az_ref, outs = refs[count], refs[count + 1 :]
    pairs, _, zb, _, cw = refs[0].shape
    depth = outs[0].shape[1]
    bit = ids_ref[2] & 1
    matrix = az_ref[ids_ref[2] >> 1]
    sign = sign_row(cw)
    for at in tuple(range(1, pairs)) + (0,):
        ref = outs[at]
        for x0 in range(0, zb, 2):
            xs = range(x0, min(x0 + 2, zb))
            columns = []
            for x in xs:
                rows = []
                for a, f in layout:
                    kept, got = refs[2 * a][at, f, x], refs[2 * a + 1][at, f, x]
                    rows += [pick(bit, got, kept), pick(bit, kept, got)]
                columns.append(jnp.concatenate(rows, axis=0))
            h, l = parts(jnp.concatenate(columns, axis=-1))
            out = dot(matrix, jnp.concatenate([h, h, l], axis=0))
            for i, x in enumerate(xs):
                lanes = slice(i * cw, (i + 1) * cw)
                ref[x] = out[:depth, lanes] + swap(out[depth:, lanes]) * sign


def first_sweep(*refs, e, chunks, pieces):
    tx, ty, tz = (refs[c * pieces : (c + 1) * pieces] for c in range(3))
    (
        p_ref, txl_ref, txh_ref, pl_ref, ph_ref, rot_ref, ky_ref, kz_ref, rden_ref,
        div_ref, out_ref, lo_ref, hi_ref,
    ) = refs[3 * pieces :]
    nx, _, cols = div_ref.shape
    sign = sign_row(cols)
    ky = ky_ref[...] * sign
    kz = kz_ref[...] * sign
    rden = rden_ref[...]

    def total(pieces_of, x):
        out = pieces_of[0][x]
        for ref in pieces_of[1:]:
            out = out + ref[x]
        return out

    def rot(v, k):
        return v * rot_ref[2 * k : 2 * k + 1] + swap(v) * rot_ref[2 * k + 1 : 2 * k + 2]

    def guess(v):
        return take_chunk(v, e, chunks)

    for x in range(nx):
        below = total(tx, x - 1) if x else rot(txl_ref[...], 0)
        above = total(tx, x + 1) if x < nx - 1 else rot(txh_ref[...], 1)
        p_below = guess(p_ref[x - 1]) if x else rot(guess(pl_ref[0]), 0)
        p_above = guess(p_ref[x + 1]) if x < nx - 1 else rot(guess(ph_ref[0]), 1)
        div = 0.5 * (above - below) + swap(total(ty, x)) * ky + swap(total(tz, x)) * kz
        div_ref[x] = div
        p = (p_above + p_below - div) * rden
        out_ref[x] = p
        if x == 0:
            lo_ref[0] = p
            lo_ref[1] = -div
        if x == 1:
            lo_ref[1] = lo_ref[1] + p
        if x == nx - 2:
            hi_ref[1] = p
        if x == nx - 1:
            hi_ref[0] = p
            hi_ref[1] = hi_ref[1] - div


def finish(ids_ref, *refs, e, chunks, pieces, groups):
    p1_ref, div_ref, lo_ref, hi_ref, rot_ref, ky_ref, kz_ref, rden_ref, ck_ref = refs[:9]
    refs = refs[9:]
    t_refs = [refs[c * pieces : (c + 1) * pieces] for c in range(3)]
    q_ref, bh_ref, bl_ref = refs[3 * pieces : 3 * pieces + 3]
    refs = refs[3 * pieces + 3 :]
    last = e == chunks - 1
    earlier = chunks > 1 and last
    if earlier:
        q_first, p_first = refs[:2]
        refs = refs[2:]
    qn_ref, p_ref = refs[:2]
    h_refs, press, hs = refs[2:-2], refs[-2], refs[-1]
    nx, depth, cols = p1_ref.shape
    step = pl.program_id(0)
    _, planes, nz, _ = h_refs[0].shape
    sign = sign_row(cols)

    @pl.when(step == 0)
    def _():
        rden = rden_ref[...]

        def rot(v, k):
            return v * rot_ref[2 * k : 2 * k + 1] + swap(v) * rot_ref[2 * k + 1 : 2 * k + 2]

        low = rot(lo_ref[0], 0)
        high = rot(hi_ref[0], 1)
        press[0] = (p1_ref[0] + rot(lo_ref[1], 0)) * rden
        press[nx + 1] = (p1_ref[nx - 1] + rot(hi_ref[1], 1)) * rden
        for i in range(nx):
            below = p1_ref[i - 1] if i else low
            above = p1_ref[i + 1] if i < nx - 1 else high
            press[i + 1] = (above + below - div_ref[i]) * rden

    def leave(ref, at, value, first):
        if earlier:
            re, im = merge_chunks(first, value)
            ref[at + (slice(None), slice(0, cols))] = re
            ref[at + (slice(None), slice(cols, 2 * cols))] = im
        else:
            ref[at] = value

    for i in range(planes):
        x = step * planes + i
        p = press[x + 1]
        leave(p_ref, (i,), p, p_first[i] if earlier else None)
        turned = swap(p) * sign
        grads = (0.5 * (press[x + 2] - press[x]), turned * ky_ref[...], turned * kz_ref[...])
        fresh = []
        for c in range(3):
            t = t_refs[c][0][i]
            for ref in t_refs[c][1:]:
                t = t + ref[i]
            q = keep_weight * take_chunk(q_ref[c, i], e, chunks) + time_step * (t - grads[c])
            leave(qn_ref, (c, i), q, q_first[c, i] if earlier else None)
            fresh.append(q)
        out = dot3((bh_ref[...], bl_ref[...]), parts(jnp.concatenate(fresh, axis=-1)))
        for c in range(3):
            lanes = slice(c * cols, (c + 1) * cols)
            hs[c] = (out[:depth, lanes] + swap(out[depth:, lanes]) * sign) * ck_ref[...]
            for place, ref in enumerate(h_refs):
                to = partner(ids_ref[2], place, groups)
                ref[c, i] = hs[c, pl.ds(pl.multiple_of(to * nz, 8), nz)]


def y_inverse(ids_ref, *refs, terms, groups):
    base_ref, wh_ref, wl_ref, out_ref, th, tl = refs[-6:]
    blocks = refs[:-6]
    _, xb, nz, cols = blocks[0].shape

    @pl.when((pl.program_id(0) == 0) & (pl.program_id(1) == 0))
    def _():
        for i, (e, place) in enumerate(terms):
            g = sender(ids_ref[2], place, groups)
            at = slice(i * cols, (i + 1) * cols)
            for b in range(2):
                lanes = slice(b * cols, (b + 1) * cols)

                @pl.when(g & 1 == b)
                def _():
                    th[:, at] = wh_ref[e, g >> 1, :, lanes]
                    tl[:, at] = wl_ref[e, g >> 1, :, lanes]

    rows = jnp.concatenate([b[0].reshape(xb * nz, cols) for b in blocks], axis=-1)
    total = dot3(parts(rows), (th[...], tl[...]), dot_t)
    ny = total.shape[-1]
    out_ref[0] = base_ref[0] + section_weight * total.reshape(xb, nz, ny)


def whole(shape):
    return pl.BlockSpec(shape, lambda *_: (0,) * len(shape))


SMEM = pl.BlockSpec(memory_space=pltpu.SMEM)


def shaped(*shape):
    return jax.ShapeDtypeStruct(shape, F32)


def call(body, flops, moved, **kw):
    return pl.pallas_call(
        body,
        compiler_params=pltpu.CompilerParams(vmem_limit_bytes=VMEM_LIMIT),
        cost_estimate=pl.CostEstimate(flops=int(flops), bytes_accessed=int(moved), transcendentals=0),
        **kw,
    )


def section(vel, q_old, pressure_guess, shear_shift):
    _, nx, nz, ny = vel.shape
    depth = q_old.shape[2]
    groups = lax.axis_size("yz")
    slabs = lax.axis_size("gx")
    pairs = groups // 2
    cols = ny // groups
    chunks = 2 if cols % 256 == 0 else 1
    cw = cols // chunks
    half = cw // 2
    block_len = cols // 2
    ids = jnp.stack(
        [shear_shift[0], lax.axis_index("gx").astype(jnp.int32), lax.axis_index("yz").astype(jnp.int32)]
    )

    modes = np.arange(ny // 2).reshape(pairs, 2, chunks, half).transpose(2, 0, 1, 3)[:, :, None]
    angle = 2.0 * np.pi / ny * (np.arange(ny).reshape(1, 1, ny, 1, 1) * modes % ny)
    table = np.concatenate([np.cos(angle), -np.sin(angle)], axis=-1) / math.sqrt(ny)
    wh, wl = (jnp.asarray(t) for t in np_parts(table.reshape(chunks, pairs, ny, 2 * cw)))
    kz_np = np.fft.fftfreq(depth) * 2.0 * np.pi
    angle_z = 2.0 * np.pi / depth * (np.arange(depth)[:, None] * np.arange(depth)[None, :] % depth)
    cz = np.cos(angle_z) / math.sqrt(depth)
    sz = np.sin(angle_z) / math.sqrt(depth)
    k1 = kz_np[:, None]
    k2 = viscosity * k1 * k1
    forward = np.concatenate(
        [
            np.concatenate([cz, k1 * sz, -k2 * cz], axis=1),
            np.concatenate([-sz, k1 * cz, k2 * sz], axis=1),
        ],
        axis=0,
    )
    forward = forward.reshape(2 * depth, 3, pairs, 2 * nz).transpose(2, 0, 1, 3)
    fh, fl = np_parts(forward.reshape(pairs, 2 * depth, 6 * nz))
    az = jnp.asarray(np.concatenate([fh, fl, fh], axis=-1))
    bh, bl = (jnp.asarray(t) for t in np_parts(np.concatenate([cz, sz], axis=0)))
    kz = jnp.asarray(kz_np.astype(np.float32)[:, None])

    up = [(i, (i + 1) % slabs) for i in range(slabs)]
    down = [((i + 1) % slabs, i) for i in range(slabs)]
    twins = [(i, i ^ 1) for i in range(groups)]

    def send(x, axis, to):
        return lax.ppermute(x, axis, to)

    def exchange(first, last):
        return send(last, "gx", up), send(first, "gx", down)

    m = nx * nz
    y_flops = 2 * m * ny * ny * 3
    half_bytes = 4 * m * ny
    comp = lambda c: pl.BlockSpec((1, nx, nz, ny), lambda p: (c, 0, 0, 0))

    def fields(kind, c, e, halos=(), us=()):
        moves, stays = kind != "still", kind != "moving"
        count = 2 * (moves + stays)
        n_out = 2 * stays + moves
        block = lambda f: pl.BlockSpec((1, f, nx, nz, cw), lambda p: (p, 0, 0, 0, 0))
        tables = pl.BlockSpec((1, pairs, ny, 2 * cw), lambda p: (e, 0, 0, 0))
        args, specs = [ids, vel], [SMEM, comp(c)]
        if stays:
            args.append(vel)
            specs.append(comp(2))
        if moves:
            args += [vel, vel, halos[0][0], halos[c][0], halos[0][1], halos[c][1]]
            specs += [comp(0), comp(1)] + [whole((3, nz, ny))] * 4
        args += [wh, wl, *us]
        specs += [tables] * 2 + [block(1)] * len(us)
        return call(
            functools.partial(y_fields, c=c, e=e, kind=kind, slabs=slabs, chunks=chunks),
            count * y_flops // chunks,
            count * half_bytes,
            grid=(pairs,),
            in_specs=specs,
            out_specs=[block(n_out)] * 2,
            out_shape=[shaped(pairs, n_out, nx, nz, cw)] * 2,
            scratch_shapes=[pltpu.VMEM((count * m, ny), BF16)] * 2
            + ([pltpu.VMEM((2, 6, nz, ny), F32)] if moves else []),
        )(*args)

    zb = 2 if nx % 2 == 0 else 1
    plane = (depth, cw)

    def z_part(arrays, layout):
        outs = call(
            functools.partial(z_partial, layout=layout),
            2 * az.size * nx * cw,
            10 * half_bytes // groups,
            grid=(nx // zb,),
            in_specs=[SMEM]
            + [
                pl.BlockSpec((pairs, v.shape[1], zb, nz, cw), lambda x: (0, 0, x, 0, 0))
                for v in arrays
            ]
            + [whole(az.shape)],
            out_specs=[pl.BlockSpec((zb,) + plane, lambda x: (x, 0, 0))] * pairs,
            out_shape=[shaped(nx, *plane)] * pairs,
        )(ids, *arrays, az)
        pieces = [outs[0]]
        for s in range(1, pairs):
            to = [(i, int(across(i // 2, s, pairs)) * 2 + i % 2) for i in range(groups)]
            pieces.append(send(outs[s], "yz", to))
        return pieces

    halos = [exchange(vel[0, :3], vel[0, nx - 3 :])]
    tend = [[None] * 3 for _ in range(chunks)]
    us_send, us_keep = fields("still", 0, 0)
    later, us_send, us_keep = lax.optimization_barrier((vel, us_send, us_keep))
    for d in (1, 2):
        halos.append(exchange(later[d, :3], later[d, nx - 3 :]))
    w_send, w_keep = fields("moving", 0, 0, halos, (us_send, us_keep))
    arrays = (us_keep, send(us_send, "yz", twins), w_keep, send(w_send, "yz", twins))
    tend[0][0] = z_part(arrays, ((1, 0), (0, 1), (0, 0)))
    late = ids
    guess = pressure_guess
    for e in range(chunks):
        for c in range(3):
            if (c, e) == (0, 0):
                continue
            sent, kept = fields("full", c, e, halos)
            if (c, e) == (1, chunks - 1):
                late, guess, sent, kept = lax.optimization_barrier((late, guess, sent, kept))
            arrays = (kept, send(sent, "yz", twins))
            tend[e][c] = z_part(arrays, ((0, 2), (0, 1), (0, 0)))
    p_low, p_high = exchange(guess[:1], guess[nx - 1 :])

    offset, slab_id, group_id = late[0], late[1], late[2]
    is_low = slab_id == 0
    is_high = slab_id == slabs - 1
    lane = jnp.arange(cw, dtype=jnp.int32)
    sign = jnp.where(lane < half, -1.0, 1.0)
    kys, cks, rdens, rots = [], [], [], []
    for e in range(chunks):
        own = group_id * block_len + e * half + lane % half
        ky = (2.0 * math.pi / ny * own.astype(F32)).reshape(1, cw)
        edge = (
            2.0 * math.pi / ny
            * ((own * offset % ny).astype(F32) + fraction * own.astype(F32))
        )
        cos_e, sin_e = jnp.cos(edge), jnp.sin(edge) * sign
        kys.append(ky)
        cks.append(jnp.where(own == 0, 1.0, 2.0).astype(F32).reshape(1, cw))
        rdens.append(1.0 / (2.0 + ky * ky + kz * kz))
        rots.append(
            jnp.stack(
                [
                    jnp.where(is_low, cos_e, 1.0),
                    jnp.where(is_low, sin_e, 0.0),
                    jnp.where(is_high, cos_e, 1.0),
                    jnp.where(is_high, -sin_e, 0.0),
                ]
            ).astype(F32)
        )

    fb = 2 if nx % 2 == 0 else 1
    one = pl.BlockSpec((fb,) + plane, lambda x: (x, 0, 0))
    three = pl.BlockSpec((3, fb) + plane, lambda x: (0, x, 0, 0))
    packed = (depth, cols)
    q_done = []
    edges = []
    for e in range(chunks):
        edge_of = lambda x: functools.reduce(jnp.add, [piece[x] for piece in tend[e][0]])
        edges.append(exchange(edge_of(0), edge_of(nx - 1)))
    back = []
    for e in range(chunks):
        flat = [piece for c in range(3) for piece in tend[e][c]]
        t_low, t_high = edges[e]
        div, p1, lo, hi = call(
            functools.partial(first_sweep, e=e, chunks=chunks, pieces=pairs),
            2000 * nx * depth * cw,
            2 * half_bytes,
            out_shape=[shaped(nx, *plane)] * 2 + [shaped(2, *plane)] * 2,
        )(*flat, pressure_guess, t_low, t_high, p_low, p_high, rots[e], kys[e], kz, rdens[e])
        lo_halo, hi_halo = exchange(lo, hi)
        last = e == chunks - 1
        earlier = chunks > 1 and last
        out_plane = packed if last else plane
        consts = (p1, div, lo_halo, hi_halo, rots[e], kys[e], kz, rdens[e], cks[e])
        outs = call(
            functools.partial(finish, e=e, chunks=chunks, pieces=pairs, groups=groups),
            2 * 3 * 3 * nx * 2 * depth * depth * cw,
            3 * half_bytes,
            grid=(nx // fb,),
            in_specs=[SMEM]
            + [whole(v.shape) for v in consts]
            + [one] * len(flat)
            + [pl.BlockSpec((3, fb) + packed, lambda x: (0, x, 0, 0)), whole(bh.shape), whole(bl.shape)]
            + ([three, one] if earlier else []),
            out_specs=[
                pl.BlockSpec((3, fb) + out_plane, lambda x: (0, x, 0, 0)),
                pl.BlockSpec((fb,) + out_plane, lambda x: (x, 0, 0)),
            ]
            + [pl.BlockSpec((3, fb, nz, cw), lambda x: (0, x, 0, 0))] * groups,
            out_shape=[shaped(3, nx, *out_plane), shaped(nx, *out_plane)]
            + [shaped(3, nx, nz, cw)] * groups,
            scratch_shapes=[pltpu.VMEM((nx + 2,) + plane, F32), pltpu.VMEM((3,) + plane, F32)],
        )(ids, *consts, *flat, q_old, bh, bl, *q_done)
        q_done = list(outs[:2])
        got = [outs[2]]
        for place in range(1, groups):
            to = [(i, int(partner(i, place, groups))) for i in range(groups)]
            got.append(send(outs[2 + place], "yz", to))
        back.append(got)

    vb = 3 if nx % 3 == 0 else 1
    vel_block = pl.BlockSpec((1, vb, nz, ny), lambda c, x: (c, x, 0, 0))
    batches = [[(e, place) for place in range(groups)] for e in range(chunks - 1)]
    batches += [[(chunks - 1, place) for place in range(2)]]
    batches += [[(chunks - 1, place) for place in range(2, groups)]]
    vel_next = vel
    for terms in batches:
        vel_next = call(
            functools.partial(y_inverse, terms=terms, groups=groups),
            3 * y_flops * len(terms) // (chunks * groups),
            6 * half_bytes,
            grid=(3, nx // vb),
            in_specs=[SMEM]
            + [pl.BlockSpec((1, vb, nz, cw), lambda c, x: (c, x, 0, 0))] * len(terms)
            + [vel_block, whole(wh.shape), whole(wl.shape)],
            out_specs=vel_block,
            out_shape=jax.ShapeDtypeStruct(vel.shape, F32),
            scratch_shapes=[pltpu.VMEM((ny, len(terms) * cw), BF16)] * 2,
        )(ids, *[back[e][place] for e, place in terms], vel_next, wh, wl)
    return (vel_next, q_done[0], q_done[1])


def solution(mesh):
    placed = (P(None, "gx", "yz", None), P(None, "gx", None, "yz"), P("gx", None, "yz"), P())
    return jax.shard_map(
        section,
        mesh=mesh,
        in_specs=placed,
        out_specs=(P(None, "gx", "yz", None), P(None, "gx", None, "yz"), P("gx", None, "yz")),
        check_vma=False,
    )
```

time: 390 us -> 382 us (0.979)
  starting transfers between devices: 85.8 us -> 66.5 us
  Pallas kernels: 154 us -> 165 us
  local copies, waits for them, and re-layouts: 18.6 us -> 12.4 us
    ppermute x40 -> x35, starting transfers between devices: 85.8 us -> 66.5 us  [send(): return lax.ppermute(x, axis, to)]
    pallas_call x17 -> x18, Pallas kernels: 144 us -> 156 us  [the longest x7 77.9 us: fields(): call(functools.partial(y_fields, c=c, e=e, kind=kind, slabs=slabs, chunks...]
    ppermute x40 -> x35, waiting for transfers between devices: 117 us -> 119 us  [send(): return lax.ppermute(x, axis, to)]
  transfers between devices with their start and end apart: 40 -> 35, of which waited for: 10 -> 8; matrix products, arithmetic and copies ran while one was open for 6% -> 4% of each run, Pallas kernels for 37% -> 41%
where the time goes in v1:
time: 382 us; the launch traced here: 377 us
  Pallas kernels  165 us (43%)
  waiting for transfers between devices  119 us (31%)
  starting transfers between devices  66.5 us (17%)
  local copies, waits for them, and re-layouts  12.4 us (3%)
  other arithmetic  10.8 us (3%)
    ppermute x35, waiting for transfers between devices, send(): return lax.ppermute(x, axis, to)  119 us
    pallas_call x7, Pallas kernels, fields(): call(functools.partial(y_fields, c=c, e=e, kind=kind, slabs=slabs, chunks...  77.9 us
    ppermute x35, starting transfers between devices, send(): return lax.ppermute(x, axis, to)  66.5 us
    pallas_call x6, Pallas kernels, z_part(): call(functools.partial(z_partial, layout=layout), 2 * az.size * nx * cw,...  29.9 us
    pallas_call x3, Pallas kernels, section(): call(functools.partial(y_inverse, terms=terms, groups=groups), 3 * y_flop...  29.5 us
    pallas_call x2, Pallas kernels, section(): call(functools.partial(finish, e=e, chunks=chunks, pieces=pairs, groups=g...  18.2 us
    pallas_call x2, Pallas kernels, section(): call(functools.partial(first_sweep, e=e, chunks=chunks, pieces=pairs), 20...  9.22 us
  transfers between devices with their start and end apart: 35, of which 8 were waited for; matrix products, arithmetic and copies ran while one was open for 4% of the time, Pallas kernels for 41%

profile of v1, /device:TPU:13, one launch (start us, length us, event | category | flops | bytes accessed | tf_op | source)
XLA Modules:
  0.0 376.6 jit_solution(14173322417115422057)
XLA Ops:
  0.6 2.2 slice_bitcast_fusion.4
  2.8 0.7 collective-permute-start.1
  3.5 1.1 collective-permute-start
  5.2 0.7 pad_add_fusion.ids_ref
  5.9 6.0 %shard_map.123 = (f32[2,2,6,48,128]{4,3,2,1,0:T(8,128)}, f32[2,2,6,48,128]{4,3,2,1,0:T(8,128)}) custom-call(s32[3]{0:T(128)} %pad_add_fusion.ids_ref, f32[3,6,48,1024]{3,2,1,0:T(8,128)} %refs_4_.4, f32[3,6,48,1024]{3,2,1,0:T(8,128)} %refs_4_.4, bf16[2,2,1024,256]{3,2,1,0:T(8,128)(2,1)} %constant.81.clone.refs_8_.refs_2_.refs_7_.refs_5_.refs_3_, ...), custom_call_target="tpu_custom_call" | custom-call | flops 1811939328 | bytes 2359296 | tf_op jit(solution)/shard_map/pallas_call | solution.py:474
  11.8 3.1 slice_bitcast_fusion
  14.9 1.7 collective-permute-start.4
  16.8 1.0 collective-permute-start.9
  17.8 2.3 collective-permute-start.8
  20.2 9.1 %shard_map.129 = (f32[2,1,6,48,128]{4,3,2,1,0:T(8,128)}, f32[2,1,6,48,128]{4,3,2,1,0:T(8,128)}) custom-call(s32[3]{0:T(128)} %pad_add_fusion.ids_ref, f32[3,6,48,1024]{3,2,1,0:T(8,128)} %refs_4_.4, f32[3,6,48,1024]{3,2,1,0:T(8,128)} %refs_4_.4, f32[3,6,48,1024]{3,2,1,0:T(8,128)} %refs_4_.4, f32[3,48,1024]{2,1,0:T(8,128)} %copy-done.1, ...), custom_call_target="tpu_custom_call" | custom-call | flops 1811939328 | bytes 2359296 | tf_op jit(solution)/shard_map/pallas_call | solution.py:474
  29.2 12.0 %shard_map.121 = (f32[2,3,6,48,128]{4,3,2,1,0:T(8,128)}, f32[2,3,6,48,128]{4,3,2,1,0:T(8,128)}) custom-call(s32[3]{0:T(128)} %pad_add_fusion.ids_ref, f32[3,6,48,1024]{3,2,1,0:T(8,128)} %refs_4_.4, f32[3,6,48,1024]{3,2,1,0:T(8,128)} %refs_4_.4, f32[3,6,48,1024]{3,2,1,0:T(8,128)} %refs_4_.4, f32[3,6,48,1024]{3,2,1,0:T(8,128)} %refs_4_.4, ...), custom_call_target="tpu_custom_call" | custom-call | flops 3623878656 | bytes 4718592 | tf_op jit(solution)/shard_map/pallas_call | solution.py:474
  41.5 1.3 collective-permute-start.2
  42.8 12.9 %shard_map.124 = (f32[2,3,6,48,128]{4,3,2,1,0:T(8,128)}, f32[2,3,6,48,128]{4,3,2,1,0:T(8,128)}) custom-call(s32[3]{0:T(128)} %pad_add_fusion.ids_ref, f32[3,6,48,1024]{3,2,1,0:T(8,128)} %refs_4_.4, f32[3,6,48,1024]{3,2,1,0:T(8,128)} %refs_4_.4, f32[3,6,48,1024]{3,2,1,0:T(8,128)} %refs_4_.4, f32[3,6,48,1024]{3,2,1,0:T(8,128)} %refs_4_.4, ...), custom_call_target="tpu_custom_call" | custom-call | flops 3623878656 | bytes 4718592 | tf_op jit(solution)/shard_map/pallas_call | solution.py:474
  58.2 12.7 %shard_map.131 = (f32[2,3,6,48,128]{4,3,2,1,0:T(8,128)}, f32[2,3,6,48,128]{4,3,2,1,0:T(8,128)}) custom-call(s32[3]{0:T(128)} %pad_add_fusion.ids_ref, f32[3,6,48,1024]{3,2,1,0:T(8,128)} %refs_4_.4, f32[3,6,48,1024]{3,2,1,0:T(8,128)} %refs_4_.4, f32[3,6,48,1024]{3,2,1,0:T(8,128)} %refs_4_.4, f32[3,6,48,1024]{3,2,1,0:T(8,128)} %refs_4_.4, ...), custom_call_target="tpu_custom_call" | custom-call | flops 3623878656 | bytes 4718592 | tf_op jit(solution)/shard_map/pallas_call | solution.py:474
  71.8 12.6 %shard_map.133 = (f32[2,3,6,48,128]{4,3,2,1,0:T(8,128)}, f32[2,3,6,48,128]{4,3,2,1,0:T(8,128)}) custom-call(s32[3]{0:T(128)} %pad_add_fusion.ids_ref, f32[3,6,48,1024]{3,2,1,0:T(8,128)} %refs_4_.4, f32[3,6,48,1024]{3,2,1,0:T(8,128)} %refs_4_.4, f32[3,6,48,1024]{3,2,1,0:T(8,128)} %refs_4_.4, f32[3,6,48,1024]{3,2,1,0:T(8,128)} %refs_4_.4, ...), custom_call_target="tpu_custom_call" | custom-call | flops 3623878656 | bytes 4718592 | tf_op jit(solution)/shard_map/pallas_call | solution.py:474
  84.4 0.9 collective-permute-start.23
  85.3 0.8 add_divide_fusion
  86.1 0.7 broadcast_select_fusion.6
  86.8 0.7 broadcast_select_fusion.4
  87.6 0.7 broadcast_select_fusion.2
  88.9 0.7 broadcast_select_fusion
  89.6 12.6 %shard_map.126 = (f32[2,3,6,48,128]{4,3,2,1,0:T(8,128)}, f32[2,3,6,48,128]{4,3,2,1,0:T(8,128)}) custom-call(s32[3]{0:T(128)} %pad_add_fusion.ids_ref, f32[3,6,48,1024]{3,2,1,0:T(8,128)} %refs_4_.4, f32[3,6,48,1024]{3,2,1,0:T(8,128)} %refs_4_.4, f32[3,6,48,1024]{3,2,1,0:T(8,128)} %refs_4_.4, f32[3,6,48,1024]{3,2,1,0:T(8,128)} %refs_4_.4, ...), custom_call_target="tpu_custom_call" | custom-call | flops 3623878656 | bytes 4718592 | tf_op jit(solution)/shard_map/pallas_call | solution.py:474
  102.9 0.9 collective-permute-start.10
  103.8 5.2 %shard_map.130 = (f32[6,192,128]{2,1,0:T(8,128)}, f32[6,192,128]{2,1,0:T(8,128)}) custom-call(s32[3]{0:T(128)} %pad_add_fusion.ids_ref, f32[2,2,6,48,128]{4,3,2,1,0:T(8,128)} %get-tuple-element.79.refs_10_.refs_0_, f32[2,2,6,48,128]{4,3,2,1,0:T(8,128)} %collective-permute-done.18.refs_1_, f32[2,1,6,48,128]{4,3,2,1,0:T(8,128)} %get-tuple-element.81.refs_2_, ...), custom_call_target="tpu_custom_call" | custom-call | flops 1019215872 | bytes 2949120 | tf_op jit(solution)/shard_map/pallas_call | solution.py:490
  109.0 0.9 copy-done.20
  109.9 2.3 collective-permute-start.20
  112.7 1.0 fusion.15
  113.8 3.3 collective-permute-start.15
  117.1 5.0 %shard_map.122 = (f32[6,192,128]{2,1,0:T(8,128)}, f32[6,192,128]{2,1,0:T(8,128)}) custom-call(s32[3]{0:T(128)} %pad_add_fusion.ids_ref, f32[2,3,6,48,128]{4,3,2,1,0:T(8,128)} %get-tuple-element.56.refs_0_, f32[2,3,6,48,128]{4,3,2,1,0:T(8,128)} %copy-done.20, bf16[2,384,864]{2,1,0:T(8,128)(2,1)} %constant.83.clone.refs_2_.refs_4_), custom_call_target="tpu_custom_call" | custom-call | flops 1019215872 | bytes 2949120 | tf_op jit(solution)/shard_map/pallas_call | solution.py:490
  122.1 5.0 %shard_map.132 = (f32[6,192,128]{2,1,0:T(8,128)}, f32[6,192,128]{2,1,0:T(8,128)}) custom-call(s32[3]{0:T(128)} %pad_add_fusion.ids_ref, f32[2,3,6,48,128]{4,3,2,1,0:T(8,128)} %get-tuple-element.85.refs_0_, f32[2,3,6,48,128]{4,3,2,1,0:T(8,128)} %collective-permute-done.21.refs_1_, bf16[2,384,864]{2,1,0:T(8,128)(2,1)} %constant.83.clone.refs_2_.refs_4_), custom_call_target="tpu_custom_call" | custom-call | flops 1019215872 | bytes 2949120 | tf_op jit(solution)/shard_map/pallas_call | solution.py:490
  127.0 5.0 %shard_map.134 = (f32[6,192,128]{2,1,0:T(8,128)}, f32[6,192,128]{2,1,0:T(8,128)}) custom-call(s32[3]{0:T(128)} %pad_add_fusion.ids_ref, f32[2,3,6,48,128]{4,3,2,1,0:T(8,128)} %get-tuple-element.89.refs_0_, f32[2,3,6,48,128]{4,3,2,1,0:T(8,128)} %collective-permute-done.23.refs_1_, bf16[2,384,864]{2,1,0:T(8,128)(2,1)} %constant.83.clone.refs_2_.refs_4_), custom_call_target="tpu_custom_call" | custom-call | flops 1019215872 | bytes 2949120 | tf_op jit(solution)/shard_map/pallas_call | solution.py:490
  132.1 2.3 collective-permute-start.22
  134.4 26.1 %collective-permute-done.20.refs_1_.refs_10_ = f32[6,192,128]{2,1,0:T(8,128)S(1)} collective-permute-done((f32[6,192,128]{2,1,0:T(8,128)}, f32[6,192,128]{2,1,0:T(8,128)S(1)}, u32[]{:S(2)}, u32[]{:S(2)}) %collective-permute-start.20) | collective-permute-done | bytes 589856 | tf_op jit(solution)/shard_map/ppermute | solution.py:449
  160.5 1.2 fusion
  161.7 6.5 %collective-permute-start.26 = (f32[192,128]{1,0:T(8,128)S(1)}, f32[192,128]{1,0:T(8,128)S(1)}, u32[]{:S(2)}, u32[]{:S(2)}) collective-permute-start(f32[192,128]{1,0:T(8,128)S(1)} %get-tuple-element.115), channel_id=1, source_target_pairs={{4,0},{8,4},{12,8},{16,12},{20,16},{24,20},{28,24},{0,28},{5,1},{9... | collective-permute-start | bytes 294920 | tf_op jit(solution)/shard_map/ppermute | solution.py:449
  168.2 4.7 %collective-permute-done.10.refs_1_ = f32[2,3,6,48,128]{4,3,2,1,0:T(8,128)} collective-permute-done((f32[2,3,6,48,128]{4,3,2,1,0:T(8,128)}, f32[2,3,6,48,128]{4,3,2,1,0:T(8,128)}, u32[]{:S(2)}, u32[]{:S(2)}) %collective-permute-start.10) | collective-permute-done | bytes 884768 | tf_op jit(solution)/shard_map/ppermute | solution.py:449
  172.9 6.5 %collective-permute-start.25 = (f32[192,128]{1,0:T(8,128)S(1)}, f32[192,128]{1,0:T(8,128)S(1)}, u32[]{:S(2)}, u32[]{:S(2)}) collective-permute-start(f32[192,128]{1,0:T(8,128)S(1)} %get-tuple-element.116), channel_id=1, source_target_pairs={{0,4},{4,8},{8,12},{12,16},{16,20},{20,24},{24,28},{28,0},{1,5},{5... | collective-permute-start | bytes 294920 | tf_op jit(solution)/shard_map/ppermute | solution.py:449
  179.4 4.9 %shard_map.125 = (f32[6,192,128]{2,1,0:T(8,128)}, f32[6,192,128]{2,1,0:T(8,128)}) custom-call(s32[3]{0:T(128)} %pad_add_fusion.ids_ref, f32[2,3,6,48,128]{4,3,2,1,0:T(8,128)} %get-tuple-element.65.refs_0_, f32[2,3,6,48,128]{4,3,2,1,0:T(8,128)} %collective-permute-done.6.refs_1_, bf16[2,384,864]{2,1,0:T(8,128)(2,1)} %constant.83.clone.refs_2_.refs_4_), custom_call_target="tpu_custom_call" | custom-call | flops 1019215872 | bytes 2949120 | tf_op jit(solution)/shard_map/pallas_call | solution.py:490
  184.3 4.9 %shard_map.127 = (f32[6,192,128]{2,1,0:T(8,128)}, f32[6,192,128]{2,1,0:T(8,128)}) custom-call(s32[3]{0:T(128)} %pad_add_fusion.ids_ref, f32[2,3,6,48,128]{4,3,2,1,0:T(8,128)} %get-tuple-element.69.refs_0_, f32[2,3,6,48,128]{4,3,2,1,0:T(8,128)} %collective-permute-done.10.refs_1_, bf16[2,384,864]{2,1,0:T(8,128)(2,1)} %constant.83.clone.refs_2_.refs_4_), custom_call_target="tpu_custom_call" | custom-call | flops 1019215872 | bytes 2949120 | tf_op jit(solution)/shard_map/pallas_call | solution.py:490
  189.3 2.7 collective-permute-start.7
  194.3 43.2 %collective-permute-done.24.refs_5_.refs_14_ = f32[6,192,128]{2,1,0:T(8,128)} collective-permute-done((f32[6,192,128]{2,1,0:T(8,128)}, f32[6,192,128]{2,1,0:T(8,128)}, u32[]{:S(2)}, u32[]{:S(2)}) %collective-permute-start.24) | collective-permute-done | bytes 589856 | tf_op jit(solution)/shard_map/ppermute | solution.py:449
  237.5 4.6 %shard_map.135 = (f32[6,192,128]{2,1,0:T(8,128)}, f32[6,192,128]{2,1,0:T(8,128)}, f32[2,192,128]{2,1,0:T(8,128)}, f32[2,192,128]{2,1,0:T(8,128)}) custom-call(f32[6,192,128]{2,1,0:T(8,128)} %get-tuple-element.83.refs_0_.refs_9_, f32[6,192,128]{2,1,0:T(8,128)} %copy-done.3, f32[6,192,128]{2,1,0:T(8,128)} %get-tuple-element.87.refs_2_.refs_11_, ...), custom_call_target="tpu_custom_call" | custom-call | flops 294912000 | bytes 2359296 | tf_op jit(solution)/shard_map/pallas_call | solution.py:573
  242.1 2.2 collective-permute-start.27
  244.3 17.3 %collective-permute-start.28 = (f32[2,192,128]{2,1,0:T(8,128)}, f32[2,192,128]{2,1,0:T(8,128)}, u32[]{:S(2)}, u32[]{:S(2)}) collective-permute-start(f32[2,192,128]{2,1,0:T(8,128)} %get-tuple-element.96), channel_id=1, source_target_pairs={{4,0},{8,4},{12,8},{16,12},{20,16},{24,20},{28,24},{0,28},{5,1},{9... | collective-permute-start | bytes 589832 | tf_op jit(solution)/shard_map/ppermute | solution.py:449
  261.6 1.8 fusion.2
  263.5 2.6 collective-permute-start.13
  266.7 1.6 collective-permute-done.28.refs_3_
  268.4 8.3 %shard_map.136 = (f32[3,6,192,128]{3,2,1,0:T(8,128)}, f32[6,192,128]{2,1,0:T(8,128)}, f32[3,6,48,128]{3,2,1,0:T(8,128)}, f32[3,6,48,128]{3,2,1,0:T(8,128)}, f32[...) custom-call(s32[3]{0:T(128)} %pad_add_fusion.ids_ref, f32[6,192,128]{2,1,0:T(8,128)} %get-tuple-element.93.refs_0_, ...), custom_call_target="tpu_custom_call" | custom-call | flops 1019215872 | bytes 3538944 | tf_op jit(solution)/shard_map/pallas_call | solution.py:584
  276.7 2.4 collective-permute-start.32
  279.2 0.8 copy-done.5
  280.2 4.6 %shard_map.128 = (f32[6,192,128]{2,1,0:T(8,128)}, f32[6,192,128]{2,1,0:T(8,128)}, f32[2,192,128]{2,1,0:T(8,128)}, f32[2,192,128]{2,1,0:T(8,128)}) custom-call(f32[6,192,128]{2,1,0:T(8,128)} %get-tuple-element.58.refs_0_.refs_9_, f32[6,192,128]{2,1,0:T(8,128)} %copy-done.2, f32[6,192,128]{2,1,0:T(8,128)} %get-tuple-element.67.refs_2_.refs_11_, ...), custom_call_target="tpu_custom_call" | custom-call | flops 294912000 | bytes 2359296 | tf_op jit(solution)/shard_map/pallas_call | solution.py:573
  284.8 2.7 collective-permute-start.16
  289.1 1.3 collective-permute-done.16.refs_2_
  290.4 5.7 %collective-permute-done.17.refs_3_ = f32[2,192,128]{2,1,0:T(8,128)S(1)} collective-permute-done((f32[2,192,128]{2,1,0:T(8,128)}, f32[2,192,128]{2,1,0:T(8,128)S(1)}, u32[]{:S(2)}, u32[]{:S(2)}) %collective-permute-start.17) | collective-permute-done | bytes 196640 | tf_op jit(solution)/shard_map/ppermute | solution.py:449
  296.1 0.7 copy-done.15
  296.7 9.9 %shard_map.137 = (f32[3,6,192,256]{3,2,1,0:T(8,128)}, f32[6,192,256]{2,1,0:T(8,128)}, f32[3,6,48,128]{3,2,1,0:T(8,128)}, f32[3,6,48,128]{3,2,1,0:T(8,128)}, f32[...) custom-call(s32[3]{0:T(128)} %pad_add_fusion.ids_ref, f32[6,192,128]{2,1,0:T(8,128)} %get-tuple-element.75.refs_0_, ...), custom_call_target="tpu_custom_call" | custom-call | flops 1019215872 | bytes 3538944 | tf_op jit(solution)/shard_map/pallas_call | solution.py:584
  306.7 2.2 collective-permute-start.29
  309.3 6.5 %collective-permute-done.33.refs_2_ = f32[3,6,48,128]{3,2,1,0:T(8,128)S(1)} collective-permute-done((f32[3,6,48,128]{3,2,1,0:T(8,128)}, f32[3,6,48,128]{3,2,1,0:T(8,128)S(1)}, u32[]{:S(2)}, u32[]{:S(2)}) %collective-permute-start.33) | collective-permute-done | bytes 442400 | tf_op jit(solution)/shard_map/ppermute | solution.py:449
  315.8 29.7 %collective-permute-done.34.refs_3_ = f32[3,6,48,128]{3,2,1,0:T(8,128)S(1)} collective-permute-done((f32[3,6,48,128]{3,2,1,0:T(8,128)}, f32[3,6,48,128]{3,2,1,0:T(8,128)S(1)}, u32[]{:S(2)}, u32[]{:S(2)}) %collective-permute-start.34) | collective-permute-done | bytes 442400 | tf_op jit(solution)/shard_map/ppermute | solution.py:449
  345.5 0.8 copy-done.11
  346.3 11.5 %shard_map.138.refs_2_ = f32[3,6,48,1024]{3,2,1,0:T(8,128)} custom-call(s32[3]{0:T(128)} %pad_add_fusion.ids_ref, f32[3,6,48,128]{3,2,1,0:T(8,128)} %get-tuple-element.103.refs_0_, f32[3,6,48,128]{3,2,1,0:T(8,128)} %copy-done.9, f32[3,6,48,128]{3,2,1,0:T(8,128)} %copy-done.10, f32[3,6,48,128]{3,2,1,0:T(8,128)} %copy-done.11, f32[3,6,48,1024]{3,2,1,0:T(8,128)} %refs_4_.4, ...), custom_call_target="tpu_custom_call" | custom-call | flops 2717908992 | bytes 7077888 | tf_op jit(solution)/shard_map/pallas_call | solution.py:617
  357.8 9.1 %shard_map.139.refs_2_ = f32[3,6,48,1024]{3,2,1,0:T(8,128)} custom-call(s32[3]{0:T(128)} %pad_add_fusion.ids_ref, f32[3,6,48,128]{3,2,1,0:T(8,128)} %get-tuple-element.101.refs_0_, f32[3,6,48,128]{3,2,1,0:T(8,128)} %collective-permute-done.31.refs_1_, f32[3,6,48,1024]{3,2,1,0:T(8,128)} %shard_map.138.refs_2_, ...), custom_call_target="tpu_custom_call" | custom-call | flops 1358954496 | bytes 7077888 | tf_op jit(solution)/shard_map/pallas_call | solution.py:617
  366.9 0.7 copy-done.12
  367.6 9.0 %shard_map.140 = f32[3,6,48,1024]{3,2,1,0:T(8,128)} custom-call(s32[3]{0:T(128)} %pad_add_fusion.ids_ref, f32[3,6,48,128]{3,2,1,0:T(8,128)} %copy-done.12, f32[3,6,48,128]{3,2,1,0:T(8,128)} %collective-permute-done.30.refs_1_, f32[3,6,48,1024]{3,2,1,0:T(8,128)} %shard_map.139.refs_2_, ...), custom_call_target="tpu_custom_call" | custom-call | flops 1358954496 | bytes 7077888 | tf_op jit(solution)/shard_map/pallas_call | solution.py:617
  (89 shorter events, 9.3 us)
Async XLA Ops:
  2.8 14.0 %collective-permute-start.1 = (f32[3,48,1024]{2,1,0:T(8,128)S(1)}, f32[3,48,1024]{2,1,0:T(8,128)S(1)}, u32[]{:S(2)}, u32[]{:S(2)}) collective-permute-start(f32[3,48,1024]{2,1,0:T(8,128)S(1)} %get-tuple-element.113), channel_id=1, source_target_pairs={{4,0},{8,4},{12,8},{16,12},{20,16},{24,20},{28,24},{0,28},{5,1},{9... | collective-permute-start | bytes 1769480 | tf_op jit(solution)/shard_map/ppermute | solution.py:449
  3.5 14.3 %collective-permute-start = (f32[3,48,1024]{2,1,0:T(8,128)}, f32[3,48,1024]{2,1,0:T(8,128)S(1)}, u32[]{:S(2)}, u32[]{:S(2)}) collective-permute-start(f32[3,48,1024]{2,1,0:T(8,128)} %get-tuple-element.114), channel_id=1, source_target_pairs={{0,4},{4,8},{8,12},{12,16},{16,20},{20,24},{24,28},{28,0},{1,5},{5... | collective-permute-start | bytes 1769480 | tf_op jit(solution)/shard_map/ppermute | solution.py:449
  14.9 26.3 %collective-permute-start.5 = (f32[3,48,1024]{2,1,0:T(8,128)}, f32[3,48,1024]{2,1,0:T(8,128)}, u32[]{:S(2)}, u32[]{:S(2)}) collective-permute-start(f32[3,48,1024]{2,1,0:T(8,128)} %get-tuple-element.111), channel_id=1, source_target_pairs={{4,0},{8,4},{12,8},{16,12},{20,16},{24,20},{28,24},{0,28},{5,1},{9... | collective-permute-start | bytes 1769480 | tf_op jit(solution)/shard_map/ppermute | solution.py:449
  14.9 26.6 %collective-permute-start.4 = (f32[3,48,1024]{2,1,0:T(8,128)}, f32[3,48,1024]{2,1,0:T(8,128)}, u32[]{:S(2)}, u32[]{:S(2)}) collective-permute-start(f32[3,48,1024]{2,1,0:T(8,128)} %get-tuple-element.112), channel_id=1, source_target_pairs={{0,4},{4,8},{8,12},{12,16},{16,20},{20,24},{24,28},{28,0},{1,5},{5... | collective-permute-start | bytes 1769480 | tf_op jit(solution)/shard_map/ppermute | solution.py:449
  16.6 85.6 %collective-permute-start.18 = (f32[2,2,6,48,128]{4,3,2,1,0:T(8,128)}, f32[2,2,6,48,128]{4,3,2,1,0:T(8,128)}, u32[]{:S(2)}, u32[]{:S(2)}) collective-permute-start(f32[2,2,6,48,128]{4,3,2,1,0:T(8,128)} %get-tuple-element.80.refs_9_), channel_id=1, source_target_pairs={{0,1},{1,0},{2,3},{3,2},{4,5},{5,4},{6,7},{7,6},{8,9},{9,8},{10,11... | collective-permute-start | bytes 1769480 | tf_op jit(solution)/shard_map/ppermute | solution.py:449
  16.8 3.3 copy-start
  16.8 54.1 %collective-permute-start.9 = (f32[3,48,1024]{2,1,0:T(8,128)}, f32[3,48,1024]{2,1,0:T(8,128)S(1)}, u32[]{:S(2)}, u32[]{:S(2)}) collective-permute-start(f32[3,48,1024]{2,1,0:T(8,128)} %get-tuple-element.109), channel_id=1, source_target_pairs={{4,0},{8,4},{12,8},{16,12},{20,16},{24,20},{28,24},{0,28},{5,1},{9... | collective-permute-start | bytes 1769480 | tf_op jit(solution)/shard_map/ppermute | solution.py:449
  17.8 2.3 copy-start.1
  17.8 53.4 %collective-permute-start.8 = (f32[3,48,1024]{2,1,0:T(8,128)}, f32[3,48,1024]{2,1,0:T(8,128)}, u32[]{:S(2)}, u32[]{:S(2)}) collective-permute-start(f32[3,48,1024]{2,1,0:T(8,128)} %get-tuple-element.110), channel_id=1, source_target_pairs={{0,4},{4,8},{8,12},{12,16},{16,20},{20,24},{24,28},{28,0},{1,5},{5... | collective-permute-start | bytes 1769480 | tf_op jit(solution)/shard_map/ppermute | solution.py:449
  41.2 61.6 %collective-permute-start.19 = (f32[2,1,6,48,128]{4,3,2,1,0:T(8,128)}, f32[2,1,6,48,128]{4,3,2,1,0:T(8,128)S(1)}, u32[]{:S(2)}, u32[]{:S(2)}) collective-permute-start(f32[2,1,6,48,128]{4,3,2,1,0:T(8,128)} %get-tuple-element.82), channel_id=1, source_target_pairs={{0,1},{1,0},{2,3},{3,2},{4,5},{5,4},{6,7},{7,6},{8,9},{9,8},{10,11... | collective-permute-start | bytes 884744 | tf_op jit(solution)/shard_map/ppermute | solution.py:449
  41.5 14.2 %copy-start.16 = (s32[3]{0:T(128)S(1)}, s32[3]{0:T(128)}, u32[]{:S(2)}) copy-start(s32[3]{0:T(128)} %pad_add_fusion.ids_ref) | copy-start | bytes 40
  41.5 67.5 %collective-permute-start.2 = (f32[2,3,6,48,128]{4,3,2,1,0:T(8,128)}, f32[2,3,6,48,128]{4,3,2,1,0:T(8,128)S(1)}, u32[]{:S(2)}, u32[]{:S(2)}) collective-permute-start(f32[2,3,6,48,128]{4,3,2,1,0:T(8,128)} %get-tuple-element.57), channel_id=1, source_target_pairs={{0,1},{1,0},{2,3},{3,2},{4,5},{5,4},{6,7},{7,6},{8,9},{9,8},{10,11... | collective-permute-start | bytes 2654216 | tf_op jit(solution)/shard_map/ppermute | solution.py:449
  71.0 0.9 copy-start.4
  71.0 14.4 %copy-start.19 = (f32[192]{0:T(256)S(1)}, f32[192]{0:T(256)}, u32[]{:S(2)}) copy-start(f32[192]{0:T(256)} %constant.91) | copy-start | bytes 2308
  71.0 42.8 %collective-permute-start.21 = (f32[2,3,6,48,128]{4,3,2,1,0:T(8,128)}, f32[2,3,6,48,128]{4,3,2,1,0:T(8,128)}, u32[]{:S(2)}, u32[]{:S(2)}) collective-permute-start(f32[2,3,6,48,128]{4,3,2,1,0:T(8,128)} %get-tuple-element.86), channel_id=1, source_target_pairs={{0,1},{1,0},{2,3},{3,2},{4,5},{5,4},{6,7},{7,6},{8,9},{9,8},{10,11... | collective-permute-start | bytes 2654216 | tf_op jit(solution)/shard_map/ppermute | solution.py:449
  84.4 32.7 %collective-permute-start.23 = (f32[2,3,6,48,128]{4,3,2,1,0:T(8,128)}, f32[2,3,6,48,128]{4,3,2,1,0:T(8,128)}, u32[]{:S(2)}, u32[]{:S(2)}) collective-permute-start(f32[2,3,6,48,128]{4,3,2,1,0:T(8,128)} %get-tuple-element.90), channel_id=1, source_target_pairs={{0,1},{1,0},{2,3},{3,2},{4,5},{5,4},{6,7},{7,6},{8,9},{9,8},{10,11... | collective-permute-start | bytes 2654216 | tf_op jit(solution)/shard_map/ppermute | solution.py:449
  102.2 59.5 %collective-permute-start.6 = (f32[2,3,6,48,128]{4,3,2,1,0:T(8,128)}, f32[2,3,6,48,128]{4,3,2,1,0:T(8,128)}, u32[]{:S(2)}, u32[]{:S(2)}) collective-permute-start(f32[2,3,6,48,128]{4,3,2,1,0:T(8,128)} %get-tuple-element.66), channel_id=1, source_target_pairs={{0,1},{1,0},{2,3},{3,2},{4,5},{5,4},{6,7},{7,6},{8,9},{9,8},{10,11... | collective-permute-start | bytes 2654216 | tf_op jit(solution)/shard_map/ppermute | solution.py:449
  102.9 0.9 copy-start.21
  102.9 70.0 %collective-permute-start.10 = (f32[2,3,6,48,128]{4,3,2,1,0:T(8,128)}, f32[2,3,6,48,128]{4,3,2,1,0:T(8,128)}, u32[]{:S(2)}, u32[]{:S(2)}) collective-permute-start(f32[2,3,6,48,128]{4,3,2,1,0:T(8,128)} %get-tuple-element.70), channel_id=1, source_target_pairs={{0,1},{1,0},{2,3},{3,2},{4,5},{5,4},{6,7},{7,6},{8,9},{9,8},{10,11... | collective-permute-start | bytes 2654216 | tf_op jit(solution)/shard_map/ppermute | solution.py:449
  109.0 0.9 copy-start.20
  109.9 50.6 %collective-permute-start.20 = (f32[6,192,128]{2,1,0:T(8,128)}, f32[6,192,128]{2,1,0:T(8,128)S(1)}, u32[]{:S(2)}, u32[]{:S(2)}) collective-permute-start(f32[6,192,128]{2,1,0:T(8,128)} %get-tuple-element.84), channel_id=1, source_target_pairs={{0,2},{1,3},{2,0},{3,1},{4,6},{5,7},{6,4},{7,5},{8,10},{9,11},{10,... | collective-permute-start | bytes 1769480 | tf_op jit(solution)/shard_map/ppermute | solution.py:449
  113.8 18.2 %collective-permute-start.15 = (f32[1,192,256]{2,1,0:T(8,128)S(1)}, f32[1,192,256]{2,1,0:T(8,128)S(1)}, u32[]{:S(2)}, u32[]{:S(2)}) collective-permute-start(f32[1,192,256]{2,1,0:T(8,128)S(1)} %get-tuple-element.117), channel_id=1, source_target_pairs={{4,0},{8,4},{12,8},{16,12},{20,16},{24,20},{28,24},{0,28},{5,1},{9... | collective-permute-start | bytes 589832 | tf_op jit(solution)/shard_map/ppermute | solution.py:449
  117.1 15.0 %collective-permute-start.14 = (f32[1,192,256]{2,1,0:T(8,128)S(1)}, f32[1,192,256]{2,1,0:T(8,128)S(1)}, u32[]{:S(2)}, u32[]{:S(2)}) collective-permute-start(f32[1,192,256]{2,1,0:T(8,128)S(1)} %get-tuple-element.118), channel_id=1, source_target_pairs={{0,4},{4,8},{8,12},{12,16},{16,20},{20,24},{24,28},{28,0},{1,5},{5... | collective-permute-start | bytes 589832 | tf_op jit(solution)/shard_map/ppermute | solution.py:449
  132.0 57.2 %copy-start.7 = (f32[1,192,256]{2,1,0:T(8,128)}, f32[1,192,256]{2,1,0:T(8,128)S(1)}, u32[]{:S(2)}) copy-start(f32[1,192,256]{2,1,0:T(8,128)S(1)} %collective-permute-done.15.refs_10_) | copy-start | bytes 589828
  132.0 129.6 %collective-permute-start.3 = (f32[6,192,128]{2,1,0:T(8,128)}, f32[6,192,128]{2,1,0:T(8,128)S(1)}, u32[]{:S(2)}, u32[]{:S(2)}) collective-permute-start(f32[6,192,128]{2,1,0:T(8,128)} %get-tuple-element.59), channel_id=1, source_target_pairs={{0,2},{1,3},{2,0},{3,1},{4,6},{5,7},{6,4},{7,5},{8,10},{9,11},{10,... | collective-permute-start | bytes 1769480 | tf_op jit(solution)/shard_map/ppermute | solution.py:449
  132.1 57.1 %copy-start.8 = (f32[1,192,256]{2,1,0:T(8,128)}, f32[1,192,256]{2,1,0:T(8,128)S(1)}, u32[]{:S(2)}) copy-start(f32[1,192,256]{2,1,0:T(8,128)S(1)} %collective-permute-done.14.refs_9_) | copy-start | bytes 589828
  132.1 62.2 %collective-permute-start.22 = (f32[6,192,128]{2,1,0:T(8,128)}, f32[6,192,128]{2,1,0:T(8,128)}, u32[]{:S(2)}, u32[]{:S(2)}) collective-permute-start(f32[6,192,128]{2,1,0:T(8,128)} %get-tuple-element.88), channel_id=1, source_target_pairs={{0,2},{1,3},{2,0},{3,1},{4,6},{5,7},{6,4},{7,5},{8,10},{9,11},{10,... | collective-permute-start | bytes 1769480 | tf_op jit(solution)/shard_map/ppermute | solution.py:449
  160.5 28.7 %copy-start.3 = (f32[6,192,128]{2,1,0:T(8,128)}, f32[6,192,128]{2,1,0:T(8,128)S(1)}, u32[]{:S(2)}) copy-start(f32[6,192,128]{2,1,0:T(8,128)S(1)} %collective-permute-done.20.refs_1_.refs_10_) | copy-start | bytes 1769476
  160.5 77.0 %collective-permute-start.24 = (f32[6,192,128]{2,1,0:T(8,128)}, f32[6,192,128]{2,1,0:T(8,128)}, u32[]{:S(2)}, u32[]{:S(2)}) collective-permute-start(f32[6,192,128]{2,1,0:T(8,128)} %get-tuple-element.92), channel_id=1, source_target_pairs={{0,2},{1,3},{2,0},{3,1},{4,6},{5,7},{6,4},{7,5},{8,10},{9,11},{10,... | collective-permute-start | bytes 1769480 | tf_op jit(solution)/shard_map/ppermute | solution.py:449
  161.7 27.5 %collective-permute-start.26 = (f32[192,128]{1,0:T(8,128)S(1)}, f32[192,128]{1,0:T(8,128)S(1)}, u32[]{:S(2)}, u32[]{:S(2)}) collective-permute-start(f32[192,128]{1,0:T(8,128)S(1)} %get-tuple-element.115), channel_id=1, source_target_pairs={{4,0},{8,4},{12,8},{16,12},{20,16},{24,20},{28,24},{0,28},{5,1},{9... | collective-permute-start | bytes 294920 | tf_op jit(solution)/shard_map/ppermute | solution.py:449
  172.9 19.1 %collective-permute-start.25 = (f32[192,128]{1,0:T(8,128)S(1)}, f32[192,128]{1,0:T(8,128)S(1)}, u32[]{:S(2)}, u32[]{:S(2)}) collective-permute-start(f32[192,128]{1,0:T(8,128)S(1)} %get-tuple-element.116), channel_id=1, source_target_pairs={{0,4},{4,8},{8,12},{12,16},{16,20},{20,24},{24,28},{28,0},{1,5},{5... | collective-permute-start | bytes 294920 | tf_op jit(solution)/shard_map/ppermute | solution.py:449
  189.3 2.7 copy-start.17
  189.3 89.9 %collective-permute-start.7 = (f32[6,192,128]{2,1,0:T(8,128)}, f32[6,192,128]{2,1,0:T(8,128)S(1)}, u32[]{:S(2)}, u32[]{:S(2)}) collective-permute-start(f32[6,192,128]{2,1,0:T(8,128)} %get-tuple-element.68), channel_id=1, source_target_pairs={{0,2},{1,3},{2,0},{3,1},{4,6},{5,7},{6,4},{7,5},{8,10},{9,11},{10,... | collective-permute-start | bytes 1769480 | tf_op jit(solution)/shard_map/ppermute | solution.py:449
  192.0 0.7 copy-start.18
  192.6 86.5 %collective-permute-start.11 = (f32[6,192,128]{2,1,0:T(8,128)}, f32[6,192,128]{2,1,0:T(8,128)S(1)}, u32[]{:S(2)}, u32[]{:S(2)}) collective-permute-start(f32[6,192,128]{2,1,0:T(8,128)} %get-tuple-element.72), channel_id=1, source_target_pairs={{0,2},{1,3},{2,0},{3,1},{4,6},{5,7},{6,4},{7,5},{8,10},{9,11},{10,... | collective-permute-start | bytes 1769480 | tf_op jit(solution)/shard_map/ppermute | solution.py:449
  242.1 24.0 %collective-permute-start.27 = (f32[2,192,128]{2,1,0:T(8,128)}, f32[2,192,128]{2,1,0:T(8,128)S(1)}, u32[]{:S(2)}, u32[]{:S(2)}) collective-permute-start(f32[2,192,128]{2,1,0:T(8,128)} %get-tuple-element.95), channel_id=1, source_target_pairs={{0,4},{4,8},{8,12},{12,16},{16,20},{20,24},{24,28},{28,0},{1,5},{5... | collective-permute-start | bytes 589832 | tf_op jit(solution)/shard_map/ppermute | solution.py:449
  244.3 24.0 %collective-permute-start.28 = (f32[2,192,128]{2,1,0:T(8,128)}, f32[2,192,128]{2,1,0:T(8,128)}, u32[]{:S(2)}, u32[]{:S(2)}) collective-permute-start(f32[2,192,128]{2,1,0:T(8,128)} %get-tuple-element.96), channel_id=1, source_target_pairs={{4,0},{8,4},{12,8},{16,12},{20,16},{24,20},{28,24},{0,28},{5,1},{9... | collective-permute-start | bytes 589832 | tf_op jit(solution)/shard_map/ppermute | solution.py:449
  261.6 15.0 %copy-start.2 = (f32[6,192,128]{2,1,0:T(8,128)}, f32[6,192,128]{2,1,0:T(8,128)S(1)}, u32[]{:S(2)}) copy-start(f32[6,192,128]{2,1,0:T(8,128)S(1)} %collective-permute-done.3.refs_1_.refs_10_) | copy-start | bytes 1769476
  263.5 15.7 %collective-permute-start.13 = (f32[192,128]{1,0:T(8,128)}, f32[192,128]{1,0:T(8,128)}, u32[]{:S(2)}, u32[]{:S(2)}) collective-permute-start(f32[192,128]{1,0:T(8,128)} %get-tuple-element.119), channel_id=1, source_target_pairs={{4,0},{8,4},{12,8},{16,12},{20,16},{24,20},{28,24},{0,28},{5,1},{9... | collective-permute-start | bytes 294920 | tf_op jit(solution)/shard_map/ppermute | solution.py:449
  266.1 2.3 copy-start.13
  266.1 13.1 %collective-permute-start.12 = (f32[192,128]{1,0:T(8,128)}, f32[192,128]{1,0:T(8,128)}, u32[]{:S(2)}, u32[]{:S(2)}) collective-permute-start(f32[192,128]{1,0:T(8,128)} %get-tuple-element.120), channel_id=1, source_target_pairs={{0,4},{4,8},{8,12},{12,16},{16,20},{20,24},{24,28},{28,0},{1,5},{5... | collective-permute-start | bytes 294920 | tf_op jit(solution)/shard_map/ppermute | solution.py:449
  276.7 32.2 %collective-permute-start.32 = (f32[3,6,48,128]{3,2,1,0:T(8,128)}, f32[3,6,48,128]{3,2,1,0:T(8,128)S(1)}, u32[]{:S(2)}, u32[]{:S(2)}) collective-permute-start(f32[3,6,48,128]{3,2,1,0:T(8,128)} %get-tuple-element.104), channel_id=1, source_target_pairs={{0,1},{1,0},{2,3},{3,2},{4,5},{5,4},{6,7},{7,6},{8,9},{9,8},{10,11... | collective-permute-start | bytes 1327112 | tf_op jit(solution)/shard_map/ppermute | solution.py:449
  279.1 0.8 copy-start.5
  279.1 1.0 copy-start.6
  284.8 5.6 %collective-permute-start.16 = (f32[2,192,128]{2,1,0:T(8,128)}, f32[2,192,128]{2,1,0:T(8,128)S(1)}, u32[]{:S(2)}, u32[]{:S(2)}) collective-permute-start(f32[2,192,128]{2,1,0:T(8,128)} %get-tuple-element.77), channel_id=1, source_target_pairs={{0,4},{4,8},{8,12},{12,16},{16,20},{20,24},{24,28},{28,0},{1,5},{5... | collective-permute-start | bytes 589832 | tf_op jit(solution)/shard_map/ppermute | solution.py:449
  287.4 8.6 %collective-permute-start.17 = (f32[2,192,128]{2,1,0:T(8,128)}, f32[2,192,128]{2,1,0:T(8,128)S(1)}, u32[]{:S(2)}, u32[]{:S(2)}) collective-permute-start(f32[2,192,128]{2,1,0:T(8,128)} %get-tuple-element.78), channel_id=1, source_target_pairs={{4,0},{8,4},{12,8},{16,12},{20,16},{24,20},{28,24},{0,28},{5,1},{9... | collective-permute-start | bytes 589832 | tf_op jit(solution)/shard_map/ppermute | solution.py:449
  287.4 28.3 %collective-permute-start.33 = (f32[3,6,48,128]{3,2,1,0:T(8,128)}, f32[3,6,48,128]{3,2,1,0:T(8,128)S(1)}, u32[]{:S(2)}, u32[]{:S(2)}) collective-permute-start(f32[3,6,48,128]{3,2,1,0:T(8,128)} %get-tuple-element.105), channel_id=1, source_target_pairs={{0,2},{1,3},{2,0},{3,1},{4,6},{5,7},{6,4},{7,5},{8,10},{9,11},{10,... | collective-permute-start | bytes 1327112 | tf_op jit(solution)/shard_map/ppermute | solution.py:449
  287.9 57.6 %collective-permute-start.34 = (f32[3,6,48,128]{3,2,1,0:T(8,128)}, f32[3,6,48,128]{3,2,1,0:T(8,128)S(1)}, u32[]{:S(2)}, u32[]{:S(2)}) collective-permute-start(f32[3,6,48,128]{3,2,1,0:T(8,128)} %get-tuple-element.106), channel_id=1, source_target_pairs={{0,3},{1,2},{2,1},{3,0},{4,7},{5,6},{6,5},{7,4},{8,11},{9,10},{10,... | collective-permute-start | bytes 1327112 | tf_op jit(solution)/shard_map/ppermute | solution.py:449
  290.4 5.7 %copy-start.14 = (f32[2,192,128]{2,1,0:T(8,128)}, f32[2,192,128]{2,1,0:T(8,128)S(1)}, u32[]{:S(2)}) copy-start(f32[2,192,128]{2,1,0:T(8,128)S(1)} %collective-permute-done.16.refs_2_) | copy-start | bytes 589828
  296.1 0.7 copy-start.15
  306.6 51.2 %collective-permute-start.31 = (f32[3,6,48,128]{3,2,1,0:T(8,128)}, f32[3,6,48,128]{3,2,1,0:T(8,128)}, u32[]{:S(2)}, u32[]{:S(2)}) collective-permute-start(f32[3,6,48,128]{3,2,1,0:T(8,128)} %get-tuple-element.102), channel_id=1, source_target_pairs={{0,1},{1,0},{2,3},{3,2},{4,5},{5,4},{6,7},{7,6},{8,9},{9,8},{10,11... | collective-permute-start | bytes 1327112 | tf_op jit(solution)/shard_map/ppermute | solution.py:449
  306.7 60.2 %collective-permute-start.29 = (f32[3,6,48,128]{3,2,1,0:T(8,128)}, f32[3,6,48,128]{3,2,1,0:T(8,128)S(1)}, u32[]{:S(2)}, u32[]{:S(2)}) collective-permute-start(f32[3,6,48,128]{3,2,1,0:T(8,128)} %get-tuple-element.99), channel_id=1, source_target_pairs={{0,2},{1,3},{2,0},{3,1},{4,6},{5,7},{6,4},{7,5},{8,10},{9,11},{10,... | collective-permute-start | bytes 1327112 | tf_op jit(solution)/shard_map/ppermute | solution.py:449
  308.9 36.6 %copy-start.9 = (f32[3,6,48,128]{3,2,1,0:T(8,128)}, f32[3,6,48,128]{3,2,1,0:T(8,128)S(1)}, u32[]{:S(2)}) copy-start(f32[3,6,48,128]{3,2,1,0:T(8,128)S(1)} %collective-permute-done.32.refs_1_) | copy-start | bytes 1327108
  308.9 58.0 %collective-permute-start.30 = (f32[3,6,48,128]{3,2,1,0:T(8,128)}, f32[3,6,48,128]{3,2,1,0:T(8,128)}, u32[]{:S(2)}, u32[]{:S(2)}) collective-permute-start(f32[3,6,48,128]{3,2,1,0:T(8,128)} %get-tuple-element.100), channel_id=1, source_target_pairs={{0,3},{1,2},{2,1},{3,0},{4,7},{5,6},{6,5},{7,4},{8,11},{9,10},{10,... | collective-permute-start | bytes 1327112 | tf_op jit(solution)/shard_map/ppermute | solution.py:449
  315.8 29.7 %copy-start.10 = (f32[3,6,48,128]{3,2,1,0:T(8,128)}, f32[3,6,48,128]{3,2,1,0:T(8,128)S(1)}, u32[]{:S(2)}) copy-start(f32[3,6,48,128]{3,2,1,0:T(8,128)S(1)} %collective-permute-done.33.refs_2_) | copy-start | bytes 1327108
  345.5 0.8 copy-start.11
  366.9 0.8 copy-start.12

commit v2 on v1

--- a/solution.py
+++ b/solution.py
@@ -96,7 +96,7 @@
     return group * block_len + e * half + jnp.where(lane < half, lane, lane - half)
 
 
-def y_fields(ids_ref, *refs, c, e, kind, slabs, chunks):
+def y_fields(ids_ref, *refs, c, e, kind, slabs, chunks, direct, u_pairs):
     moves, stays = kind != "still", kind != "moving"
     s = pl.program_id(0)
     pairs = pl.num_programs(0)
@@ -108,16 +108,14 @@
         refs = refs[6:]
     wh_ref, wl_ref = refs[:2]
     refs = refs[2:]
-    if kind == "moving":
-        us_send, us_keep = refs[:2]
-        refs = refs[2:]
-    send, keep, high, low = refs[:4]
-    ghost = refs[4] if moves else None
+    width = 2 * u_pairs if direct else 2
+    outs, (high, low), ghost = refs[:width], refs[width : width + 2], refs[width + 2 :]
+    ghost = ghost[0] if moves else None
     _, nx, nz, ny = u_ref.shape
     m = nx * nz
-    cw = send.shape[-1]
-    at_u, at_c = (0, m) if stays else (None, None)
-    at_a, at_b = (2 * m, 3 * m) if stays else (0, m)
+    cw = outs[0].shape[-1]
+    at_u, at_c = 0, m
+    at_a, at_b = (2 * m, 3 * m) if stays else (m, 2 * m)
     group = ids_ref[2]
     bit = group & 1
     j = across(group >> 1, s, pairs)
@@ -170,9 +168,9 @@
                 return (u_ref if which else ux_ref)[0, x, :, lanes]
 
             for x in range(nx):
+                u = u_ref[0, x, :, lanes]
+                put(at_u + x * nz, u)
                 if stays:
-                    u = u_ref[0, x, :, lanes]
-                    put(at_u + x * nz, u)
                     put(at_c + x * nz, -uz_ref[0, x, :, lanes] * u)
                 if not moves:
                     continue
@@ -205,22 +203,53 @@
     halves = []
     for b in range(2):
         o = out[:, b * cw : (b + 1) * cw]
-        got = [o[at_u : at_u + m], o[at_c : at_c + m]] if stays else []
+        yu = o[at_u : at_u + m]
+        got = [yu, o[at_c : at_c + m]] if stays else []
         if moves:
             modes = mode_numbers(2 * j + b, e, cw * chunks // 2, cw)
             k = (2.0 * math.pi / ny) * modes.astype(F32)
-            if stays:
-                yu = got[0]
-            else:
-                sent, kept = us_send[0, 0].reshape(m, cw), us_keep[0, 0].reshape(m, cw)
-                yu = pick(bit, kept, sent) if b else pick(bit, sent, kept)
             got.append(
                 o[at_a : at_a + m] + swap(o[at_b : at_b + m]) * (k * sign) - viscosity * (k * k) * yu
             )
         halves.append(got)
-    for f, (lo, hi) in enumerate(zip(*halves)):
-        send[0, f] = pick(bit, lo, hi).reshape(nx, nz, cw)
-        keep[0, f] = pick(bit, hi, lo).reshape(nx, nz, cw)
+
+    def store(send, keep):
+        for f, (lo, hi) in enumerate(zip(*halves)):
+            send[0, f] = pick(bit, lo, hi).reshape(nx, nz, cw)
+            keep[0, f] = pick(bit, hi, lo).reshape(nx, nz, cw)
+
+    if not direct:
+        store(*outs)
+    else:
+        for k in range(u_pairs):
+            pl.when(s == k)(functools.partial(store, outs[2 * k], outs[2 * k + 1]))
+
+
+def z_whole(ids_ref, *refs, layout, pairs):
+    az_ref, ref = refs[-2:]
+    _, _, zb, _, cw = refs[0].shape
+    depth = ref.shape[1]
+    bit, pair = ids_ref[2] & 1, ids_ref[2] >> 1
+    sign = sign_row(cw)
+    for x0 in range(0, zb, 2):
+        xs = range(x0, min(x0 + 2, zb))
+        out = None
+        for s in range(pairs):
+            columns = []
+            for x in xs:
+                rows = []
+                for a, f in layout:
+                    at = 2 * (a * pairs + s)
+                    same, other = refs[at][0, f, x], refs[at + 1][0, f, x]
+                    rows += [pick(bit, other, same), pick(bit, same, other)]
+                columns.append(jnp.concatenate(rows, axis=0))
+            h, l = parts(jnp.concatenate(columns, axis=-1))
+            matrix = az_ref[sender(pair, s, pairs)]
+            term = dot(matrix, jnp.concatenate([h, h, l], axis=0))
+            out = term if out is None else out + term
+        for i, x in enumerate(xs):
+            lanes = slice(i * cw, (i + 1) * cw)
+            ref[x] = out[:depth, lanes] + swap(out[depth:, lanes]) * sign
 
 
 def z_partial(ids_ref, *refs, layout):
@@ -249,12 +278,20 @@
                 ref[x] = out[:depth, lanes] + swap(out[depth:, lanes]) * sign
 
 
+def split(refs, pieces):
+    out, at = [], 0
+    for n in pieces:
+        out.append(refs[at : at + n])
+        at += n
+    return out
+
+
 def first_sweep(*refs, e, chunks, pieces):
-    tx, ty, tz = (refs[c * pieces : (c + 1) * pieces] for c in range(3))
+    tx, ty, tz = split(refs, pieces)
     (
         p_ref, txl_ref, txh_ref, pl_ref, ph_ref, rot_ref, ky_ref, kz_ref, rden_ref,
         div_ref, out_ref, lo_ref, hi_ref,
-    ) = refs[3 * pieces :]
+    ) = refs[sum(pieces) :]
     nx, _, cols = div_ref.shape
     sign = sign_row(cols)
     ky = ky_ref[...] * sign
@@ -297,9 +334,9 @@
 def finish(ids_ref, *refs, e, chunks, pieces, groups):
     p1_ref, div_ref, lo_ref, hi_ref, rot_ref, ky_ref, kz_ref, rden_ref, ck_ref = refs[:9]
     refs = refs[9:]
-    t_refs = [refs[c * pieces : (c + 1) * pieces] for c in range(3)]
-    q_ref, bh_ref, bl_ref = refs[3 * pieces : 3 * pieces + 3]
-    refs = refs[3 * pieces + 3 :]
+    t_refs = split(refs, pieces)
+    q_ref, bh_ref, bl_ref = refs[sum(pieces) : sum(pieces) + 3]
+    refs = refs[sum(pieces) + 3 :]
     last = e == chunks - 1
     earlier = chunks > 1 and last
     if earlier:
@@ -360,27 +397,33 @@
 
 
 def y_inverse(ids_ref, *refs, terms, groups):
-    base_ref, wh_ref, wl_ref, out_ref, th, tl = refs[-6:]
-    blocks = refs[:-6]
-    _, xb, nz, cols = blocks[0].shape
-
-    @pl.when((pl.program_id(0) == 0) & (pl.program_id(1) == 0))
+    base_ref, wh_ref, wl_ref, out_ref, rh, rl, th, tl = refs[-8:]
+    blocks = refs[:-8]
+    comps, nx, nz, cols = blocks[0].shape
+    m = nx * nz
+
+    @pl.when(pl.program_id(0) == 0)
     def _():
-        for i, (e, place) in enumerate(terms):
-            g = sender(ids_ref[2], place, groups)
+        for i, block in enumerate(blocks):
             at = slice(i * cols, (i + 1) * cols)
-            for b in range(2):
-                lanes = slice(b * cols, (b + 1) * cols)
-
-                @pl.when(g & 1 == b)
-                def _():
-                    th[:, at] = wh_ref[e, g >> 1, :, lanes]
-                    tl[:, at] = wl_ref[e, g >> 1, :, lanes]
-
-    rows = jnp.concatenate([b[0].reshape(xb * nz, cols) for b in blocks], axis=-1)
-    total = dot3(parts(rows), (th[...], tl[...]), dot_t)
-    ny = total.shape[-1]
-    out_ref[0] = base_ref[0] + section_weight * total.reshape(xb, nz, ny)
+            for c in range(comps):
+                h, l = parts(block[c].reshape(m, cols))
+                rh[c * m : (c + 1) * m, at] = h
+                rl[c * m : (c + 1) * m, at] = l
+
+    for i, (e, place) in enumerate(terms):
+        g = sender(ids_ref[2], place, groups)
+        at = slice(i * cols, (i + 1) * cols)
+        for b in range(2):
+            lanes = slice(b * cols, (b + 1) * cols)
+
+            @pl.when(g & 1 == b)
+            def _():
+                th[:, at] = wh_ref[e, g >> 1, :, lanes]
+                tl[:, at] = wl_ref[e, g >> 1, :, lanes]
+
+    total = dot3((rh[...], rl[...]), (th[...], tl[...]), dot_t)
+    out_ref[...] = base_ref[...] + section_weight * total.reshape(out_ref.shape)
 
 
 def whole(shape):
@@ -401,6 +444,9 @@
         cost_estimate=pl.CostEstimate(flops=int(flops), bytes_accessed=int(moved), transcendentals=0),
         **kw,
     )
+
+
+DIRECT = ((0, 0), (2, 1))
 
 
 def section(vel, q_old, pressure_guess, shear_shift):
@@ -445,22 +491,20 @@
     down = [((i + 1) % slabs, i) for i in range(slabs)]
     twins = [(i, i ^ 1) for i in range(groups)]
 
-    def send(x, axis, to):
-        return lax.ppermute(x, axis, to)
-
     def exchange(first, last):
-        return send(last, "gx", up), send(first, "gx", down)
+        return lax.ppermute(last, "gx", up), lax.ppermute(first, "gx", down)
 
     m = nx * nz
     y_flops = 2 * m * ny * ny * 3
     half_bytes = 4 * m * ny
     comp = lambda c: pl.BlockSpec((1, nx, nz, ny), lambda p: (c, 0, 0, 0))
 
-    def fields(kind, c, e, halos=(), us=()):
+    def fields(kind, c, e, halos=(), direct=False):
         moves, stays = kind != "still", kind != "moving"
-        count = 2 * (moves + stays)
+        count = {"still": 2, "moving": 3, "full": 4}[kind]
+        width = 2 * pairs if direct else 2
         n_out = 2 * stays + moves
-        block = lambda f: pl.BlockSpec((1, f, nx, nz, cw), lambda p: (p, 0, 0, 0, 0))
+        block = lambda f: pl.BlockSpec((1, f, nx, nz, cw), lambda p: (0 if direct else p, 0, 0, 0, 0))
         tables = pl.BlockSpec((1, pairs, ny, 2 * cw), lambda p: (e, 0, 0, 0))
         args, specs = [ids, vel], [SMEM, comp(c)]
         if stays:
@@ -469,16 +513,18 @@
         if moves:
             args += [vel, vel, halos[0][0], halos[c][0], halos[0][1], halos[c][1]]
             specs += [comp(0), comp(1)] + [whole((3, nz, ny))] * 4
-        args += [wh, wl, *us]
-        specs += [tables] * 2 + [block(1)] * len(us)
+        args += [wh, wl]
+        specs += [tables] * 2
         return call(
-            functools.partial(y_fields, c=c, e=e, kind=kind, slabs=slabs, chunks=chunks),
+            functools.partial(
+                y_fields, c=c, e=e, kind=kind, slabs=slabs, chunks=chunks, direct=direct, u_pairs=pairs
+            ),
             count * y_flops // chunks,
             count * half_bytes,
             grid=(pairs,),
             in_specs=specs,
-            out_specs=[block(n_out)] * 2,
-            out_shape=[shaped(pairs, n_out, nx, nz, cw)] * 2,
+            out_specs=[block(n_out)] * width,
+            out_shape=[shaped(1 if direct else pairs, n_out, nx, nz, cw)] * width,
             scratch_shapes=[pltpu.VMEM((count * m, ny), BF16)] * 2
             + ([pltpu.VMEM((2, 6, nz, ny), F32)] if moves else []),
         )(*args)
@@ -504,29 +550,64 @@
         pieces = [outs[0]]
         for s in range(1, pairs):
             to = [(i, int(across(i // 2, s, pairs)) * 2 + i % 2) for i in range(groups)]
-            pieces.append(send(outs[s], "yz", to))
+            pieces.append(lax.ppermute(outs[s], "yz", to))
         return pieces
 
     halos = [exchange(vel[0, :3], vel[0, nx - 3 :])]
     tend = [[None] * 3 for _ in range(chunks)]
-    us_send, us_keep = fields("still", 0, 0)
-    later, us_send, us_keep = lax.optimization_barrier((vel, us_send, us_keep))
+
+    def spread_out(outs):
+        got = []
+        for s in range(pairs):
+            send_s, keep_s = outs[2 * s], outs[2 * s + 1]
+            same = [(i, int(across(i // 2, s, pairs)) * 2 + i % 2) for i in range(groups)]
+            other = [(i, t ^ 1) for i, t in same]
+            got.append(lax.ppermute(keep_s, "yz", same) if s else keep_s)
+            got.append(lax.ppermute(send_s, "yz", other))
+        return got
+
+    def z_direct(arrays, layout):
+        return [
+            call(
+                functools.partial(z_whole, layout=layout, pairs=pairs),
+                2 * az.size * nx * cw,
+                10 * half_bytes // groups,
+                grid=(nx // zb,),
+                in_specs=[SMEM]
+                + [
+                    pl.BlockSpec((1, v.shape[1], zb, nz, cw), lambda x: (0, 0, x, 0, 0))
+                    for v in arrays
+                ]
+                + [whole(az.shape)],
+                out_specs=pl.BlockSpec((zb,) + plane, lambda x: (x, 0, 0)),
+                out_shape=shaped(nx, *plane),
+            )(ids, *arrays, az)
+        ]
+
+    us = fields("still", 0, 0, direct=True)
+    later, us = lax.optimization_barrier((vel, us))
     for d in (1, 2):
         halos.append(exchange(later[d, :3], later[d, nx - 3 :]))
-    w_send, w_keep = fields("moving", 0, 0, halos, (us_send, us_keep))
-    arrays = (us_keep, send(us_send, "yz", twins), w_keep, send(w_send, "yz", twins))
-    tend[0][0] = z_part(arrays, ((1, 0), (0, 1), (0, 0)))
+    w = fields("moving", 0, 0, halos, direct=True)
+    arrays = spread_out(us) + spread_out(w)
+    tend[0][0] = z_direct(arrays, ((1, 0), (0, 1), (0, 0)))
     late = ids
     guess = pressure_guess
     for e in range(chunks):
         for c in range(3):
-            if (c, e) == (0, 0):
+            if tend[e][c]:
                 continue
-            sent, kept = fields("full", c, e, halos)
+            direct = (c, e) in DIRECT
+            outs = fields("full", c, e, halos, direct)
             if (c, e) == (1, chunks - 1):
-                late, guess, sent, kept = lax.optimization_barrier((late, guess, sent, kept))
-            arrays = (kept, send(sent, "yz", twins))
-            tend[e][c] = z_part(arrays, ((0, 2), (0, 1), (0, 0)))
+                late, guess, outs = lax.optimization_barrier((late, guess, outs))
+            if direct:
+                arrays = spread_out(outs)
+                tend[e][c] = z_direct(arrays, ((0, 2), (0, 1), (0, 0)))
+            else:
+                sent, kept = outs
+                arrays = (kept, lax.ppermute(sent, "yz", twins))
+                tend[e][c] = z_part(arrays, ((0, 2), (0, 1), (0, 0)))
     p_low, p_high = exchange(guess[:1], guess[nx - 1 :])
 
     offset, slab_id, group_id = late[0], late[1], late[2]
@@ -569,9 +650,10 @@
     back = []
     for e in range(chunks):
         flat = [piece for c in range(3) for piece in tend[e][c]]
+        pieces = tuple(len(tend[e][c]) for c in range(3))
         t_low, t_high = edges[e]
         div, p1, lo, hi = call(
-            functools.partial(first_sweep, e=e, chunks=chunks, pieces=pairs),
+            functools.partial(first_sweep, e=e, chunks=chunks, pieces=pieces),
             2000 * nx * depth * cw,
             2 * half_bytes,
             out_shape=[shaped(nx, *plane)] * 2 + [shaped(2, *plane)] * 2,
@@ -582,7 +664,7 @@
         out_plane = packed if last else plane
         consts = (p1, div, lo_halo, hi_halo, rots[e], kys[e], kz, rdens[e], cks[e])
         outs = call(
-            functools.partial(finish, e=e, chunks=chunks, pieces=pairs, groups=groups),
+            functools.partial(finish, e=e, chunks=chunks, pieces=pieces, groups=groups),
             2 * 3 * 3 * nx * 2 * depth * depth * cw,
             3 * half_bytes,
             grid=(nx // fb,),
@@ -604,27 +686,28 @@
         got = [outs[2]]
         for place in range(1, groups):
             to = [(i, int(partner(i, place, groups))) for i in range(groups)]
-            got.append(send(outs[2 + place], "yz", to))
+            got.append(lax.ppermute(outs[2 + place], "yz", to))
         back.append(got)
 
-    vb = 3 if nx % 3 == 0 else 1
-    vel_block = pl.BlockSpec((1, vb, nz, ny), lambda c, x: (c, x, 0, 0))
+    yb = ny // 4
+    vel_block = pl.BlockSpec((3, nx, nz, yb), lambda i: (0, 0, 0, i))
+    table_block = pl.BlockSpec((chunks, pairs, yb, 2 * cw), lambda i: (0, 0, i, 0))
     batches = [[(e, place) for place in range(groups)] for e in range(chunks - 1)]
-    batches += [[(chunks - 1, place) for place in range(2)]]
-    batches += [[(chunks - 1, place) for place in range(2, groups)]]
+    batches += [[(chunks - 1, place) for place in range(groups)]]
     vel_next = vel
     for terms in batches:
         vel_next = call(
             functools.partial(y_inverse, terms=terms, groups=groups),
             3 * y_flops * len(terms) // (chunks * groups),
             6 * half_bytes,
-            grid=(3, nx // vb),
+            grid=(ny // yb,),
             in_specs=[SMEM]
-            + [pl.BlockSpec((1, vb, nz, cw), lambda c, x: (c, x, 0, 0))] * len(terms)
-            + [vel_block, whole(wh.shape), whole(wl.shape)],
+            + [whole((3, nx, nz, cw))] * len(terms)
+            + [vel_block, table_block, table_block],
             out_specs=vel_block,
             out_shape=jax.ShapeDtypeStruct(vel.shape, F32),
-            scratch_shapes=[pltpu.VMEM((ny, len(terms) * cw), BF16)] * 2,
+            scratch_shapes=[pltpu.VMEM((3 * m, len(terms) * cw), BF16)] * 2
+            + [pltpu.VMEM((yb, len(terms) * cw), BF16)] * 2,
         )(ids, *[back[e][place] for e, place in terms], vel_next, wh, wl)
     return (vel_next, q_done[0], q_done[1])
 

time: 382 us -> 388 us (1.016); the launches traced: 377 us -> 387 us
  waiting for transfers between devices: 119 us -> 151 us
  Pallas kernels: 165 us -> 153 us
  starting transfers between devices: 66.5 us -> 57.3 us
    ppermute x35 -> x39, waiting for transfers between devices: 119 us -> 151 us  [the longest x6 50.8 us: section(): got.append(lax.ppermute(outs[2 + place], 'yz', to))]
    pallas_call x3 -> x2, Pallas kernels: 29.5 us -> 16.7 us  [section(): call(functools.partial(y_inverse, terms=terms, groups=groups), 3 * y_flop...]
    pallas_call x6 -> x4, Pallas kernels: 29.9 us -> 19.8 us  [z_part(): call(functools.partial(z_partial, layout=layout), 2 * az.size * nx * cw,...]
    ppermute x35 -> x39, starting transfers between devices: 66.5 us -> 57.3 us  [the longest x16 29.2 us: exchange(): return (lax.ppermute(last, 'gx', up), lax.ppermute(first, 'gx', down))]
    pallas_call x4 -> x6, Pallas kernels: 27.4 us -> 36.4 us  [the longest x2 17.8 us: section(): call(functools.partial(finish, e=e, chunks=chunks, pieces=pieces, groups=...]
  transfers between devices with their start and end apart: 35 -> 39, of which waited for: 8 -> 14; matrix products, arithmetic and copies ran while one was open for 4% -> 4% of each run, Pallas kernels for 41% -> 37%
where the time goes in v2:
time: 388 us; the launch traced here: 387 us
  Pallas kernels  153 us (39%)
  waiting for transfers between devices  151 us (39%)
  starting transfers between devices  57.3 us (15%)
  local copies, waits for them, and re-layouts  14.3 us (4%)
  other arithmetic  8.59 us (2%)
    pallas_call x7, Pallas kernels, fields(): call(functools.partial(y_fields, c=c, e=e, kind=kind, slabs=slabs, chunks...  79.9 us
    ppermute x6, waiting for transfers between devices, section(): got.append(lax.ppermute(outs[2 + place], 'yz', to))  50.8 us
    ppermute x4, waiting for transfers between devices, z_part(): pieces.append(lax.ppermute(outs[s], 'yz', to))  42.8 us
    ppermute x16, starting transfers between devices, exchange(): return (lax.ppermute(last, 'gx', up), lax.ppermute(first, 'gx', down))  29.2 us
    ppermute x6, waiting for transfers between devices, spread_out(): got.append(lax.ppermute(send_s, 'yz', other))  28.6 us
    ppermute x16, waiting for transfers between devices, exchange(): return (lax.ppermute(last, 'gx', up), lax.ppermute(first, 'gx', down))  22.1 us
    pallas_call x4, Pallas kernels, z_part(): call(functools.partial(z_partial, layout=layout), 2 * az.size * nx * cw,...  19.8 us
    pallas_call x2, Pallas kernels, section(): call(functools.partial(finish, e=e, chunks=chunks, pieces=pieces, groups=...  17.8 us
  transfers between devices with their start and end apart: 39, of which 14 were waited for; matrix products, arithmetic and copies ran while one was open for 4% of the time, Pallas kernels for 37%

profile of v2, /device:TPU:13, one launch (start us, length us, event | category | flops | bytes accessed | tf_op | source)
XLA Modules:
  0.0 387.4 jit_solution(14107081157665804756)
XLA Ops:
  0.6 2.4 slice_bitcast_fusion.4
  3.0 0.7 collective-permute-start.1
  3.7 1.1 collective-permute-start
  6.0 6.3 %shard_map.123 = (f32[1,2,6,48,128]{4,3,2,1,0:T(8,128)}, f32[1,2,6,48,128]{4,3,2,1,0:T(8,128)}, f32[1,2,6,48,128]{4,3,2,1,0:T(8,128)}, f32[1,2,6,48,128]{4,3,2,1,0:T(8,128)}) custom-call(s32[3]{0:T(128)} %pad_add_fusion.ids_ref, f32[3,6,48,1024]{3,2,1,0:T(8,128)} %refs_4_.2, f32[3,6,48,1024]{3,2,1,0:T(8,128)} %refs_4_.2, ...), custom_call_target="tpu_custom_call" | custom-call | flops 1811939328 | bytes 2359296 | tf_op jit(solution)/shard_map/pallas_call | solution.py:518
  12.3 3.1 slice_bitcast_fusion
  15.4 1.7 collective-permute-start.8
  17.4 1.2 collective-permute-start.5
  18.6 2.0 collective-permute-start.4
  20.6 12.1 %shard_map.121 = (f32[2,3,6,48,128]{4,3,2,1,0:T(8,128)}, f32[2,3,6,48,128]{4,3,2,1,0:T(8,128)}) custom-call(s32[3]{0:T(128)} %pad_add_fusion.ids_ref, f32[3,6,48,1024]{3,2,1,0:T(8,128)} %refs_4_.2, f32[3,6,48,1024]{3,2,1,0:T(8,128)} %refs_4_.2, f32[3,6,48,1024]{3,2,1,0:T(8,128)} %refs_4_.2, f32[3,6,48,1024]{3,2,1,0:T(8,128)} %refs_4_.2, ...), custom_call_target="tpu_custom_call" | custom-call | flops 3623878656 | bytes 4718592 | tf_op jit(solution)/shard_map/pallas_call | solution.py:518
  32.7 2.4 collective-permute-start.20
  35.2 12.6 %shard_map.133 = (f32[2,3,6,48,128]{4,3,2,1,0:T(8,128)}, f32[2,3,6,48,128]{4,3,2,1,0:T(8,128)}) custom-call(s32[3]{0:T(128)} %pad_add_fusion.ids_ref, f32[3,6,48,1024]{3,2,1,0:T(8,128)} %refs_4_.2, f32[3,6,48,1024]{3,2,1,0:T(8,128)} %refs_4_.2, f32[3,6,48,1024]{3,2,1,0:T(8,128)} %refs_4_.2, f32[3,6,48,1024]{3,2,1,0:T(8,128)} %refs_4_.2, ...), custom_call_target="tpu_custom_call" | custom-call | flops 3623878656 | bytes 4718592 | tf_op jit(solution)/shard_map/pallas_call | solution.py:518
  47.9 1.4 collective-permute-start.27
  49.2 12.8 %shard_map.124 = (f32[2,3,6,48,128]{4,3,2,1,0:T(8,128)}, f32[2,3,6,48,128]{4,3,2,1,0:T(8,128)}) custom-call(s32[3]{0:T(128)} %pad_add_fusion.ids_ref, f32[3,6,48,1024]{3,2,1,0:T(8,128)} %refs_4_.2, f32[3,6,48,1024]{3,2,1,0:T(8,128)} %refs_4_.2, f32[3,6,48,1024]{3,2,1,0:T(8,128)} %refs_4_.2, f32[3,6,48,1024]{3,2,1,0:T(8,128)} %refs_4_.2, ...), custom_call_target="tpu_custom_call" | custom-call | flops 3623878656 | bytes 4718592 | tf_op jit(solution)/shard_map/pallas_call | solution.py:518
  64.0 1.7 fusion.13
  65.8 12.7 %shard_map.131 = (f32[2,3,6,48,128]{4,3,2,1,0:T(8,128)}, f32[2,3,6,48,128]{4,3,2,1,0:T(8,128)}) custom-call(s32[3]{0:T(128)} %pad_add_fusion.ids_ref, f32[3,6,48,1024]{3,2,1,0:T(8,128)} %refs_4_.2, f32[3,6,48,1024]{3,2,1,0:T(8,128)} %refs_4_.2, f32[3,6,48,1024]{3,2,1,0:T(8,128)} %refs_4_.2, f32[3,6,48,1024]{3,2,1,0:T(8,128)} %refs_4_.2, ...), custom_call_target="tpu_custom_call" | custom-call | flops 3623878656 | bytes 4718592 | tf_op jit(solution)/shard_map/pallas_call | solution.py:518
  79.2 10.2 %shard_map.129 = (f32[1,1,6,48,128]{4,3,2,1,0:T(8,128)}, f32[1,1,6,48,128]{4,3,2,1,0:T(8,128)}, f32[1,1,6,48,128]{4,3,2,1,0:T(8,128)}, f32[1,1,6,48,128]{4,3,2,1,0:T(8,128)}) custom-call(s32[3]{0:T(128)} %pad_add_fusion.ids_ref, f32[3,6,48,1024]{3,2,1,0:T(8,128)} %refs_4_.2, f32[3,6,48,1024]{3,2,1,0:T(8,128)} %refs_4_.2, f32[3,6,48,1024]{3,2,1,0:T(8,128)} %refs_4_.2, ...), custom_call_target="tpu_custom_call" | custom-call | flops 2717908992 | bytes 3538944 | tf_op jit(solution)/shard_map/pallas_call | solution.py:518
  89.4 13.2 %shard_map.126 = (f32[1,3,6,48,128]{4,3,2,1,0:T(8,128)}, f32[1,3,6,48,128]{4,3,2,1,0:T(8,128)}, f32[1,3,6,48,128]{4,3,2,1,0:T(8,128)}, f32[1,3,6,48,128]{4,3,2,1,0:T(8,128)}) custom-call(s32[3]{0:T(128)} %pad_add_fusion.ids_ref, f32[3,6,48,1024]{3,2,1,0:T(8,128)} %refs_4_.2, f32[3,6,48,1024]{3,2,1,0:T(8,128)} %refs_4_.2, f32[3,6,48,1024]{3,2,1,0:T(8,128)} %refs_4_.2, ...), custom_call_target="tpu_custom_call" | custom-call | flops 3623878656 | bytes 4718592 | tf_op jit(solution)/shard_map/pallas_call | solution.py:518
  102.6 0.7 broadcast_select_fusion.6
  103.3 0.7 broadcast_select_fusion.2
  104.9 0.8 add_divide_fusion
  105.6 1.5 collective-permute-start.22
  107.2 0.7 broadcast_select_fusion.4
  107.8 10.1 %collective-permute-done.21.refs_3_ = f32[1,2,6,48,128]{4,3,2,1,0:T(8,128)S(1)} collective-permute-done((f32[1,2,6,48,128]{4,3,2,1,0:T(8,128)S(1)}, f32[1,2,6,48,128]{4,3,2,1,0:T(8,128)S(1)}, u32[]{:S(2)}, u32[]{:S(2)}) %collective-permute-start.21) | collective-permute-done | bytes 294944 | tf_op jit(solution)/shard_map/ppermute | solution.py:566
  118.0 0.7 broadcast_select_fusion
  118.7 2.1 collective-permute-start.23
  121.8 5.0 %shard_map.134 = (f32[6,192,128]{2,1,0:T(8,128)}, f32[6,192,128]{2,1,0:T(8,128)}) custom-call(s32[3]{0:T(128)} %pad_add_fusion.ids_ref, f32[2,3,6,48,128]{4,3,2,1,0:T(8,128)} %get-tuple-element.97.refs_0_, f32[2,3,6,48,128]{4,3,2,1,0:T(8,128)} %copy-done.22, bf16[2,384,864]{2,1,0:T(8,128)(2,1)} %constant.83.clone.refs_2_.refs_4_.refs_8_), custom_call_target="tpu_custom_call" | custom-call | flops 1019215872 | bytes 2949120 | tf_op jit(solution)/shard_map/pallas_call | solution.py:536
  126.8 3.0 collective-permute-start.16
  129.8 5.0 %shard_map.132 = (f32[6,192,128]{2,1,0:T(8,128)}, f32[6,192,128]{2,1,0:T(8,128)}) custom-call(s32[3]{0:T(128)} %pad_add_fusion.ids_ref, f32[2,3,6,48,128]{4,3,2,1,0:T(8,128)} %get-tuple-element.93.refs_0_, f32[2,3,6,48,128]{4,3,2,1,0:T(8,128)} %collective-permute-done.25.refs_1_, bf16[2,384,864]{2,1,0:T(8,128)(2,1)} %constant.83.clone.refs_2_.refs_4_.refs_8_), custom_call_target="tpu_custom_call" | custom-call | flops 1019215872 | bytes 2949120 | tf_op jit(solution)/shard_map/pallas_call | solution.py:536
  134.7 6.4 %collective-permute-done.23.refs_6_ = f32[1,1,6,48,128]{4,3,2,1,0:T(8,128)S(1)} collective-permute-done((f32[1,1,6,48,128]{4,3,2,1,0:T(8,128)}, f32[1,1,6,48,128]{4,3,2,1,0:T(8,128)S(1)}, u32[]{:S(2)}, u32[]{:S(2)}) %collective-permute-start.23) | collective-permute-done | bytes 147488 | tf_op jit(solution)/shard_map/ppermute | solution.py:565
  142.5 3.3 collective-permute-start.26
  145.8 4.8 %shard_map.130.refs_0_.refs_9_ = f32[6,192,128]{2,1,0:T(8,128)} custom-call(s32[3]{0:T(128)} %pad_add_fusion.ids_ref, f32[1,2,6,48,128]{4,3,2,1,0:T(8,128)} %get-tuple-element.85.refs_0_, f32[1,2,6,48,128]{4,3,2,1,0:T(8,128)} %collective-permute-done.19.refs_1_, f32[1,2,6,48,128]{4,3,2,1,0:T(8,128)} %copy-done.23, f32[1,2,6,48,128]{4,3,2,1,0:T(8,128)} %copy-done.25, ...), custom_call_target="tpu_custom_call" | custom-call | flops 1019215872 | bytes 2949120 | tf_op jit(solution)/shard_map/pallas_call | solution.py:571
  150.6 8.7 %collective-permute-start.15 = (f32[1,192,256]{2,1,0:T(8,128)}, f32[1,192,256]{2,1,0:T(8,128)}, u32[]{:S(2)}, u32[]{:S(2)}) collective-permute-start(f32[1,192,256]{2,1,0:T(8,128)} %get-tuple-element.124), channel_id=1, source_target_pairs={{0,4},{4,8},{8,12},{12,16},{16,20},{20,24},{24,28},{28,0},{1,5},{5... | collective-permute-start | bytes 589832 | tf_op jit(solution)/shard_map/ppermute | solution.py:495
  159.3 5.0 %shard_map.122 = (f32[6,192,128]{2,1,0:T(8,128)}, f32[6,192,128]{2,1,0:T(8,128)}) custom-call(s32[3]{0:T(128)} %pad_add_fusion.ids_ref, f32[2,3,6,48,128]{4,3,2,1,0:T(8,128)} %get-tuple-element.60.refs_0_, f32[2,3,6,48,128]{4,3,2,1,0:T(8,128)} %collective-permute-done.2.refs_1_, bf16[2,384,864]{2,1,0:T(8,128)(2,1)} %constant.83.clone.refs_2_.refs_4_.refs_8_), custom_call_target="tpu_custom_call" | custom-call | flops 1019215872 | bytes 2949120 | tf_op jit(solution)/shard_map/pallas_call | solution.py:536
  164.3 1.0 slice_bitcast_fusion.6
  166.1 3.7 collective-permute-done.30.refs_7_
  170.4 1.1 collective-permute-done.29.refs_6_
  172.0 23.7 %collective-permute-done.28.refs_4_.refs_13_ = f32[6,192,128]{2,1,0:T(8,128)S(1)} collective-permute-done((f32[6,192,128]{2,1,0:T(8,128)}, f32[6,192,128]{2,1,0:T(8,128)S(1)}, u32[]{:S(2)}, u32[]{:S(2)}) %collective-permute-start.28) | collective-permute-done | bytes 589856 | tf_op jit(solution)/shard_map/ppermute | solution.py:553
  195.7 3.0 collective-permute-start.11
  198.7 19.1 %collective-permute-done.26.refs_2_.refs_11_ = f32[6,192,128]{2,1,0:T(8,128)S(1)} collective-permute-done((f32[6,192,128]{2,1,0:T(8,128)}, f32[6,192,128]{2,1,0:T(8,128)S(1)}, u32[]{:S(2)}, u32[]{:S(2)}) %collective-permute-start.26) | collective-permute-done | bytes 589856 | tf_op jit(solution)/shard_map/ppermute | solution.py:553
  217.8 0.8 copy-done.6
  218.6 4.4 %shard_map.135 = (f32[6,192,128]{2,1,0:T(8,128)}, f32[6,192,128]{2,1,0:T(8,128)}, f32[2,192,128]{2,1,0:T(8,128)}, f32[2,192,128]{2,1,0:T(8,128)}) custom-call(f32[6,192,128]{2,1,0:T(8,128)} %shard_map.130.refs_0_.refs_9_, f32[6,192,128]{2,1,0:T(8,128)} %get-tuple-element.95.refs_1_.refs_10_, f32[6,192,128]{2,1,0:T(8,128)} %copy-done.6, ...), custom_call_target="tpu_custom_call" | custom-call | flops 294912000 | bytes 2359296 | tf_op jit(solution)/shard_map/pallas_call | solution.py:655
  223.1 5.2 %collective-permute-start.31 = (f32[2,192,128]{2,1,0:T(8,128)}, f32[2,192,128]{2,1,0:T(8,128)S(1)}, u32[]{:S(2)}, u32[]{:S(2)}) collective-permute-start(f32[2,192,128]{2,1,0:T(8,128)} %get-tuple-element.103), channel_id=1, source_target_pairs={{0,4},{4,8},{8,12},{12,16},{16,20},{20,24},{24,28},{28,0},{1,5},{5... | collective-permute-start | bytes 589832 | tf_op jit(solution)/shard_map/ppermute | solution.py:495
  228.3 5.0 %shard_map.125 = (f32[6,192,128]{2,1,0:T(8,128)}, f32[6,192,128]{2,1,0:T(8,128)}) custom-call(s32[3]{0:T(128)} %pad_add_fusion.ids_ref, f32[2,3,6,48,128]{4,3,2,1,0:T(8,128)} %get-tuple-element.71.refs_0_, f32[2,3,6,48,128]{4,3,2,1,0:T(8,128)} %collective-permute-done.6.refs_1_, bf16[2,384,864]{2,1,0:T(8,128)(2,1)} %constant.83.clone.refs_2_.refs_4_.refs_8_), custom_call_target="tpu_custom_call" | custom-call | flops 1019215872 | bytes 2949120 | tf_op jit(solution)/shard_map/pallas_call | solution.py:536
  233.3 3.0 collective-permute-start.7
  236.9 1.2 fusion
  238.1 13.8 %collective-permute-done.32.refs_3_ = f32[2,192,128]{2,1,0:T(8,128)S(1)} collective-permute-done((f32[2,192,128]{2,1,0:T(8,128)}, f32[2,192,128]{2,1,0:T(8,128)S(1)}, u32[]{:S(2)}, u32[]{:S(2)}) %collective-permute-start.32) | collective-permute-done | bytes 196640 | tf_op jit(solution)/shard_map/ppermute | solution.py:495
  252.6 8.1 %shard_map.136 = (f32[3,6,192,128]{3,2,1,0:T(8,128)}, f32[6,192,128]{2,1,0:T(8,128)}, f32[3,6,48,128]{3,2,1,0:T(8,128)}, f32[3,6,48,128]{3,2,1,0:T(8,128)}, f32[...) custom-call(s32[3]{0:T(128)} %pad_add_fusion.ids_ref, f32[6,192,128]{2,1,0:T(8,128)} %get-tuple-element.101.refs_0_, ...), custom_call_target="tpu_custom_call" | custom-call | flops 1019215872 | bytes 3538944 | tf_op jit(solution)/shard_map/pallas_call | solution.py:666
  260.7 1.1 collective-permute-start.13
  262.1 4.6 %collective-permute-start.36 = (f32[3,6,48,128]{3,2,1,0:T(8,128)}, f32[3,6,48,128]{3,2,1,0:T(8,128)S(1)}, u32[]{:S(2)}, u32[]{:S(2)}) collective-permute-start(f32[3,6,48,128]{3,2,1,0:T(8,128)} %get-tuple-element.112), channel_id=1, source_target_pairs={{0,1},{1,0},{2,3},{3,2},{4,5},{5,4},{6,7},{7,6},{8,9},{9,8},{10,11... | collective-permute-start | bytes 1327112 | tf_op jit(solution)/shard_map/ppermute | solution.py:689
  267.2 18.4 %collective-permute-done.12.refs_3_ = f32[1,3,6,48,128]{4,3,2,1,0:T(8,128)} collective-permute-done((f32[1,3,6,48,128]{4,3,2,1,0:T(8,128)}, f32[1,3,6,48,128]{4,3,2,1,0:T(8,128)}, u32[]{:S(2)}, u32[]{:S(2)}) %collective-permute-start.12) | collective-permute-done | bytes 442400 | tf_op jit(solution)/shard_map/ppermute | solution.py:566
  285.7 4.9 %shard_map.127.refs_4_.refs_13_ = f32[6,192,128]{2,1,0:T(8,128)} custom-call(s32[3]{0:T(128)} %pad_add_fusion.ids_ref, f32[1,3,6,48,128]{4,3,2,1,0:T(8,128)} %get-tuple-element.75.refs_0_, f32[1,3,6,48,128]{4,3,2,1,0:T(8,128)} %collective-permute-done.10.refs_1_, f32[1,3,6,48,128]{4,3,2,1,0:T(8,128)} %collective-permute-done.11.refs_2_, ...), custom_call_target="tpu_custom_call" | custom-call | flops 1019215872 | bytes 2949120 | tf_op jit(solution)/shard_map/pallas_call | solution.py:571
  290.6 0.8 copy-done.3
  291.4 4.4 %shard_map.128 = (f32[6,192,128]{2,1,0:T(8,128)}, f32[6,192,128]{2,1,0:T(8,128)}, f32[2,192,128]{2,1,0:T(8,128)}, f32[2,192,128]{2,1,0:T(8,128)}) custom-call(f32[6,192,128]{2,1,0:T(8,128)} %get-tuple-element.62.refs_0_.refs_9_, f32[6,192,128]{2,1,0:T(8,128)} %copy-done.2, f32[6,192,128]{2,1,0:T(8,128)} %get-tuple-element.73.refs_2_.refs_11_, ...), custom_call_target="tpu_custom_call" | custom-call | flops 294912000 | bytes 2359296 | tf_op jit(solution)/shard_map/pallas_call | solution.py:655
  295.9 4.2 %collective-permute-start.17 = (f32[2,192,128]{2,1,0:T(8,128)}, f32[2,192,128]{2,1,0:T(8,128)S(1)}, u32[]{:S(2)}, u32[]{:S(2)}) collective-permute-start(f32[2,192,128]{2,1,0:T(8,128)} %get-tuple-element.83), channel_id=1, source_target_pairs={{0,4},{4,8},{8,12},{12,16},{16,20},{20,24},{24,28},{28,0},{1,5},{5... | collective-permute-start | bytes 589832 | tf_op jit(solution)/shard_map/ppermute | solution.py:495
  300.0 1.7 collective-permute-start.38
  302.3 2.7 collective-permute-done.17.refs_2_
  306.3 9.7 %shard_map.137 = (f32[3,6,192,256]{3,2,1,0:T(8,128)}, f32[6,192,256]{2,1,0:T(8,128)}, f32[3,6,48,128]{3,2,1,0:T(8,128)}, f32[3,6,48,128]{3,2,1,0:T(8,128)}, f32[...) custom-call(s32[3]{0:T(128)} %pad_add_fusion.ids_ref, f32[6,192,128]{2,1,0:T(8,128)} %get-tuple-element.81.refs_0_, ...), custom_call_target="tpu_custom_call" | custom-call | flops 1019215872 | bytes 3538944 | tf_op jit(solution)/shard_map/pallas_call | solution.py:666
  316.1 2.9 collective-permute-start.34
  319.1 10.2 %collective-permute-done.37.refs_2_ = f32[3,6,48,128]{3,2,1,0:T(8,128)S(1)} collective-permute-done((f32[3,6,48,128]{3,2,1,0:T(8,128)}, f32[3,6,48,128]{3,2,1,0:T(8,128)S(1)}, u32[]{:S(2)}, u32[]{:S(2)}) %collective-permute-start.37) | collective-permute-done | bytes 442400 | tf_op jit(solution)/shard_map/ppermute | solution.py:689
  329.3 30.6 %collective-permute-done.38.refs_3_ = f32[3,6,48,128]{3,2,1,0:T(8,128)S(1)} collective-permute-done((f32[3,6,48,128]{3,2,1,0:T(8,128)}, f32[3,6,48,128]{3,2,1,0:T(8,128)S(1)}, u32[]{:S(2)}, u32[]{:S(2)}) %collective-permute-start.38) | collective-permute-done | bytes 442400 | tf_op jit(solution)/shard_map/ppermute | solution.py:689
  360.0 0.8 copy-done.10
  360.7 8.4 %shard_map.138.refs_4_ = f32[3,6,48,1024]{3,2,1,0:T(8,128)} custom-call(s32[3]{0:T(128)} %pad_add_fusion.ids_ref, f32[3,6,48,128]{3,2,1,0:T(8,128)} %get-tuple-element.111.refs_0_, f32[3,6,48,128]{3,2,1,0:T(8,128)} %copy-done.8, f32[3,6,48,128]{3,2,1,0:T(8,128)} %copy-done.9, f32[3,6,48,128]{3,2,1,0:T(8,128)} %copy-done.10, f32[3,6,48,1024]{3,2,1,0:T(8,128)} %refs_4_.2, ...), custom_call_target="tpu_custom_call" | custom-call | flops 2717908992 | bytes 7077888 | tf_op jit(solution)/shard_map/pallas_call | solution.py:699
  369.1 9.9 %collective-permute-done.35.refs_3_ = f32[3,6,48,128]{3,2,1,0:T(8,128)} collective-permute-done((f32[3,6,48,128]{3,2,1,0:T(8,128)}, f32[3,6,48,128]{3,2,1,0:T(8,128)}, u32[]{:S(2)}, u32[]{:S(2)}) %collective-permute-start.35) | collective-permute-done | bytes 442400 | tf_op jit(solution)/shard_map/ppermute | solution.py:689
  379.0 8.3 %shard_map.139 = f32[3,6,48,1024]{3,2,1,0:T(8,128)} custom-call(s32[3]{0:T(128)} %pad_add_fusion.ids_ref, f32[3,6,48,128]{3,2,1,0:T(8,128)} %get-tuple-element.107.refs_0_, f32[3,6,48,128]{3,2,1,0:T(8,128)} %copy-done.11, f32[3,6,48,128]{3,2,1,0:T(8,128)} %collective-permute-done.34.refs_2_, f32[3,6,48,128]{3,2,1,0:T(8,128)} %collective-permute-done.35.refs_3_, ...), custom_call_target="tpu_custom_call" | custom-call | flops 2717908992 | bytes 7077888 | tf_op jit(solution)/shard_map/pallas_call | solution.py:699
  (110 shorter events, 11.1 us)
Async XLA Ops:
  3.0 14.4 %collective-permute-start.1 = (f32[3,48,1024]{2,1,0:T(8,128)}, f32[3,48,1024]{2,1,0:T(8,128)S(1)}, u32[]{:S(2)}, u32[]{:S(2)}) collective-permute-start(f32[3,48,1024]{2,1,0:T(8,128)} %get-tuple-element.121), channel_id=1, source_target_pairs={{4,0},{8,4},{12,8},{16,12},{20,16},{24,20},{28,24},{0,28},{5,1},{9... | collective-permute-start | bytes 1769480 | tf_op jit(solution)/shard_map/ppermute | solution.py:495
  3.7 14.9 %collective-permute-start = (f32[3,48,1024]{2,1,0:T(8,128)}, f32[3,48,1024]{2,1,0:T(8,128)S(1)}, u32[]{:S(2)}, u32[]{:S(2)}) collective-permute-start(f32[3,48,1024]{2,1,0:T(8,128)} %get-tuple-element.122), channel_id=1, source_target_pairs={{0,4},{4,8},{8,12},{12,16},{16,20},{20,24},{24,28},{28,0},{1,5},{5... | collective-permute-start | bytes 1769480 | tf_op jit(solution)/shard_map/ppermute | solution.py:495
  15.4 17.3 %collective-permute-start.9 = (f32[3,48,1024]{2,1,0:T(8,128)}, f32[3,48,1024]{2,1,0:T(8,128)S(1)}, u32[]{:S(2)}, u32[]{:S(2)}) collective-permute-start(f32[3,48,1024]{2,1,0:T(8,128)} %get-tuple-element.117), channel_id=1, source_target_pairs={{4,0},{8,4},{12,8},{16,12},{20,16},{24,20},{28,24},{0,28},{5,1},{9... | collective-permute-start | bytes 1769480 | tf_op jit(solution)/shard_map/ppermute | solution.py:495
  15.4 19.6 %collective-permute-start.8 = (f32[3,48,1024]{2,1,0:T(8,128)}, f32[3,48,1024]{2,1,0:T(8,128)}, u32[]{:S(2)}, u32[]{:S(2)}) collective-permute-start(f32[3,48,1024]{2,1,0:T(8,128)} %get-tuple-element.118), channel_id=1, source_target_pairs={{0,4},{4,8},{8,12},{12,16},{16,20},{20,24},{24,28},{28,0},{1,5},{5... | collective-permute-start | bytes 1769480 | tf_op jit(solution)/shard_map/ppermute | solution.py:495
  17.2 87.4 %collective-permute-start.19 = (f32[1,2,6,48,128]{4,3,2,1,0:T(8,128)}, f32[1,2,6,48,128]{4,3,2,1,0:T(8,128)}, u32[]{:S(2)}, u32[]{:S(2)}) collective-permute-start(f32[1,2,6,48,128]{4,3,2,1,0:T(8,128)} %get-tuple-element.86), channel_id=1, source_target_pairs={{0,1},{1,0},{2,3},{3,2},{4,5},{5,4},{6,7},{7,6},{8,9},{9,8},{10,11... | collective-permute-start | bytes 884744 | tf_op jit(solution)/shard_map/ppermute | solution.py:566
  17.4 3.2 copy-start
  17.4 30.5 %collective-permute-start.5 = (f32[3,48,1024]{2,1,0:T(8,128)}, f32[3,48,1024]{2,1,0:T(8,128)}, u32[]{:S(2)}, u32[]{:S(2)}) collective-permute-start(f32[3,48,1024]{2,1,0:T(8,128)} %get-tuple-element.119), channel_id=1, source_target_pairs={{4,0},{8,4},{12,8},{16,12},{20,16},{24,20},{28,24},{0,28},{5,1},{9... | collective-permute-start | bytes 1769480 | tf_op jit(solution)/shard_map/ppermute | solution.py:495
  18.6 2.0 copy-start.1
  18.6 30.7 %collective-permute-start.4 = (f32[3,48,1024]{2,1,0:T(8,128)}, f32[3,48,1024]{2,1,0:T(8,128)}, u32[]{:S(2)}, u32[]{:S(2)}) collective-permute-start(f32[3,48,1024]{2,1,0:T(8,128)} %get-tuple-element.120), channel_id=1, source_target_pairs={{0,4},{4,8},{8,12},{12,16},{16,20},{20,24},{24,28},{28,0},{1,5},{5... | collective-permute-start | bytes 1769480 | tf_op jit(solution)/shard_map/ppermute | solution.py:495
  32.7 2.6 copy-start.4
  32.7 72.9 %collective-permute-start.20 = (f32[1,2,6,48,128]{4,3,2,1,0:T(8,128)}, f32[1,2,6,48,128]{4,3,2,1,0:T(8,128)S(1)}, u32[]{:S(2)}, u32[]{:S(2)}) collective-permute-start(f32[1,2,6,48,128]{4,3,2,1,0:T(8,128)} %get-tuple-element.87), channel_id=1, source_target_pairs={{0,2},{1,3},{2,0},{3,1},{4,6},{5,7},{6,4},{7,5},{8,10},{9,11},{10,... | collective-permute-start | bytes 884744 | tf_op jit(solution)/shard_map/ppermute | solution.py:565
  35.1 115.5 %collective-permute-start.2 = (f32[2,3,6,48,128]{4,3,2,1,0:T(8,128)}, f32[2,3,6,48,128]{4,3,2,1,0:T(8,128)}, u32[]{:S(2)}, u32[]{:S(2)}) collective-permute-start(f32[2,3,6,48,128]{4,3,2,1,0:T(8,128)} %get-tuple-element.61), channel_id=1, source_target_pairs={{0,1},{1,0},{2,3},{3,2},{4,5},{5,4},{6,7},{7,6},{8,9},{9,8},{10,11... | collective-permute-start | bytes 2654216 | tf_op jit(solution)/shard_map/ppermute | solution.py:609
  47.9 14.2 %copy-start.16 = (s32[3]{0:T(128)S(1)}, s32[3]{0:T(128)}, u32[]{:S(2)}) copy-start(s32[3]{0:T(128)} %pad_add_fusion.ids_ref) | copy-start | bytes 40
  47.9 72.9 %collective-permute-start.27 = (f32[2,3,6,48,128]{4,3,2,1,0:T(8,128)}, f32[2,3,6,48,128]{4,3,2,1,0:T(8,128)S(1)}, u32[]{:S(2)}, u32[]{:S(2)}) collective-permute-start(f32[2,3,6,48,128]{4,3,2,1,0:T(8,128)} %get-tuple-element.98), channel_id=1, source_target_pairs={{0,1},{1,0},{2,3},{3,2},{4,5},{5,4},{6,7},{7,6},{8,9},{9,8},{10,11... | collective-permute-start | bytes 2654216 | tf_op jit(solution)/shard_map/ppermute | solution.py:609
  78.4 48.3 %collective-permute-start.25 = (f32[2,3,6,48,128]{4,3,2,1,0:T(8,128)}, f32[2,3,6,48,128]{4,3,2,1,0:T(8,128)}, u32[]{:S(2)}, u32[]{:S(2)}) collective-permute-start(f32[2,3,6,48,128]{4,3,2,1,0:T(8,128)} %get-tuple-element.94), channel_id=1, source_target_pairs={{0,1},{1,0},{2,3},{3,2},{4,5},{5,4},{6,7},{7,6},{8,9},{9,8},{10,11... | collective-permute-start | bytes 2654216 | tf_op jit(solution)/shard_map/ppermute | solution.py:609
  89.4 15.2 %copy-start.24 = (f32[1,2,6,48,128]{4,3,2,1,0:T(8,128)S(1)}, f32[1,2,6,48,128]{4,3,2,1,0:T(8,128)}, u32[]{:S(2)}) copy-start(f32[1,2,6,48,128]{4,3,2,1,0:T(8,128)} %get-tuple-element.88) | copy-start | bytes 884740
  89.4 15.5 %copy-start.21 = (f32[192]{0:T(256)S(1)}, f32[192]{0:T(256)}, u32[]{:S(2)}) copy-start(f32[192]{0:T(256)} %constant.91) | copy-start | bytes 2308
  104.6 13.4 %collective-permute-start.21 = (f32[1,2,6,48,128]{4,3,2,1,0:T(8,128)S(1)}, f32[1,2,6,48,128]{4,3,2,1,0:T(8,128)S(1)}, u32[]{:S(2)}, u32[]{:S(2)}) collective-permute-start(f32[1,2,6,48,128]{4,3,2,1,0:T(8,128)S(1)} %copy-done.24), channel_id=1, source_target_pairs={{0,3},{1,2},{2,1},{3,0},{4,7},{5,6},{6,5},{7,4},{8,11},{9,10},{10,... | collective-permute-start | bytes 884744 | tf_op jit(solution)/shard_map/ppermute | solution.py:566
  105.6 40.1 %copy-start.23 = (f32[1,2,6,48,128]{4,3,2,1,0:T(8,128)}, f32[1,2,6,48,128]{4,3,2,1,0:T(8,128)S(1)}, u32[]{:S(2)}) copy-start(f32[1,2,6,48,128]{4,3,2,1,0:T(8,128)S(1)} %collective-permute-done.20.refs_2_) | copy-start | bytes 884740
  105.6 13.0 %collective-permute-start.22 = (f32[1,1,6,48,128]{4,3,2,1,0:T(8,128)}, f32[1,1,6,48,128]{4,3,2,1,0:T(8,128)S(1)}, u32[]{:S(2)}, u32[]{:S(2)}) collective-permute-start(f32[1,1,6,48,128]{4,3,2,1,0:T(8,128)} %get-tuple-element.90), channel_id=1, source_target_pairs={{0,1},{1,0},{2,3},{3,2},{4,5},{5,4},{6,7},{7,6},{8,9},{9,8},{10,11... | collective-permute-start | bytes 442376 | tf_op jit(solution)/shard_map/ppermute | solution.py:566
  118.0 2.9 copy-start.25
  118.0 110.4 %collective-permute-start.6 = (f32[2,3,6,48,128]{4,3,2,1,0:T(8,128)}, f32[2,3,6,48,128]{4,3,2,1,0:T(8,128)}, u32[]{:S(2)}, u32[]{:S(2)}) collective-permute-start(f32[2,3,6,48,128]{4,3,2,1,0:T(8,128)} %get-tuple-element.72), channel_id=1, source_target_pairs={{0,1},{1,0},{2,3},{3,2},{4,5},{5,4},{6,7},{7,6},{8,9},{9,8},{10,11... | collective-permute-start | bytes 2654216 | tf_op jit(solution)/shard_map/ppermute | solution.py:609
  118.7 8.1 %copy-start.26 = (f32[1,1,6,48,128]{4,3,2,1,0:T(8,128)}, f32[1,1,6,48,128]{4,3,2,1,0:T(8,128)S(1)}, u32[]{:S(2)}) copy-start(f32[1,1,6,48,128]{4,3,2,1,0:T(8,128)S(1)} %collective-permute-done.22.refs_5_) | copy-start | bytes 442372
  118.7 22.5 %collective-permute-start.23 = (f32[1,1,6,48,128]{4,3,2,1,0:T(8,128)}, f32[1,1,6,48,128]{4,3,2,1,0:T(8,128)S(1)}, u32[]{:S(2)}, u32[]{:S(2)}) collective-permute-start(f32[1,1,6,48,128]{4,3,2,1,0:T(8,128)} %get-tuple-element.91), channel_id=1, source_target_pairs={{0,2},{1,3},{2,0},{3,1},{4,6},{5,7},{6,4},{7,5},{8,10},{9,11},{10,... | collective-permute-start | bytes 442376 | tf_op jit(solution)/shard_map/ppermute | solution.py:565
  120.8 1.0 copy-start.22
  120.8 20.3 %collective-permute-start.24 = (f32[1,1,6,48,128]{4,3,2,1,0:T(8,128)}, f32[1,1,6,48,128]{4,3,2,1,0:T(8,128)S(1)}, u32[]{:S(2)}, u32[]{:S(2)}) collective-permute-start(f32[1,1,6,48,128]{4,3,2,1,0:T(8,128)} %get-tuple-element.92), channel_id=1, source_target_pairs={{0,3},{1,2},{2,1},{3,0},{4,7},{5,6},{6,5},{7,4},{8,11},{9,10},{10,... | collective-permute-start | bytes 442376 | tf_op jit(solution)/shard_map/ppermute | solution.py:566
  126.8 37.5 %collective-permute-start.16 = (f32[1,192,256]{2,1,0:T(8,128)S(1)}, f32[1,192,256]{2,1,0:T(8,128)S(1)}, u32[]{:S(2)}, u32[]{:S(2)}) collective-permute-start(f32[1,192,256]{2,1,0:T(8,128)S(1)} %get-tuple-element.123), channel_id=1, source_target_pairs={{4,0},{8,4},{12,8},{16,12},{20,16},{24,20},{28,24},{0,28},{5,1},{9... | collective-permute-start | bytes 589832 | tf_op jit(solution)/shard_map/ppermute | solution.py:495
  141.1 54.6 %collective-permute-start.28 = (f32[6,192,128]{2,1,0:T(8,128)}, f32[6,192,128]{2,1,0:T(8,128)S(1)}, u32[]{:S(2)}, u32[]{:S(2)}) collective-permute-start(f32[6,192,128]{2,1,0:T(8,128)} %get-tuple-element.100), channel_id=1, source_target_pairs={{0,2},{1,3},{2,0},{3,1},{4,6},{5,7},{6,4},{7,5},{8,10},{9,11},{10,... | collective-permute-start | bytes 1769480 | tf_op jit(solution)/shard_map/ppermute | solution.py:553
  142.5 75.4 %collective-permute-start.26 = (f32[6,192,128]{2,1,0:T(8,128)}, f32[6,192,128]{2,1,0:T(8,128)S(1)}, u32[]{:S(2)}, u32[]{:S(2)}) collective-permute-start(f32[6,192,128]{2,1,0:T(8,128)} %get-tuple-element.96), channel_id=1, source_target_pairs={{0,2},{1,3},{2,0},{3,1},{4,6},{5,7},{6,4},{7,5},{8,10},{9,11},{10,... | collective-permute-start | bytes 1769480 | tf_op jit(solution)/shard_map/ppermute | solution.py:553
  150.6 14.7 %collective-permute-start.15 = (f32[1,192,256]{2,1,0:T(8,128)}, f32[1,192,256]{2,1,0:T(8,128)}, u32[]{:S(2)}, u32[]{:S(2)}) collective-permute-start(f32[1,192,256]{2,1,0:T(8,128)} %get-tuple-element.124), channel_id=1, source_target_pairs={{0,4},{4,8},{8,12},{12,16},{16,20},{20,24},{24,28},{28,0},{1,5},{5... | collective-permute-start | bytes 589832 | tf_op jit(solution)/shard_map/ppermute | solution.py:495
  164.2 53.6 %copy-start.7 = (f32[1,192,256]{2,1,0:T(8,128)}, f32[1,192,256]{2,1,0:T(8,128)S(1)}, u32[]{:S(2)}) copy-start(f32[1,192,256]{2,1,0:T(8,128)S(1)} %collective-permute-done.16.refs_9_) | copy-start | bytes 589828
  164.2 72.6 %collective-permute-start.3 = (f32[6,192,128]{2,1,0:T(8,128)}, f32[6,192,128]{2,1,0:T(8,128)S(1)}, u32[]{:S(2)}, u32[]{:S(2)}) collective-permute-start(f32[6,192,128]{2,1,0:T(8,128)} %get-tuple-element.63), channel_id=1, source_target_pairs={{0,2},{1,3},{2,0},{3,1},{4,6},{5,7},{6,4},{7,5},{8,10},{9,11},{10,... | collective-permute-start | bytes 1769480 | tf_op jit(solution)/shard_map/ppermute | solution.py:553
  165.3 4.6 %collective-permute-start.30 = (f32[192,128]{1,0:T(8,128)S(1)}, f32[192,128]{1,0:T(8,128)S(1)}, u32[]{:S(2)}, u32[]{:S(2)}) collective-permute-start(f32[192,128]{1,0:T(8,128)S(1)} %get-tuple-element.127), channel_id=1, source_target_pairs={{4,0},{8,4},{12,8},{16,12},{20,16},{24,20},{28,24},{0,28},{5,1},{9... | collective-permute-start | bytes 294920 | tf_op jit(solution)/shard_map/ppermute | solution.py:495
  169.9 47.9 %copy-start.18 = (f32[192,128]{1,0:T(8,128)}, f32[192,128]{1,0:T(8,128)S(1)}, u32[]{:S(2)}) copy-start(f32[192,128]{1,0:T(8,128)S(1)} %collective-permute-done.30.refs_7_) | copy-start | bytes 294916
  169.9 1.6 collective-permute-start.29
  171.5 46.3 %copy-start.20 = (f32[192,128]{1,0:T(8,128)}, f32[192,128]{1,0:T(8,128)S(1)}, u32[]{:S(2)}) copy-start(f32[192,128]{1,0:T(8,128)S(1)} %collective-permute-done.29.refs_6_) | copy-start | bytes 294916
  171.5 89.2 %collective-permute-start.10 = (f32[1,3,6,48,128]{4,3,2,1,0:T(8,128)}, f32[1,3,6,48,128]{4,3,2,1,0:T(8,128)}, u32[]{:S(2)}, u32[]{:S(2)}) collective-permute-start(f32[1,3,6,48,128]{4,3,2,1,0:T(8,128)} %get-tuple-element.76), channel_id=1, source_target_pairs={{0,1},{1,0},{2,3},{3,2},{4,5},{5,4},{6,7},{7,6},{8,9},{9,8},{10,11... | collective-permute-start | bytes 1327112 | tf_op jit(solution)/shard_map/ppermute | solution.py:566
  195.7 22.1 %copy-start.5 = (f32[6,192,128]{2,1,0:T(8,128)}, f32[6,192,128]{2,1,0:T(8,128)S(1)}, u32[]{:S(2)}) copy-start(f32[6,192,128]{2,1,0:T(8,128)S(1)} %collective-permute-done.28.refs_4_.refs_13_) | copy-start | bytes 1769476
  195.7 66.4 %collective-permute-start.11 = (f32[1,3,6,48,128]{4,3,2,1,0:T(8,128)}, f32[1,3,6,48,128]{4,3,2,1,0:T(8,128)}, u32[]{:S(2)}, u32[]{:S(2)}) collective-permute-start(f32[1,3,6,48,128]{4,3,2,1,0:T(8,128)} %get-tuple-element.77), channel_id=1, source_target_pairs={{0,2},{1,3},{2,0},{3,1},{4,6},{5,7},{6,4},{7,5},{8,10},{9,11},{10,... | collective-permute-start | bytes 1327112 | tf_op jit(solution)/shard_map/ppermute | solution.py:565
  217.8 0.8 copy-start.6
  223.1 13.8 %collective-permute-start.31 = (f32[2,192,128]{2,1,0:T(8,128)}, f32[2,192,128]{2,1,0:T(8,128)S(1)}, u32[]{:S(2)}, u32[]{:S(2)}) collective-permute-start(f32[2,192,128]{2,1,0:T(8,128)} %get-tuple-element.103), channel_id=1, source_target_pairs={{0,4},{4,8},{8,12},{12,16},{16,20},{20,24},{24,28},{28,0},{1,5},{5... | collective-permute-start | bytes 589832 | tf_op jit(solution)/shard_map/ppermute | solution.py:495
  233.3 57.3 %collective-permute-start.7 = (f32[6,192,128]{2,1,0:T(8,128)}, f32[6,192,128]{2,1,0:T(8,128)S(1)}, u32[]{:S(2)}, u32[]{:S(2)}) collective-permute-start(f32[6,192,128]{2,1,0:T(8,128)} %get-tuple-element.74), channel_id=1, source_target_pairs={{0,2},{1,3},{2,0},{3,1},{4,6},{5,7},{6,4},{7,5},{8,10},{9,11},{10,... | collective-permute-start | bytes 1769480 | tf_op jit(solution)/shard_map/ppermute | solution.py:553
  236.8 23.9 %copy-start.2 = (f32[6,192,128]{2,1,0:T(8,128)}, f32[6,192,128]{2,1,0:T(8,128)S(1)}, u32[]{:S(2)}) copy-start(f32[6,192,128]{2,1,0:T(8,128)S(1)} %collective-permute-done.3.refs_1_.refs_10_) | copy-start | bytes 1769476
  236.8 48.9 %collective-permute-start.12 = (f32[1,3,6,48,128]{4,3,2,1,0:T(8,128)}, f32[1,3,6,48,128]{4,3,2,1,0:T(8,128)}, u32[]{:S(2)}, u32[]{:S(2)}) collective-permute-start(f32[1,3,6,48,128]{4,3,2,1,0:T(8,128)} %get-tuple-element.78), channel_id=1, source_target_pairs={{0,3},{1,2},{2,1},{3,0},{4,7},{5,6},{6,5},{7,4},{8,11},{9,10},{10,... | collective-permute-start | bytes 1327112 | tf_op jit(solution)/shard_map/ppermute | solution.py:566
  236.8 15.1 %copy-start.14 = (f32[2,192,128]{2,1,0:T(8,128)}, f32[2,192,128]{2,1,0:T(8,128)S(1)}, u32[]{:S(2)}) copy-start(f32[2,192,128]{2,1,0:T(8,128)S(1)} %collective-permute-done.31.refs_2_) | copy-start | bytes 589828
  236.9 15.1 %collective-permute-start.32 = (f32[2,192,128]{2,1,0:T(8,128)}, f32[2,192,128]{2,1,0:T(8,128)S(1)}, u32[]{:S(2)}, u32[]{:S(2)}) collective-permute-start(f32[2,192,128]{2,1,0:T(8,128)} %get-tuple-element.104), channel_id=1, source_target_pairs={{4,0},{8,4},{12,8},{16,12},{20,16},{24,20},{28,24},{0,28},{5,1},{9... | collective-permute-start | bytes 589832 | tf_op jit(solution)/shard_map/ppermute | solution.py:495
  251.9 0.7 copy-start.15
  251.9 38.6 %collective-permute-start.14 = (f32[192,128]{1,0:T(8,128)S(1)}, f32[192,128]{1,0:T(8,128)S(1)}, u32[]{:S(2)}, u32[]{:S(2)}) collective-permute-start(f32[192,128]{1,0:T(8,128)S(1)} %get-tuple-element.125), channel_id=1, source_target_pairs={{4,0},{8,4},{12,8},{16,12},{20,16},{24,20},{28,24},{0,28},{5,1},{9... | collective-permute-start | bytes 294920 | tf_op jit(solution)/shard_map/ppermute | solution.py:495
  260.7 29.9 %collective-permute-start.13 = (f32[192,128]{1,0:T(8,128)S(1)}, f32[192,128]{1,0:T(8,128)S(1)}, u32[]{:S(2)}, u32[]{:S(2)}) collective-permute-start(f32[192,128]{1,0:T(8,128)S(1)} %get-tuple-element.126), channel_id=1, source_target_pairs={{0,4},{4,8},{8,12},{12,16},{16,20},{20,24},{24,28},{28,0},{1,5},{5... | collective-permute-start | bytes 294920 | tf_op jit(solution)/shard_map/ppermute | solution.py:495
  262.1 57.0 %collective-permute-start.36 = (f32[3,6,48,128]{3,2,1,0:T(8,128)}, f32[3,6,48,128]{3,2,1,0:T(8,128)S(1)}, u32[]{:S(2)}, u32[]{:S(2)}) collective-permute-start(f32[3,6,48,128]{3,2,1,0:T(8,128)} %get-tuple-element.112), channel_id=1, source_target_pairs={{0,1},{1,0},{2,3},{3,2},{4,5},{5,4},{6,7},{7,6},{8,9},{9,8},{10,11... | collective-permute-start | bytes 1327112 | tf_op jit(solution)/shard_map/ppermute | solution.py:689
  290.5 0.8 copy-start.3
  290.6 0.8 copy-start.17
  290.6 0.9 copy-start.19
  295.9 9.1 %collective-permute-start.17 = (f32[2,192,128]{2,1,0:T(8,128)}, f32[2,192,128]{2,1,0:T(8,128)S(1)}, u32[]{:S(2)}, u32[]{:S(2)}) collective-permute-start(f32[2,192,128]{2,1,0:T(8,128)} %get-tuple-element.83), channel_id=1, source_target_pairs={{0,4},{4,8},{8,12},{12,16},{16,20},{20,24},{24,28},{28,0},{1,5},{5... | collective-permute-start | bytes 589832 | tf_op jit(solution)/shard_map/ppermute | solution.py:495
  300.0 5.6 %collective-permute-start.18 = (f32[2,192,128]{2,1,0:T(8,128)}, f32[2,192,128]{2,1,0:T(8,128)S(1)}, u32[]{:S(2)}, u32[]{:S(2)}) collective-permute-start(f32[2,192,128]{2,1,0:T(8,128)} %get-tuple-element.84), channel_id=1, source_target_pairs={{4,0},{8,4},{12,8},{16,12},{20,16},{24,20},{28,24},{0,28},{5,1},{9... | collective-permute-start | bytes 589832 | tf_op jit(solution)/shard_map/ppermute | solution.py:495
  300.0 29.3 %collective-permute-start.37 = (f32[3,6,48,128]{3,2,1,0:T(8,128)}, f32[3,6,48,128]{3,2,1,0:T(8,128)S(1)}, u32[]{:S(2)}, u32[]{:S(2)}) collective-permute-start(f32[3,6,48,128]{3,2,1,0:T(8,128)} %get-tuple-element.113), channel_id=1, source_target_pairs={{0,2},{1,3},{2,0},{3,1},{4,6},{5,7},{6,4},{7,5},{8,10},{9,11},{10,... | collective-permute-start | bytes 1327112 | tf_op jit(solution)/shard_map/ppermute | solution.py:689
  300.0 59.9 %collective-permute-start.38 = (f32[3,6,48,128]{3,2,1,0:T(8,128)}, f32[3,6,48,128]{3,2,1,0:T(8,128)S(1)}, u32[]{:S(2)}, u32[]{:S(2)}) collective-permute-start(f32[3,6,48,128]{3,2,1,0:T(8,128)} %get-tuple-element.114), channel_id=1, source_target_pairs={{0,3},{1,2},{2,1},{3,0},{4,7},{5,6},{6,5},{7,4},{8,11},{9,10},{10,... | collective-permute-start | bytes 1327112 | tf_op jit(solution)/shard_map/ppermute | solution.py:689
  316.1 53.0 %collective-permute-start.33 = (f32[3,6,48,128]{3,2,1,0:T(8,128)}, f32[3,6,48,128]{3,2,1,0:T(8,128)S(1)}, u32[]{:S(2)}, u32[]{:S(2)}) collective-permute-start(f32[3,6,48,128]{3,2,1,0:T(8,128)} %get-tuple-element.108), channel_id=1, source_target_pairs={{0,1},{1,0},{2,3},{3,2},{4,5},{5,4},{6,7},{7,6},{8,9},{9,8},{10,11... | collective-permute-start | bytes 1327112 | tf_op jit(solution)/shard_map/ppermute | solution.py:689
  316.1 53.0 %collective-permute-start.34 = (f32[3,6,48,128]{3,2,1,0:T(8,128)}, f32[3,6,48,128]{3,2,1,0:T(8,128)}, u32[]{:S(2)}, u32[]{:S(2)}) collective-permute-start(f32[3,6,48,128]{3,2,1,0:T(8,128)} %get-tuple-element.109), channel_id=1, source_target_pairs={{0,2},{1,3},{2,0},{3,1},{4,6},{5,7},{6,4},{7,5},{8,10},{9,11},{10,... | collective-permute-start | bytes 1327112 | tf_op jit(solution)/shard_map/ppermute | solution.py:689
  319.1 40.9 %copy-start.8 = (f32[3,6,48,128]{3,2,1,0:T(8,128)}, f32[3,6,48,128]{3,2,1,0:T(8,128)S(1)}, u32[]{:S(2)}) copy-start(f32[3,6,48,128]{3,2,1,0:T(8,128)S(1)} %collective-permute-done.36.refs_1_) | copy-start | bytes 1327108
  319.1 59.9 %collective-permute-start.35 = (f32[3,6,48,128]{3,2,1,0:T(8,128)}, f32[3,6,48,128]{3,2,1,0:T(8,128)}, u32[]{:S(2)}, u32[]{:S(2)}) collective-permute-start(f32[3,6,48,128]{3,2,1,0:T(8,128)} %get-tuple-element.110), channel_id=1, source_target_pairs={{0,3},{1,2},{2,1},{3,0},{4,7},{5,6},{6,5},{7,4},{8,11},{9,10},{10,... | collective-permute-start | bytes 1327112 | tf_op jit(solution)/shard_map/ppermute | solution.py:689
  329.3 30.6 %copy-start.9 = (f32[3,6,48,128]{3,2,1,0:T(8,128)}, f32[3,6,48,128]{3,2,1,0:T(8,128)S(1)}, u32[]{:S(2)}) copy-start(f32[3,6,48,128]{3,2,1,0:T(8,128)S(1)} %collective-permute-done.37.refs_2_) | copy-start | bytes 1327108
  359.9 0.8 copy-start.10
  369.1 9.9 %copy-start.11 = (f32[3,6,48,128]{3,2,1,0:T(8,128)}, f32[3,6,48,128]{3,2,1,0:T(8,128)S(1)}, u32[]{:S(2)}) copy-start(f32[3,6,48,128]{3,2,1,0:T(8,128)S(1)} %collective-permute-done.33.refs_1_) | copy-start | bytes 1327108
  (4 other events, 2.7 us)

commit v3 on v2

--- a/solution.py
+++ b/solution.py
@@ -446,7 +446,8 @@
     )
 
 
-DIRECT = ((0, 0), (2, 1))
+SPLIT = ((0, 0), (1, 0))
+DIRECT = ((0, 0), (1, 0), (2, 0))
 
 
 def section(vel, q_old, pressure_guess, shear_shift):
@@ -588,9 +589,12 @@
     later, us = lax.optimization_barrier((vel, us))
     for d in (1, 2):
         halos.append(exchange(later[d, :3], later[d, nx - 3 :]))
-    w = fields("moving", 0, 0, halos, direct=True)
-    arrays = spread_out(us) + spread_out(w)
-    tend[0][0] = z_direct(arrays, ((1, 0), (0, 1), (0, 0)))
+    still = {(0, 0): us}
+    for c, e in SPLIT:
+        us = still.get((c, e)) or fields("still", c, e, direct=True)
+        w = fields("moving", c, e, halos, direct=True)
+        arrays = spread_out(us) + spread_out(w)
+        tend[e][c] = z_direct(arrays, ((1, 0), (0, 1), (0, 0)))
     late = ids
     guess = pressure_guess
     for e in range(chunks):

time: 388 us -> 402 us (1.036)
  starting transfers between devices: 57.3 us -> 76.7 us
  waiting for transfers between devices: 151 us -> 141 us
    ppermute x3 -> x5, waiting for transfers between devices: 6.63 us -> 37.8 us  [spread_out(): got.append(lax.ppermute(keep_s, 'yz', same) if s else keep_s)]
    ppermute x16, waiting for transfers between devices: 22.1 us -> 4.55 us  [exchange(): return (lax.ppermute(last, 'gx', up), lax.ppermute(first, 'gx', down))]
    ppermute x4 -> x3, waiting for transfers between devices: 42.8 us -> 27.6 us  [z_part(): pieces.append(lax.ppermute(outs[s], 'yz', to))]
    ppermute x16, starting transfers between devices: 29.2 us -> 42 us  [exchange(): return (lax.ppermute(last, 'gx', up), lax.ppermute(first, 'gx', down))]
    ppermute x6 -> x10, waiting for transfers between devices: 28.6 us -> 19.4 us  [spread_out(): got.append(lax.ppermute(send_s, 'yz', other))]
    ppermute x6 -> x10, starting transfers between devices: 3.12 us -> 12.2 us  [spread_out(): got.append(lax.ppermute(send_s, 'yz', other))]
    pallas_call x2 -> x3, Pallas kernels: 9.66 us -> 14.5 us  [z_direct(): call(functools.partial(z_whole, layout=layout, pairs=pairs), 2 * az.size...]
    pallas_call x4 -> x3, Pallas kernels: 19.8 us -> 15.2 us  [z_part(): call(functools.partial(z_partial, layout=layout), 2 * az.size * nx * cw,...]
  transfers between devices with their start and end apart: 39 -> 43, of which waited for: 14 -> 14; matrix products, arithmetic and copies ran while one was open for 4% -> 4% of each run, Pallas kernels for 37% -> 37%
where the time goes in v3:
time: 402 us; the launch traced here: 399 us
  Pallas kernels  157 us (39%)
  waiting for transfers between devices  141 us (35%)
  starting transfers between devices  76.7 us (19%)
  local copies, waits for them, and re-layouts  12.6 us (3%)
  other arithmetic  8.59 us (2%)
    pallas_call x8, Pallas kernels, fields(): call(functools.partial(y_fields, c=c, e=e, kind=kind, slabs=slabs, chunks...  84.2 us
    ppermute x6, waiting for transfers between devices, section(): got.append(lax.ppermute(outs[2 + place], 'yz', to))  51.4 us
    ppermute x16, starting transfers between devices, exchange(): return (lax.ppermute(last, 'gx', up), lax.ppermute(first, 'gx', down))  42 us
    ppermute x5, waiting for transfers between devices, spread_out(): got.append(lax.ppermute(keep_s, 'yz', same) if s else keep_s)  37.8 us
    ppermute x3, waiting for transfers between devices, z_part(): pieces.append(lax.ppermute(outs[s], 'yz', to))  27.6 us
    ppermute x10, waiting for transfers between devices, spread_out(): got.append(lax.ppermute(send_s, 'yz', other))  19.4 us
    pallas_call x2, Pallas kernels, section(): call(functools.partial(finish, e=e, chunks=chunks, pieces=pieces, groups=...  17.6 us
    pallas_call x2, Pallas kernels, section(): call(functools.partial(y_inverse, terms=terms, groups=groups), 3 * y_flop...  16.8 us
  transfers between devices with their start and end apart: 43, of which 14 were waited for; matrix products, arithmetic and copies ran while one was open for 4% of the time, Pallas kernels for 37%

profile of v3, /device:TPU:13, one launch (start us, length us, event | category | flops | bytes accessed | tf_op | source)
XLA Modules:
  0.0 399.2 jit_solution(1246938003629157039)
XLA Ops:
  0.6 2.4 slice_bitcast_fusion.4
  3.7 1.1 collective-permute-start
  6.0 6.3 %shard_map.123 = (f32[1,2,6,48,128]{4,3,2,1,0:T(8,128)}, f32[1,2,6,48,128]{4,3,2,1,0:T(8,128)}, f32[1,2,6,48,128]{4,3,2,1,0:T(8,128)}, f32[1,2,6,48,128]{4,3,2,1,0:T(8,128)}) custom-call(s32[3]{0:T(128)} %pad_add_fusion.ids_ref, f32[3,6,48,1024]{3,2,1,0:T(8,128)} %refs_4_.2, f32[3,6,48,1024]{3,2,1,0:T(8,128)} %refs_4_.2, ...), custom_call_target="tpu_custom_call" | custom-call | flops 1811939328 | bytes 2359296 | tf_op jit(solution)/shard_map/pallas_call | solution.py:519
  12.3 3.1 slice_bitcast_fusion
  15.4 1.7 collective-permute-start.4
  17.1 6.2 %shard_map.131 = (f32[1,2,6,48,128]{4,3,2,1,0:T(8,128)}, f32[1,2,6,48,128]{4,3,2,1,0:T(8,128)}, f32[1,2,6,48,128]{4,3,2,1,0:T(8,128)}, f32[1,2,6,48,128]{4,3,2,1,0:T(8,128)}) custom-call(s32[3]{0:T(128)} %pad_add_fusion.ids_ref, f32[3,6,48,1024]{3,2,1,0:T(8,128)} %refs_4_.2, f32[3,6,48,1024]{3,2,1,0:T(8,128)} %refs_4_.2, ...), custom_call_target="tpu_custom_call" | custom-call | flops 1811939328 | bytes 2359296 | tf_op jit(solution)/shard_map/pallas_call | solution.py:519
  23.5 2.3 collective-permute-start.25
  26.1 3.5 collective-permute-done.5.refs_7_.refs_6_
  29.5 1.7 collective-permute-start.9
  31.2 1.5 collective-permute-start.8
  32.7 12.8 %shard_map.124 = (f32[2,3,6,48,128]{4,3,2,1,0:T(8,128)}, f32[2,3,6,48,128]{4,3,2,1,0:T(8,128)}) custom-call(s32[3]{0:T(128)} %pad_add_fusion.ids_ref, f32[3,6,48,1024]{3,2,1,0:T(8,128)} %refs_4_.2, f32[3,6,48,1024]{3,2,1,0:T(8,128)} %refs_4_.2, f32[3,6,48,1024]{3,2,1,0:T(8,128)} %refs_4_.2, f32[3,6,48,1024]{3,2,1,0:T(8,128)} %refs_4_.2, ...), custom_call_target="tpu_custom_call" | custom-call | flops 3623878656 | bytes 4718592 | tf_op jit(solution)/shard_map/pallas_call | solution.py:519
  46.8 10.2 %shard_map.129 = (f32[1,1,6,48,128]{4,3,2,1,0:T(8,128)}, f32[1,1,6,48,128]{4,3,2,1,0:T(8,128)}, f32[1,1,6,48,128]{4,3,2,1,0:T(8,128)}, f32[1,1,6,48,128]{4,3,2,1,0:T(8,128)}) custom-call(s32[3]{0:T(128)} %pad_add_fusion.ids_ref, f32[3,6,48,1024]{3,2,1,0:T(8,128)} %refs_4_.2, f32[3,6,48,1024]{3,2,1,0:T(8,128)} %refs_4_.2, f32[3,6,48,1024]{3,2,1,0:T(8,128)} %refs_4_.2, ...), custom_call_target="tpu_custom_call" | custom-call | flops 2717908992 | bytes 3538944 | tf_op jit(solution)/shard_map/pallas_call | solution.py:519
  57.0 11.1 %shard_map.132 = (f32[1,1,6,48,128]{4,3,2,1,0:T(8,128)}, f32[1,1,6,48,128]{4,3,2,1,0:T(8,128)}, f32[1,1,6,48,128]{4,3,2,1,0:T(8,128)}, f32[1,1,6,48,128]{4,3,2,1,0:T(8,128)}) custom-call(s32[3]{0:T(128)} %pad_add_fusion.ids_ref, f32[3,6,48,1024]{3,2,1,0:T(8,128)} %refs_4_.2, f32[3,6,48,1024]{3,2,1,0:T(8,128)} %refs_4_.2, f32[3,6,48,1024]{3,2,1,0:T(8,128)} %refs_4_.2, ...), custom_call_target="tpu_custom_call" | custom-call | flops 2717908992 | bytes 3538944 | tf_op jit(solution)/shard_map/pallas_call | solution.py:519
  68.1 12.0 %shard_map.121 = (f32[2,3,6,48,128]{4,3,2,1,0:T(8,128)}, f32[2,3,6,48,128]{4,3,2,1,0:T(8,128)}) custom-call(s32[3]{0:T(128)} %pad_add_fusion.ids_ref, f32[3,6,48,1024]{3,2,1,0:T(8,128)} %refs_4_.2, f32[3,6,48,1024]{3,2,1,0:T(8,128)} %refs_4_.2, f32[3,6,48,1024]{3,2,1,0:T(8,128)} %refs_4_.2, f32[3,6,48,1024]{3,2,1,0:T(8,128)} %refs_4_.2, ...), custom_call_target="tpu_custom_call" | custom-call | flops 3623878656 | bytes 4718592 | tf_op jit(solution)/shard_map/pallas_call | solution.py:519
  80.3 2.3 collective-permute-start.19
  82.6 13.0 %shard_map.134 = (f32[1,3,6,48,128]{4,3,2,1,0:T(8,128)}, f32[1,3,6,48,128]{4,3,2,1,0:T(8,128)}, f32[1,3,6,48,128]{4,3,2,1,0:T(8,128)}, f32[1,3,6,48,128]{4,3,2,1,0:T(8,128)}) custom-call(s32[3]{0:T(128)} %pad_add_fusion.ids_ref, f32[3,6,48,1024]{3,2,1,0:T(8,128)} %refs_4_.2, f32[3,6,48,1024]{3,2,1,0:T(8,128)} %refs_4_.2, f32[3,6,48,1024]{3,2,1,0:T(8,128)} %refs_4_.2, ...), custom_call_target="tpu_custom_call" | custom-call | flops 3623878656 | bytes 4718592 | tf_op jit(solution)/shard_map/pallas_call | solution.py:519
  95.6 12.7 %shard_map.126 = (f32[2,3,6,48,128]{4,3,2,1,0:T(8,128)}, f32[2,3,6,48,128]{4,3,2,1,0:T(8,128)}) custom-call(s32[3]{0:T(128)} %pad_add_fusion.ids_ref, f32[3,6,48,1024]{3,2,1,0:T(8,128)} %refs_4_.2, f32[3,6,48,1024]{3,2,1,0:T(8,128)} %refs_4_.2, f32[3,6,48,1024]{3,2,1,0:T(8,128)} %refs_4_.2, f32[3,6,48,1024]{3,2,1,0:T(8,128)} %refs_4_.2, ...), custom_call_target="tpu_custom_call" | custom-call | flops 3623878656 | bytes 4718592 | tf_op jit(solution)/shard_map/pallas_call | solution.py:519
  108.3 1.0 fusion.13
  109.8 1.1 collective-permute-start.21
  110.9 2.0 collective-permute-start.22
  112.9 0.8 add_divide_fusion
  114.6 1.3 collective-permute-start.27
  117.3 9.9 %collective-permute-done.20.refs_3_ = f32[1,2,6,48,128]{4,3,2,1,0:T(8,128)S(1)} collective-permute-done((f32[1,2,6,48,128]{4,3,2,1,0:T(8,128)}, f32[1,2,6,48,128]{4,3,2,1,0:T(8,128)S(1)}, u32[]{:S(2)}, u32[]{:S(2)}) %collective-permute-start.20) | collective-permute-done | bytes 294944 | tf_op jit(solution)/shard_map/ppermute | solution.py:567
  127.2 3.8 collective-permute-start.28
  131.0 1.0 collective-permute-done.22.refs_6_
  132.6 2.7 collective-permute-done.23.refs_7_
  135.3 4.7 %collective-permute-start.15 = (f32[1,192,256]{2,1,0:T(8,128)S(1)}, f32[1,192,256]{2,1,0:T(8,128)S(1)}, u32[]{:S(2)}, u32[]{:S(2)}) collective-permute-start(f32[1,192,256]{2,1,0:T(8,128)S(1)} %get-tuple-element.131), channel_id=1, source_target_pairs={{4,0},{8,4},{12,8},{16,12},{20,16},{24,20},{28,24},{0,28},{5,1},{9... | collective-permute-start | bytes 589832 | tf_op jit(solution)/shard_map/ppermute | solution.py:496
  140.7 11.7 %collective-permute-done.28.refs_6_ = f32[1,1,6,48,128]{4,3,2,1,0:T(8,128)S(1)} collective-permute-done((f32[1,1,6,48,128]{4,3,2,1,0:T(8,128)}, f32[1,1,6,48,128]{4,3,2,1,0:T(8,128)S(1)}, u32[]{:S(2)}, u32[]{:S(2)}) %collective-permute-start.28) | collective-permute-done | bytes 147488 | tf_op jit(solution)/shard_map/ppermute | solution.py:566
  152.4 4.6 %collective-permute-start.14 = (f32[1,192,256]{2,1,0:T(8,128)S(1)}, f32[1,192,256]{2,1,0:T(8,128)S(1)}, u32[]{:S(2)}, u32[]{:S(2)}) collective-permute-start(f32[1,192,256]{2,1,0:T(8,128)S(1)} %get-tuple-element.132), channel_id=1, source_target_pairs={{0,4},{4,8},{8,12},{12,16},{16,20},{20,24},{24,28},{28,0},{1,5},{5... | collective-permute-start | bytes 589832 | tf_op jit(solution)/shard_map/ppermute | solution.py:496
  157.8 1.5 collective-permute-start.10
  161.2 6.8 %collective-permute-done.30.refs_1_ = f32[1,3,6,48,128]{4,3,2,1,0:T(8,128)S(1)} collective-permute-done((f32[1,3,6,48,128]{4,3,2,1,0:T(8,128)S(1)}, f32[1,3,6,48,128]{4,3,2,1,0:T(8,128)S(1)}, u32[]{:S(2)}, u32[]{:S(2)}) %collective-permute-start.30) | collective-permute-done | bytes 442400 | tf_op jit(solution)/shard_map/ppermute | solution.py:567
  168.7 8.4 %collective-permute-start.32 = (f32[1,3,6,48,128]{4,3,2,1,0:T(8,128)}, f32[1,3,6,48,128]{4,3,2,1,0:T(8,128)}, u32[]{:S(2)}, u32[]{:S(2)}) collective-permute-start(f32[1,3,6,48,128]{4,3,2,1,0:T(8,128)} %get-tuple-element.108), channel_id=1, source_target_pairs={{0,3},{1,2},{2,1},{3,0},{4,7},{5,6},{6,5},{7,4},{8,11},{9,10},{10,... | collective-permute-start | bytes 1327112 | tf_op jit(solution)/shard_map/ppermute | solution.py:567
  177.1 4.8 %shard_map.130.refs_0_.refs_9_ = f32[6,192,128]{2,1,0:T(8,128)} custom-call(s32[3]{0:T(128)} %pad_add_fusion.ids_ref, f32[1,2,6,48,128]{4,3,2,1,0:T(8,128)} %get-tuple-element.89.refs_0_, f32[1,2,6,48,128]{4,3,2,1,0:T(8,128)} %copy-done.24, f32[1,2,6,48,128]{4,3,2,1,0:T(8,128)} %collective-permute-done.19.refs_2_, f32[1,2,6,48,128]{4,3,2,1,0:T(8,128)} %copy-done.25, ...), custom_call_target="tpu_custom_call" | custom-call | flops 1019215872 | bytes 2949120 | tf_op jit(solution)/shard_map/pallas_call | solution.py:572
  181.9 4.8 %shard_map.133.refs_1_.refs_10_ = f32[6,192,128]{2,1,0:T(8,128)} custom-call(s32[3]{0:T(128)} %pad_add_fusion.ids_ref, f32[1,2,6,48,128]{4,3,2,1,0:T(8,128)} %get-tuple-element.97.refs_0_, f32[1,2,6,48,128]{4,3,2,1,0:T(8,128)} %collective-permute-done.24.refs_1_, f32[1,2,6,48,128]{4,3,2,1,0:T(8,128)} %collective-permute-done.25.refs_2_, ...), custom_call_target="tpu_custom_call" | custom-call | flops 1019215872 | bytes 2949120 | tf_op jit(solution)/shard_map/pallas_call | solution.py:572
  186.8 1.0 slice_bitcast_fusion.6
  187.7 25.1 %collective-permute-done.31.refs_2_ = f32[1,3,6,48,128]{4,3,2,1,0:T(8,128)} collective-permute-done((f32[1,3,6,48,128]{4,3,2,1,0:T(8,128)}, f32[1,3,6,48,128]{4,3,2,1,0:T(8,128)}, u32[]{:S(2)}, u32[]{:S(2)}) %collective-permute-start.31) | collective-permute-done | bytes 442400 | tf_op jit(solution)/shard_map/ppermute | solution.py:566
  212.9 5.8 %collective-permute-start.34 = (f32[192,128]{1,0:T(8,128)S(1)}, f32[192,128]{1,0:T(8,128)S(1)}, u32[]{:S(2)}, u32[]{:S(2)}) collective-permute-start(f32[192,128]{1,0:T(8,128)S(1)} %get-tuple-element.135), channel_id=1, source_target_pairs={{4,0},{8,4},{12,8},{16,12},{20,16},{24,20},{28,24},{0,28},{5,1},{9... | collective-permute-start | bytes 294920 | tf_op jit(solution)/shard_map/ppermute | solution.py:496
  218.6 5.0 %shard_map.122 = (f32[6,192,128]{2,1,0:T(8,128)}, f32[6,192,128]{2,1,0:T(8,128)}) custom-call(s32[3]{0:T(128)} %pad_add_fusion.ids_ref, f32[2,3,6,48,128]{4,3,2,1,0:T(8,128)} %get-tuple-element.64.refs_0_, f32[2,3,6,48,128]{4,3,2,1,0:T(8,128)} %collective-permute-done.2.refs_1_, bf16[2,384,864]{2,1,0:T(8,128)(2,1)} %constant.83.clone.refs_2_.refs_8_.refs_4_), custom_call_target="tpu_custom_call" | custom-call | flops 1019215872 | bytes 2949120 | tf_op jit(solution)/shard_map/pallas_call | solution.py:537
  223.7 4.9 %shard_map.135.refs_2_.refs_11_ = f32[6,192,128]{2,1,0:T(8,128)} custom-call(s32[3]{0:T(128)} %pad_add_fusion.ids_ref, f32[1,3,6,48,128]{4,3,2,1,0:T(8,128)} %get-tuple-element.105.refs_0_, f32[1,3,6,48,128]{4,3,2,1,0:T(8,128)} %copy-done.23, f32[1,3,6,48,128]{4,3,2,1,0:T(8,128)} %collective-permute-done.31.refs_2_, ...), custom_call_target="tpu_custom_call" | custom-call | flops 1019215872 | bytes 2949120 | tf_op jit(solution)/shard_map/pallas_call | solution.py:572
  229.3 4.1 %shard_map.136 = (f32[6,192,128]{2,1,0:T(8,128)}, f32[6,192,128]{2,1,0:T(8,128)}, f32[2,192,128]{2,1,0:T(8,128)}, f32[2,192,128]{2,1,0:T(8,128)}) custom-call(f32[6,192,128]{2,1,0:T(8,128)} %shard_map.130.refs_0_.refs_9_, f32[6,192,128]{2,1,0:T(8,128)} %shard_map.133.refs_1_.refs_10_, f32[6,192,128]{2,1,0:T(8,128)} %shard_map.135.refs_2_.refs_11_, ...), custom_call_target="tpu_custom_call" | custom-call | flops 294912000 | bytes 2359296 | tf_op jit(solution)/shard_map/pallas_call | solution.py:659
  233.4 5.0 %collective-permute-start.35 = (f32[2,192,128]{2,1,0:T(8,128)}, f32[2,192,128]{2,1,0:T(8,128)S(1)}, u32[]{:S(2)}, u32[]{:S(2)}) collective-permute-start(f32[2,192,128]{2,1,0:T(8,128)} %get-tuple-element.111), channel_id=1, source_target_pairs={{0,4},{4,8},{8,12},{12,16},{16,20},{20,24},{24,28},{28,0},{1,5},{5... | collective-permute-start | bytes 589832 | tf_op jit(solution)/shard_map/ppermute | solution.py:496
  238.3 5.2 %shard_map.125 = (f32[6,192,128]{2,1,0:T(8,128)}, f32[6,192,128]{2,1,0:T(8,128)}) custom-call(s32[3]{0:T(128)} %pad_add_fusion.ids_ref, f32[2,3,6,48,128]{4,3,2,1,0:T(8,128)} %get-tuple-element.75.refs_0_, f32[2,3,6,48,128]{4,3,2,1,0:T(8,128)} %collective-permute-done.6.refs_1_, bf16[2,384,864]{2,1,0:T(8,128)(2,1)} %constant.83.clone.refs_2_.refs_8_.refs_4_), custom_call_target="tpu_custom_call" | custom-call | flops 1019215872 | bytes 2949120 | tf_op jit(solution)/shard_map/pallas_call | solution.py:537
  243.6 5.0 %shard_map.127 = (f32[6,192,128]{2,1,0:T(8,128)}, f32[6,192,128]{2,1,0:T(8,128)}) custom-call(s32[3]{0:T(128)} %pad_add_fusion.ids_ref, f32[2,3,6,48,128]{4,3,2,1,0:T(8,128)} %get-tuple-element.79.refs_0_, f32[2,3,6,48,128]{4,3,2,1,0:T(8,128)} %collective-permute-done.10.refs_1_, bf16[2,384,864]{2,1,0:T(8,128)(2,1)} %constant.83.clone.refs_2_.refs_8_.refs_4_), custom_call_target="tpu_custom_call" | custom-call | flops 1019215872 | bytes 2949120 | tf_op jit(solution)/shard_map/pallas_call | solution.py:537
  248.5 2.3 collective-permute-start.11
  252.7 7.7 %shard_map.137 = (f32[3,6,192,128]{3,2,1,0:T(8,128)}, f32[6,192,128]{2,1,0:T(8,128)}, f32[3,6,48,128]{3,2,1,0:T(8,128)}, f32[3,6,48,128]{3,2,1,0:T(8,128)}, f32[...) custom-call(s32[3]{0:T(128)} %pad_add_fusion.ids_ref, f32[6,192,128]{2,1,0:T(8,128)} %get-tuple-element.109.refs_0_, ...), custom_call_target="tpu_custom_call" | custom-call | flops 1019215872 | bytes 3538944 | tf_op jit(solution)/shard_map/pallas_call | solution.py:670
  260.5 11.0 %collective-permute-done.3.refs_1_.refs_10_ = f32[6,192,128]{2,1,0:T(8,128)S(1)} collective-permute-done((f32[6,192,128]{2,1,0:T(8,128)}, f32[6,192,128]{2,1,0:T(8,128)S(1)}, u32[]{:S(2)}, u32[]{:S(2)}) %collective-permute-start.3) | collective-permute-done | bytes 589856 | tf_op jit(solution)/shard_map/ppermute | solution.py:554
  271.5 1.2 fusion
  272.6 6.4 %collective-permute-start.13 = (f32[192,128]{1,0:T(8,128)S(1)}, f32[192,128]{1,0:T(8,128)S(1)}, u32[]{:S(2)}, u32[]{:S(2)}) collective-permute-start(f32[192,128]{1,0:T(8,128)S(1)} %get-tuple-element.133), channel_id=1, source_target_pairs={{4,0},{8,4},{12,8},{16,12},{20,16},{24,20},{28,24},{0,28},{5,1},{9... | collective-permute-start | bytes 294920 | tf_op jit(solution)/shard_map/ppermute | solution.py:496
  279.0 2.0 collective-permute-start.12
  281.5 3.9 collective-permute-done.7.refs_3_.refs_12_
  285.4 12.6 %collective-permute-done.11.refs_5_.refs_14_ = f32[6,192,128]{2,1,0:T(8,128)S(1)} collective-permute-done((f32[6,192,128]{2,1,0:T(8,128)}, f32[6,192,128]{2,1,0:T(8,128)S(1)}, u32[]{:S(2)}, u32[]{:S(2)}) %collective-permute-start.11) | collective-permute-done | bytes 589856 | tf_op jit(solution)/shard_map/ppermute | solution.py:554
  298.1 0.8 copy-done.5
  299.0 4.6 %shard_map.128 = (f32[6,192,128]{2,1,0:T(8,128)}, f32[6,192,128]{2,1,0:T(8,128)}, f32[2,192,128]{2,1,0:T(8,128)}, f32[2,192,128]{2,1,0:T(8,128)}) custom-call(f32[6,192,128]{2,1,0:T(8,128)} %get-tuple-element.66.refs_0_.refs_9_, f32[6,192,128]{2,1,0:T(8,128)} %copy-done.2, f32[6,192,128]{2,1,0:T(8,128)} %get-tuple-element.77.refs_2_.refs_11_, ...), custom_call_target="tpu_custom_call" | custom-call | flops 294912000 | bytes 2359296 | tf_op jit(solution)/shard_map/pallas_call | solution.py:659
  303.6 6.9 %collective-permute-start.16 = (f32[2,192,128]{2,1,0:T(8,128)}, f32[2,192,128]{2,1,0:T(8,128)S(1)}, u32[]{:S(2)}, u32[]{:S(2)}) collective-permute-start(f32[2,192,128]{2,1,0:T(8,128)} %get-tuple-element.87), channel_id=1, source_target_pairs={{0,4},{4,8},{8,12},{12,16},{16,20},{20,24},{24,28},{28,0},{1,5},{5... | collective-permute-start | bytes 589832 | tf_op jit(solution)/shard_map/ppermute | solution.py:496
  310.5 3.0 collective-permute-start.41
  314.7 1.1 collective-permute-done.17.refs_3_
  316.5 9.9 %shard_map.138 = (f32[3,6,192,256]{3,2,1,0:T(8,128)}, f32[6,192,256]{2,1,0:T(8,128)}, f32[3,6,48,128]{3,2,1,0:T(8,128)}, f32[3,6,48,128]{3,2,1,0:T(8,128)}, f32[...) custom-call(s32[3]{0:T(128)} %pad_add_fusion.ids_ref, f32[6,192,128]{2,1,0:T(8,128)} %get-tuple-element.85.refs_0_, ...), custom_call_target="tpu_custom_call" | custom-call | flops 1019215872 | bytes 3538944 | tf_op jit(solution)/shard_map/pallas_call | solution.py:670
  326.3 2.6 collective-permute-start.37
  330.2 12.5 %collective-permute-done.41.refs_2_ = f32[3,6,48,128]{3,2,1,0:T(8,128)S(1)} collective-permute-done((f32[3,6,48,128]{3,2,1,0:T(8,128)}, f32[3,6,48,128]{3,2,1,0:T(8,128)S(1)}, u32[]{:S(2)}, u32[]{:S(2)}) %collective-permute-start.41) | collective-permute-done | bytes 442400 | tf_op jit(solution)/shard_map/ppermute | solution.py:693
  342.7 29.0 %collective-permute-done.42.refs_3_ = f32[3,6,48,128]{3,2,1,0:T(8,128)S(1)} collective-permute-done((f32[3,6,48,128]{3,2,1,0:T(8,128)}, f32[3,6,48,128]{3,2,1,0:T(8,128)S(1)}, u32[]{:S(2)}, u32[]{:S(2)}) %collective-permute-start.42) | collective-permute-done | bytes 442400 | tf_op jit(solution)/shard_map/ppermute | solution.py:693
  371.8 0.8 copy-done.9
  372.5 8.4 %shard_map.139.refs_4_ = f32[3,6,48,1024]{3,2,1,0:T(8,128)} custom-call(s32[3]{0:T(128)} %pad_add_fusion.ids_ref, f32[3,6,48,128]{3,2,1,0:T(8,128)} %get-tuple-element.119.refs_0_, f32[3,6,48,128]{3,2,1,0:T(8,128)} %collective-permute-done.40.refs_1_, f32[3,6,48,128]{3,2,1,0:T(8,128)} %copy-done.8, f32[3,6,48,128]{3,2,1,0:T(8,128)} %copy-done.9, ...), custom_call_target="tpu_custom_call" | custom-call | flops 2717908992 | bytes 7077888 | tf_op jit(solution)/shard_map/pallas_call | solution.py:703
  381.0 9.9 %collective-permute-done.39.refs_3_ = f32[3,6,48,128]{3,2,1,0:T(8,128)} collective-permute-done((f32[3,6,48,128]{3,2,1,0:T(8,128)}, f32[3,6,48,128]{3,2,1,0:T(8,128)}, u32[]{:S(2)}, u32[]{:S(2)}) %collective-permute-start.39) | collective-permute-done | bytes 442400 | tf_op jit(solution)/shard_map/ppermute | solution.py:693
  390.8 8.3 %shard_map.140 = f32[3,6,48,1024]{3,2,1,0:T(8,128)} custom-call(s32[3]{0:T(128)} %pad_add_fusion.ids_ref, f32[3,6,48,128]{3,2,1,0:T(8,128)} %get-tuple-element.115.refs_0_, f32[3,6,48,128]{3,2,1,0:T(8,128)} %copy-done.10, f32[3,6,48,128]{3,2,1,0:T(8,128)} %copy-done.11, f32[3,6,48,128]{3,2,1,0:T(8,128)} %collective-permute-done.39.refs_3_, ...), custom_call_target="tpu_custom_call" | custom-call | flops 2717908992 | bytes 7077888 | tf_op jit(solution)/shard_map/pallas_call | solution.py:703
  (127 shorter events, 15.2 us)
Async XLA Ops:
  3.0 20.5 %collective-permute-start.1 = (f32[3,48,1024]{2,1,0:T(8,128)}, f32[3,48,1024]{2,1,0:T(8,128)S(1)}, u32[]{:S(2)}, u32[]{:S(2)}) collective-permute-start(f32[3,48,1024]{2,1,0:T(8,128)} %get-tuple-element.129), channel_id=1, source_target_pairs={{4,0},{8,4},{12,8},{16,12},{20,16},{24,20},{28,24},{0,28},{5,1},{9... | collective-permute-start | bytes 1769480 | tf_op jit(solution)/shard_map/ppermute | solution.py:496
  3.7 22.2 %collective-permute-start = (f32[3,48,1024]{2,1,0:T(8,128)}, f32[3,48,1024]{2,1,0:T(8,128)S(1)}, u32[]{:S(2)}, u32[]{:S(2)}) collective-permute-start(f32[3,48,1024]{2,1,0:T(8,128)} %get-tuple-element.130), channel_id=1, source_target_pairs={{0,4},{4,8},{8,12},{12,16},{16,20},{20,24},{24,28},{28,0},{1,5},{5... | collective-permute-start | bytes 1769480 | tf_op jit(solution)/shard_map/ppermute | solution.py:496
  15.4 14.1 %collective-permute-start.5 = (f32[3,48,1024]{2,1,0:T(8,128)}, f32[3,48,1024]{2,1,0:T(8,128)S(1)}, u32[]{:S(2)}, u32[]{:S(2)}) collective-permute-start(f32[3,48,1024]{2,1,0:T(8,128)} %get-tuple-element.127), channel_id=1, source_target_pairs={{4,0},{8,4},{12,8},{16,12},{20,16},{24,20},{28,24},{0,28},{5,1},{9... | collective-permute-start | bytes 1769480 | tf_op jit(solution)/shard_map/ppermute | solution.py:496
  15.4 15.9 %collective-permute-start.4 = (f32[3,48,1024]{2,1,0:T(8,128)}, f32[3,48,1024]{2,1,0:T(8,128)}, u32[]{:S(2)}, u32[]{:S(2)}) collective-permute-start(f32[3,48,1024]{2,1,0:T(8,128)} %get-tuple-element.128), channel_id=1, source_target_pairs={{0,4},{4,8},{8,12},{12,16},{16,20},{20,24},{24,28},{28,0},{1,5},{5... | collective-permute-start | bytes 1769480 | tf_op jit(solution)/shard_map/ppermute | solution.py:496
  23.4 86.0 %collective-permute-start.24 = (f32[1,2,6,48,128]{4,3,2,1,0:T(8,128)}, f32[1,2,6,48,128]{4,3,2,1,0:T(8,128)}, u32[]{:S(2)}, u32[]{:S(2)}) collective-permute-start(f32[1,2,6,48,128]{4,3,2,1,0:T(8,128)} %get-tuple-element.98), channel_id=1, source_target_pairs={{0,1},{1,0},{2,3},{3,2},{4,5},{5,4},{6,7},{7,6},{8,9},{9,8},{10,11... | collective-permute-start | bytes 884744 | tf_op jit(solution)/shard_map/ppermute | solution.py:567
  23.5 9.2 %copy-start = (f32[3,48,1024]{2,1,0:T(8,128)}, f32[3,48,1024]{2,1,0:T(8,128)S(1)}, u32[]{:S(2)}) copy-start(f32[3,48,1024]{2,1,0:T(8,128)S(1)} %collective-permute-done.1.refs_6_.refs_7_.refs_5_) | copy-start | bytes 1769476
  23.5 86.3 %collective-permute-start.25 = (f32[1,2,6,48,128]{4,3,2,1,0:T(8,128)}, f32[1,2,6,48,128]{4,3,2,1,0:T(8,128)}, u32[]{:S(2)}, u32[]{:S(2)}) collective-permute-start(f32[1,2,6,48,128]{4,3,2,1,0:T(8,128)} %get-tuple-element.99), channel_id=1, source_target_pairs={{0,2},{1,3},{2,0},{3,1},{4,6},{5,7},{6,4},{7,5},{8,10},{9,11},{10,... | collective-permute-start | bytes 884744 | tf_op jit(solution)/shard_map/ppermute | solution.py:566
  25.9 6.9 %copy-start.1 = (f32[3,48,1024]{2,1,0:T(8,128)}, f32[3,48,1024]{2,1,0:T(8,128)S(1)}, u32[]{:S(2)}) copy-start(f32[3,48,1024]{2,1,0:T(8,128)S(1)} %collective-permute-done.refs_4_.refs_5_.refs_3_) | copy-start | bytes 1769476
  25.9 85.0 %collective-permute-start.26 = (f32[1,2,6,48,128]{4,3,2,1,0:T(8,128)}, f32[1,2,6,48,128]{4,3,2,1,0:T(8,128)}, u32[]{:S(2)}, u32[]{:S(2)}) collective-permute-start(f32[1,2,6,48,128]{4,3,2,1,0:T(8,128)} %get-tuple-element.100), channel_id=1, source_target_pairs={{0,3},{1,2},{2,1},{3,0},{4,7},{5,6},{6,5},{7,4},{8,11},{9,10},{10,... | collective-permute-start | bytes 884744 | tf_op jit(solution)/shard_map/ppermute | solution.py:567
  29.5 50.5 %collective-permute-start.9 = (f32[3,48,1024]{2,1,0:T(8,128)}, f32[3,48,1024]{2,1,0:T(8,128)}, u32[]{:S(2)}, u32[]{:S(2)}) collective-permute-start(f32[3,48,1024]{2,1,0:T(8,128)} %get-tuple-element.125), channel_id=1, source_target_pairs={{4,0},{8,4},{12,8},{16,12},{20,16},{24,20},{28,24},{0,28},{5,1},{9... | collective-permute-start | bytes 1769480 | tf_op jit(solution)/shard_map/ppermute | solution.py:496
  31.2 14.3 %copy-start.15 = (s32[3]{0:T(128)S(1)}, s32[3]{0:T(128)}, u32[]{:S(2)}) copy-start(s32[3]{0:T(128)} %pad_add_fusion.ids_ref) | copy-start | bytes 40
  31.2 49.1 %collective-permute-start.8 = (f32[3,48,1024]{2,1,0:T(8,128)}, f32[3,48,1024]{2,1,0:T(8,128)}, u32[]{:S(2)}, u32[]{:S(2)}) collective-permute-start(f32[3,48,1024]{2,1,0:T(8,128)} %get-tuple-element.126), channel_id=1, source_target_pairs={{0,4},{4,8},{8,12},{12,16},{16,20},{20,24},{24,28},{28,0},{1,5},{5... | collective-permute-start | bytes 1769480 | tf_op jit(solution)/shard_map/ppermute | solution.py:496
  80.0 34.3 %collective-permute-start.18 = (f32[1,2,6,48,128]{4,3,2,1,0:T(8,128)}, f32[1,2,6,48,128]{4,3,2,1,0:T(8,128)S(1)}, u32[]{:S(2)}, u32[]{:S(2)}) collective-permute-start(f32[1,2,6,48,128]{4,3,2,1,0:T(8,128)} %get-tuple-element.90), channel_id=1, source_target_pairs={{0,1},{1,0},{2,3},{3,2},{4,5},{5,4},{6,7},{7,6},{8,9},{9,8},{10,11... | collective-permute-start | bytes 884744 | tf_op jit(solution)/shard_map/ppermute | solution.py:567
  80.3 34.3 %collective-permute-start.19 = (f32[1,2,6,48,128]{4,3,2,1,0:T(8,128)}, f32[1,2,6,48,128]{4,3,2,1,0:T(8,128)}, u32[]{:S(2)}, u32[]{:S(2)}) collective-permute-start(f32[1,2,6,48,128]{4,3,2,1,0:T(8,128)} %get-tuple-element.91), channel_id=1, source_target_pairs={{0,2},{1,3},{2,0},{3,1},{4,6},{5,7},{6,4},{7,5},{8,10},{9,11},{10,... | collective-permute-start | bytes 884744 | tf_op jit(solution)/shard_map/ppermute | solution.py:566
  95.6 17.3 %copy-start.20 = (f32[192]{0:T(256)S(1)}, f32[192]{0:T(256)}, u32[]{:S(2)}) copy-start(f32[192]{0:T(256)} %constant.91) | copy-start | bytes 2308
  95.6 31.6 %copy-start.21 = (f32[2,3,6,48,128]{4,3,2,1,0:T(8,128)S(1)}, f32[2,3,6,48,128]{4,3,2,1,0:T(8,128)}, u32[]{:S(2)}) copy-start(f32[2,3,6,48,128]{4,3,2,1,0:T(8,128)} %get-tuple-element.65) | copy-start | bytes 2654212
  95.6 36.3 %copy-start.26 = (f32[1,1,6,48,128]{4,3,2,1,0:T(8,128)S(1)}, f32[1,1,6,48,128]{4,3,2,1,0:T(8,128)}, u32[]{:S(2)}) copy-start(f32[1,1,6,48,128]{4,3,2,1,0:T(8,128)} %get-tuple-element.104) | copy-start | bytes 442372
  95.6 44.5 %copy-start.22 = (f32[1,3,6,48,128]{4,3,2,1,0:T(8,128)S(1)}, f32[1,3,6,48,128]{4,3,2,1,0:T(8,128)}, u32[]{:S(2)}) copy-start(f32[1,3,6,48,128]{4,3,2,1,0:T(8,128)} %get-tuple-element.106) | copy-start | bytes 1327108
  109.4 17.8 %collective-permute-start.20 = (f32[1,2,6,48,128]{4,3,2,1,0:T(8,128)}, f32[1,2,6,48,128]{4,3,2,1,0:T(8,128)S(1)}, u32[]{:S(2)}, u32[]{:S(2)}) collective-permute-start(f32[1,2,6,48,128]{4,3,2,1,0:T(8,128)} %get-tuple-element.92), channel_id=1, source_target_pairs={{0,3},{1,2},{2,1},{3,0},{4,7},{5,6},{6,5},{7,4},{8,11},{9,10},{10,... | collective-permute-start | bytes 884744 | tf_op jit(solution)/shard_map/ppermute | solution.py:567
  109.8 17.4 %collective-permute-start.21 = (f32[1,1,6,48,128]{4,3,2,1,0:T(8,128)}, f32[1,1,6,48,128]{4,3,2,1,0:T(8,128)S(1)}, u32[]{:S(2)}, u32[]{:S(2)}) collective-permute-start(f32[1,1,6,48,128]{4,3,2,1,0:T(8,128)} %get-tuple-element.94), channel_id=1, source_target_pairs={{0,1},{1,0},{2,3},{3,2},{4,5},{5,4},{6,7},{7,6},{8,9},{9,8},{10,11... | collective-permute-start | bytes 442376 | tf_op jit(solution)/shard_map/ppermute | solution.py:567
  110.9 21.0 %collective-permute-start.22 = (f32[1,1,6,48,128]{4,3,2,1,0:T(8,128)}, f32[1,1,6,48,128]{4,3,2,1,0:T(8,128)S(1)}, u32[]{:S(2)}, u32[]{:S(2)}) collective-permute-start(f32[1,1,6,48,128]{4,3,2,1,0:T(8,128)} %get-tuple-element.95), channel_id=1, source_target_pairs={{0,2},{1,3},{2,0},{3,1},{4,6},{5,7},{6,4},{7,5},{8,10},{9,11},{10,... | collective-permute-start | bytes 442376 | tf_op jit(solution)/shard_map/ppermute | solution.py:566
  114.3 21.0 %copy-start.24 = (f32[1,2,6,48,128]{4,3,2,1,0:T(8,128)}, f32[1,2,6,48,128]{4,3,2,1,0:T(8,128)S(1)}, u32[]{:S(2)}) copy-start(f32[1,2,6,48,128]{4,3,2,1,0:T(8,128)S(1)} %collective-permute-done.18.refs_1_) | copy-start | bytes 884740
  114.3 21.0 %collective-permute-start.23 = (f32[1,1,6,48,128]{4,3,2,1,0:T(8,128)}, f32[1,1,6,48,128]{4,3,2,1,0:T(8,128)S(1)}, u32[]{:S(2)}, u32[]{:S(2)}) collective-permute-start(f32[1,1,6,48,128]{4,3,2,1,0:T(8,128)} %get-tuple-element.96), channel_id=1, source_target_pairs={{0,3},{1,2},{2,1},{3,0},{4,7},{5,6},{6,5},{7,4},{8,11},{9,10},{10,... | collective-permute-start | bytes 442376 | tf_op jit(solution)/shard_map/ppermute | solution.py:567
  114.6 25.4 %collective-permute-start.27 = (f32[1,1,6,48,128]{4,3,2,1,0:T(8,128)}, f32[1,1,6,48,128]{4,3,2,1,0:T(8,128)S(1)}, u32[]{:S(2)}, u32[]{:S(2)}) collective-permute-start(f32[1,1,6,48,128]{4,3,2,1,0:T(8,128)} %get-tuple-element.102), channel_id=1, source_target_pairs={{0,1},{1,0},{2,3},{3,2},{4,5},{5,4},{6,7},{7,6},{8,9},{9,8},{10,11... | collective-permute-start | bytes 442376 | tf_op jit(solution)/shard_map/ppermute | solution.py:567
  127.2 91.5 %collective-permute-start.2 = (f32[2,3,6,48,128]{4,3,2,1,0:T(8,128)S(1)}, f32[2,3,6,48,128]{4,3,2,1,0:T(8,128)}, u32[]{:S(2)}, u32[]{:S(2)}) collective-permute-start(f32[2,3,6,48,128]{4,3,2,1,0:T(8,128)S(1)} %copy-done.21), channel_id=1, source_target_pairs={{0,1},{1,0},{2,3},{3,2},{4,5},{5,4},{6,7},{7,6},{8,9},{9,8},{10,11... | collective-permute-start | bytes 2654216 | tf_op jit(solution)/shard_map/ppermute | solution.py:613
  127.2 12.9 %copy-start.27 = (f32[1,1,6,48,128]{4,3,2,1,0:T(8,128)}, f32[1,1,6,48,128]{4,3,2,1,0:T(8,128)S(1)}, u32[]{:S(2)}) copy-start(f32[1,1,6,48,128]{4,3,2,1,0:T(8,128)S(1)} %collective-permute-done.21.refs_5_) | copy-start | bytes 442372
  127.2 25.3 %collective-permute-start.28 = (f32[1,1,6,48,128]{4,3,2,1,0:T(8,128)}, f32[1,1,6,48,128]{4,3,2,1,0:T(8,128)S(1)}, u32[]{:S(2)}, u32[]{:S(2)}) collective-permute-start(f32[1,1,6,48,128]{4,3,2,1,0:T(8,128)} %get-tuple-element.103), channel_id=1, source_target_pairs={{0,2},{1,3},{2,0},{3,1},{4,6},{5,7},{6,4},{7,5},{8,10},{9,11},{10,... | collective-permute-start | bytes 442376 | tf_op jit(solution)/shard_map/ppermute | solution.py:566
  131.9 8.1 %copy-start.28 = (f32[1,1,6,48,128]{4,3,2,1,0:T(8,128)}, f32[1,1,6,48,128]{4,3,2,1,0:T(8,128)S(1)}, u32[]{:S(2)}) copy-start(f32[1,1,6,48,128]{4,3,2,1,0:T(8,128)S(1)} %collective-permute-done.22.refs_6_) | copy-start | bytes 442372
  131.9 25.2 %collective-permute-start.29 = (f32[1,1,6,48,128]{4,3,2,1,0:T(8,128)S(1)}, f32[1,1,6,48,128]{4,3,2,1,0:T(8,128)S(1)}, u32[]{:S(2)}, u32[]{:S(2)}) collective-permute-start(f32[1,1,6,48,128]{4,3,2,1,0:T(8,128)S(1)} %copy-done.26), channel_id=1, source_target_pairs={{0,3},{1,2},{2,1},{3,0},{4,7},{5,6},{6,5},{7,4},{8,11},{9,10},{10,... | collective-permute-start | bytes 442376 | tf_op jit(solution)/shard_map/ppermute | solution.py:567
  135.3 41.8 %copy-start.30 = (f32[1,1,6,48,128]{4,3,2,1,0:T(8,128)}, f32[1,1,6,48,128]{4,3,2,1,0:T(8,128)S(1)}, u32[]{:S(2)}) copy-start(f32[1,1,6,48,128]{4,3,2,1,0:T(8,128)S(1)} %collective-permute-done.23.refs_7_) | copy-start | bytes 442372
  135.3 22.4 %collective-permute-start.15 = (f32[1,192,256]{2,1,0:T(8,128)S(1)}, f32[1,192,256]{2,1,0:T(8,128)S(1)}, u32[]{:S(2)}, u32[]{:S(2)}) collective-permute-start(f32[1,192,256]{2,1,0:T(8,128)S(1)} %get-tuple-element.131), channel_id=1, source_target_pairs={{4,0},{8,4},{12,8},{16,12},{20,16},{24,20},{28,24},{0,28},{5,1},{9... | collective-permute-start | bytes 589832 | tf_op jit(solution)/shard_map/ppermute | solution.py:496
  140.1 28.7 %copy-start.29 = (f32[1,1,6,48,128]{4,3,2,1,0:T(8,128)}, f32[1,1,6,48,128]{4,3,2,1,0:T(8,128)S(1)}, u32[]{:S(2)}) copy-start(f32[1,1,6,48,128]{4,3,2,1,0:T(8,128)S(1)} %collective-permute-done.27.refs_5_) | copy-start | bytes 442372
  140.1 27.9 %collective-permute-start.30 = (f32[1,3,6,48,128]{4,3,2,1,0:T(8,128)S(1)}, f32[1,3,6,48,128]{4,3,2,1,0:T(8,128)S(1)}, u32[]{:S(2)}, u32[]{:S(2)}) collective-permute-start(f32[1,3,6,48,128]{4,3,2,1,0:T(8,128)S(1)} %copy-done.22), channel_id=1, source_target_pairs={{0,1},{1,0},{2,3},{3,2},{4,5},{5,4},{6,7},{7,6},{8,9},{9,8},{10,11... | collective-permute-start | bytes 1327112 | tf_op jit(solution)/shard_map/ppermute | solution.py:567
  152.4 24.7 %copy-start.31 = (f32[1,1,6,48,128]{4,3,2,1,0:T(8,128)}, f32[1,1,6,48,128]{4,3,2,1,0:T(8,128)S(1)}, u32[]{:S(2)}) copy-start(f32[1,1,6,48,128]{4,3,2,1,0:T(8,128)S(1)} %collective-permute-done.28.refs_6_) | copy-start | bytes 442372
  152.4 7.6 %collective-permute-start.14 = (f32[1,192,256]{2,1,0:T(8,128)S(1)}, f32[1,192,256]{2,1,0:T(8,128)S(1)}, u32[]{:S(2)}, u32[]{:S(2)}) collective-permute-start(f32[1,192,256]{2,1,0:T(8,128)S(1)} %get-tuple-element.132), channel_id=1, source_target_pairs={{0,4},{4,8},{8,12},{12,16},{16,20},{20,24},{24,28},{28,0},{1,5},{5... | collective-permute-start | bytes 589832 | tf_op jit(solution)/shard_map/ppermute | solution.py:496
  157.1 20.0 %copy-start.32 = (f32[1,1,6,48,128]{4,3,2,1,0:T(8,128)}, f32[1,1,6,48,128]{4,3,2,1,0:T(8,128)S(1)}, u32[]{:S(2)}) copy-start(f32[1,1,6,48,128]{4,3,2,1,0:T(8,128)S(1)} %collective-permute-done.29.refs_7_) | copy-start | bytes 442372
  157.1 81.2 %collective-permute-start.6 = (f32[2,3,6,48,128]{4,3,2,1,0:T(8,128)}, f32[2,3,6,48,128]{4,3,2,1,0:T(8,128)}, u32[]{:S(2)}, u32[]{:S(2)}) collective-permute-start(f32[2,3,6,48,128]{4,3,2,1,0:T(8,128)} %get-tuple-element.76), channel_id=1, source_target_pairs={{0,1},{1,0},{2,3},{3,2},{4,5},{5,4},{6,7},{7,6},{8,9},{9,8},{10,11... | collective-permute-start | bytes 2654216 | tf_op jit(solution)/shard_map/ppermute | solution.py:613
  157.8 29.0 %copy-start.6 = (f32[1,192,256]{2,1,0:T(8,128)}, f32[1,192,256]{2,1,0:T(8,128)S(1)}, u32[]{:S(2)}) copy-start(f32[1,192,256]{2,1,0:T(8,128)S(1)} %collective-permute-done.15.refs_10_.refs_7_) | copy-start | bytes 589828
  157.8 85.8 %collective-permute-start.10 = (f32[2,3,6,48,128]{4,3,2,1,0:T(8,128)}, f32[2,3,6,48,128]{4,3,2,1,0:T(8,128)}, u32[]{:S(2)}, u32[]{:S(2)}) collective-permute-start(f32[2,3,6,48,128]{4,3,2,1,0:T(8,128)} %get-tuple-element.80), channel_id=1, source_target_pairs={{0,1},{1,0},{2,3},{3,2},{4,5},{5,4},{6,7},{7,6},{8,9},{9,8},{10,11... | collective-permute-start | bytes 2654216 | tf_op jit(solution)/shard_map/ppermute | solution.py:613
  160.0 26.8 %copy-start.7 = (f32[1,192,256]{2,1,0:T(8,128)}, f32[1,192,256]{2,1,0:T(8,128)S(1)}, u32[]{:S(2)}) copy-start(f32[1,192,256]{2,1,0:T(8,128)S(1)} %collective-permute-done.14.refs_9_.refs_6_) | copy-start | bytes 589828
  160.0 52.9 %collective-permute-start.31 = (f32[1,3,6,48,128]{4,3,2,1,0:T(8,128)}, f32[1,3,6,48,128]{4,3,2,1,0:T(8,128)}, u32[]{:S(2)}, u32[]{:S(2)}) collective-permute-start(f32[1,3,6,48,128]{4,3,2,1,0:T(8,128)} %get-tuple-element.107), channel_id=1, source_target_pairs={{0,2},{1,3},{2,0},{3,1},{4,6},{5,7},{6,4},{7,5},{8,10},{9,11},{10,... | collective-permute-start | bytes 1327112 | tf_op jit(solution)/shard_map/ppermute | solution.py:566
  168.7 54.9 %collective-permute-start.32 = (f32[1,3,6,48,128]{4,3,2,1,0:T(8,128)}, f32[1,3,6,48,128]{4,3,2,1,0:T(8,128)}, u32[]{:S(2)}, u32[]{:S(2)}) collective-permute-start(f32[1,3,6,48,128]{4,3,2,1,0:T(8,128)} %get-tuple-element.108), channel_id=1, source_target_pairs={{0,3},{1,2},{2,1},{3,0},{4,7},{5,6},{6,5},{7,4},{8,11},{9,10},{10,... | collective-permute-start | bytes 1327112 | tf_op jit(solution)/shard_map/ppermute | solution.py:567
  212.9 15.7 %collective-permute-start.34 = (f32[192,128]{1,0:T(8,128)S(1)}, f32[192,128]{1,0:T(8,128)S(1)}, u32[]{:S(2)}, u32[]{:S(2)}) collective-permute-start(f32[192,128]{1,0:T(8,128)S(1)} %get-tuple-element.135), channel_id=1, source_target_pairs={{4,0},{8,4},{12,8},{16,12},{20,16},{24,20},{28,24},{0,28},{5,1},{9... | collective-permute-start | bytes 294920 | tf_op jit(solution)/shard_map/ppermute | solution.py:496
  218.6 10.0 %collective-permute-start.33 = (f32[192,128]{1,0:T(8,128)S(1)}, f32[192,128]{1,0:T(8,128)S(1)}, u32[]{:S(2)}, u32[]{:S(2)}) collective-permute-start(f32[192,128]{1,0:T(8,128)S(1)} %get-tuple-element.136), channel_id=1, source_target_pairs={{0,4},{4,8},{8,12},{12,16},{16,20},{20,24},{24,28},{28,0},{1,5},{5... | collective-permute-start | bytes 294920 | tf_op jit(solution)/shard_map/ppermute | solution.py:496
  223.6 47.8 %collective-permute-start.3 = (f32[6,192,128]{2,1,0:T(8,128)}, f32[6,192,128]{2,1,0:T(8,128)S(1)}, u32[]{:S(2)}, u32[]{:S(2)}) collective-permute-start(f32[6,192,128]{2,1,0:T(8,128)} %get-tuple-element.67), channel_id=1, source_target_pairs={{0,2},{1,3},{2,0},{3,1},{4,6},{5,7},{6,4},{7,5},{8,10},{9,11},{10,... | collective-permute-start | bytes 1769480 | tf_op jit(solution)/shard_map/ppermute | solution.py:554
  233.4 18.7 %collective-permute-start.35 = (f32[2,192,128]{2,1,0:T(8,128)}, f32[2,192,128]{2,1,0:T(8,128)S(1)}, u32[]{:S(2)}, u32[]{:S(2)}) collective-permute-start(f32[2,192,128]{2,1,0:T(8,128)} %get-tuple-element.111), channel_id=1, source_target_pairs={{0,4},{4,8},{8,12},{12,16},{16,20},{20,24},{24,28},{28,0},{1,5},{5... | collective-permute-start | bytes 589832 | tf_op jit(solution)/shard_map/ppermute | solution.py:496
  238.3 13.7 %collective-permute-start.36 = (f32[2,192,128]{2,1,0:T(8,128)}, f32[2,192,128]{2,1,0:T(8,128)}, u32[]{:S(2)}, u32[]{:S(2)}) collective-permute-start(f32[2,192,128]{2,1,0:T(8,128)} %get-tuple-element.112), channel_id=1, source_target_pairs={{4,0},{8,4},{12,8},{16,12},{20,16},{24,20},{28,24},{0,28},{5,1},{9... | collective-permute-start | bytes 589832 | tf_op jit(solution)/shard_map/ppermute | solution.py:496
  243.5 41.9 %collective-permute-start.7 = (f32[6,192,128]{2,1,0:T(8,128)}, f32[6,192,128]{2,1,0:T(8,128)S(1)}, u32[]{:S(2)}, u32[]{:S(2)}) collective-permute-start(f32[6,192,128]{2,1,0:T(8,128)} %get-tuple-element.78), channel_id=1, source_target_pairs={{0,2},{1,3},{2,0},{3,1},{4,6},{5,7},{6,4},{7,5},{8,10},{9,11},{10,... | collective-permute-start | bytes 1769480 | tf_op jit(solution)/shard_map/ppermute | solution.py:554
  248.5 49.5 %collective-permute-start.11 = (f32[6,192,128]{2,1,0:T(8,128)}, f32[6,192,128]{2,1,0:T(8,128)S(1)}, u32[]{:S(2)}, u32[]{:S(2)}) collective-permute-start(f32[6,192,128]{2,1,0:T(8,128)} %get-tuple-element.82), channel_id=1, source_target_pairs={{0,2},{1,3},{2,0},{3,1},{4,6},{5,7},{6,4},{7,5},{8,10},{9,11},{10,... | collective-permute-start | bytes 1769480 | tf_op jit(solution)/shard_map/ppermute | solution.py:554
  260.4 69.1 %collective-permute-start.40 = (f32[3,6,48,128]{3,2,1,0:T(8,128)}, f32[3,6,48,128]{3,2,1,0:T(8,128)}, u32[]{:S(2)}, u32[]{:S(2)}) collective-permute-start(f32[3,6,48,128]{3,2,1,0:T(8,128)} %get-tuple-element.120), channel_id=1, source_target_pairs={{0,1},{1,0},{2,3},{3,2},{4,5},{5,4},{6,7},{7,6},{8,9},{9,8},{10,11... | collective-permute-start | bytes 1327112 | tf_op jit(solution)/shard_map/ppermute | solution.py:693
  271.5 26.6 %copy-start.2 = (f32[6,192,128]{2,1,0:T(8,128)}, f32[6,192,128]{2,1,0:T(8,128)S(1)}, u32[]{:S(2)}) copy-start(f32[6,192,128]{2,1,0:T(8,128)S(1)} %collective-permute-done.3.refs_1_.refs_10_) | copy-start | bytes 1769476
  272.6 25.4 %collective-permute-start.13 = (f32[192,128]{1,0:T(8,128)S(1)}, f32[192,128]{1,0:T(8,128)S(1)}, u32[]{:S(2)}, u32[]{:S(2)}) collective-permute-start(f32[192,128]{1,0:T(8,128)S(1)} %get-tuple-element.133), channel_id=1, source_target_pairs={{4,0},{8,4},{12,8},{16,12},{20,16},{24,20},{28,24},{0,28},{5,1},{9... | collective-permute-start | bytes 294920 | tf_op jit(solution)/shard_map/ppermute | solution.py:496
  279.0 19.1 %collective-permute-start.12 = (f32[192,128]{1,0:T(8,128)S(1)}, f32[192,128]{1,0:T(8,128)S(1)}, u32[]{:S(2)}, u32[]{:S(2)}) collective-permute-start(f32[192,128]{1,0:T(8,128)S(1)} %get-tuple-element.134), channel_id=1, source_target_pairs={{0,4},{4,8},{8,12},{12,16},{16,20},{20,24},{24,28},{28,0},{1,5},{5... | collective-permute-start | bytes 294920 | tf_op jit(solution)/shard_map/ppermute | solution.py:496
  285.4 12.7 %copy-start.4 = (f32[6,192,128]{2,1,0:T(8,128)}, f32[6,192,128]{2,1,0:T(8,128)S(1)}, u32[]{:S(2)}) copy-start(f32[6,192,128]{2,1,0:T(8,128)S(1)} %collective-permute-done.7.refs_3_.refs_12_) | copy-start | bytes 1769476
  303.6 11.2 %collective-permute-start.16 = (f32[2,192,128]{2,1,0:T(8,128)}, f32[2,192,128]{2,1,0:T(8,128)S(1)}, u32[]{:S(2)}, u32[]{:S(2)}) collective-permute-start(f32[2,192,128]{2,1,0:T(8,128)} %get-tuple-element.87), channel_id=1, source_target_pairs={{0,4},{4,8},{8,12},{12,16},{16,20},{20,24},{24,28},{28,0},{1,5},{5... | collective-permute-start | bytes 589832 | tf_op jit(solution)/shard_map/ppermute | solution.py:496
  310.5 5.3 %collective-permute-start.17 = (f32[2,192,128]{2,1,0:T(8,128)}, f32[2,192,128]{2,1,0:T(8,128)S(1)}, u32[]{:S(2)}, u32[]{:S(2)}) collective-permute-start(f32[2,192,128]{2,1,0:T(8,128)} %get-tuple-element.88), channel_id=1, source_target_pairs={{4,0},{8,4},{12,8},{16,12},{20,16},{24,20},{28,24},{0,28},{5,1},{9... | collective-permute-start | bytes 589832 | tf_op jit(solution)/shard_map/ppermute | solution.py:496
  310.5 32.3 %collective-permute-start.41 = (f32[3,6,48,128]{3,2,1,0:T(8,128)}, f32[3,6,48,128]{3,2,1,0:T(8,128)S(1)}, u32[]{:S(2)}, u32[]{:S(2)}) collective-permute-start(f32[3,6,48,128]{3,2,1,0:T(8,128)} %get-tuple-element.121), channel_id=1, source_target_pairs={{0,2},{1,3},{2,0},{3,1},{4,6},{5,7},{6,4},{7,5},{8,10},{9,11},{10,... | collective-permute-start | bytes 1327112 | tf_op jit(solution)/shard_map/ppermute | solution.py:693
  313.5 58.3 %collective-permute-start.42 = (f32[3,6,48,128]{3,2,1,0:T(8,128)}, f32[3,6,48,128]{3,2,1,0:T(8,128)S(1)}, u32[]{:S(2)}, u32[]{:S(2)}) collective-permute-start(f32[3,6,48,128]{3,2,1,0:T(8,128)} %get-tuple-element.122), channel_id=1, source_target_pairs={{0,3},{1,2},{2,1},{3,0},{4,7},{5,6},{6,5},{7,4},{8,11},{9,10},{10,... | collective-permute-start | bytes 1327112 | tf_op jit(solution)/shard_map/ppermute | solution.py:693
  326.3 54.6 %collective-permute-start.37 = (f32[3,6,48,128]{3,2,1,0:T(8,128)}, f32[3,6,48,128]{3,2,1,0:T(8,128)S(1)}, u32[]{:S(2)}, u32[]{:S(2)}) collective-permute-start(f32[3,6,48,128]{3,2,1,0:T(8,128)} %get-tuple-element.116), channel_id=1, source_target_pairs={{0,1},{1,0},{2,3},{3,2},{4,5},{5,4},{6,7},{7,6},{8,9},{9,8},{10,11... | collective-permute-start | bytes 1327112 | tf_op jit(solution)/shard_map/ppermute | solution.py:693
  328.9 52.0 %collective-permute-start.38 = (f32[3,6,48,128]{3,2,1,0:T(8,128)}, f32[3,6,48,128]{3,2,1,0:T(8,128)S(1)}, u32[]{:S(2)}, u32[]{:S(2)}) collective-permute-start(f32[3,6,48,128]{3,2,1,0:T(8,128)} %get-tuple-element.117), channel_id=1, source_target_pairs={{0,2},{1,3},{2,0},{3,1},{4,6},{5,7},{6,4},{7,5},{8,10},{9,11},{10,... | collective-permute-start | bytes 1327112 | tf_op jit(solution)/shard_map/ppermute | solution.py:693
  329.5 61.3 %collective-permute-start.39 = (f32[3,6,48,128]{3,2,1,0:T(8,128)}, f32[3,6,48,128]{3,2,1,0:T(8,128)}, u32[]{:S(2)}, u32[]{:S(2)}) collective-permute-start(f32[3,6,48,128]{3,2,1,0:T(8,128)} %get-tuple-element.118), channel_id=1, source_target_pairs={{0,3},{1,2},{2,1},{3,0},{4,7},{5,6},{6,5},{7,4},{8,11},{9,10},{10,... | collective-permute-start | bytes 1327112 | tf_op jit(solution)/shard_map/ppermute | solution.py:693
  342.7 29.0 %copy-start.8 = (f32[3,6,48,128]{3,2,1,0:T(8,128)}, f32[3,6,48,128]{3,2,1,0:T(8,128)S(1)}, u32[]{:S(2)}) copy-start(f32[3,6,48,128]{3,2,1,0:T(8,128)S(1)} %collective-permute-done.41.refs_2_) | copy-start | bytes 1327108
  380.9 9.9 %copy-start.10 = (f32[3,6,48,128]{3,2,1,0:T(8,128)}, f32[3,6,48,128]{3,2,1,0:T(8,128)S(1)}, u32[]{:S(2)}) copy-start(f32[3,6,48,128]{3,2,1,0:T(8,128)S(1)} %collective-permute-done.37.refs_1_) | copy-start | bytes 1327108
  381.0 9.9 %copy-start.11 = (f32[3,6,48,128]{3,2,1,0:T(8,128)}, f32[3,6,48,128]{3,2,1,0:T(8,128)S(1)}, u32[]{:S(2)}) copy-start(f32[3,6,48,128]{3,2,1,0:T(8,128)S(1)} %collective-permute-done.38.refs_2_) | copy-start | bytes 1327108
  (12 other events, 15.8 us)
